TPU v7x, 512 devices: a whole 4x4x16 slice. The times are simulated.
512 devices in a mesh: src: 32 (over z, y_hi), tgt: 16 (over y_lo, x, core).
Axes of the slice: x: 4, y: 4 (y_hi: 2, y_lo: 2; y = y_hi * 2 + y_lo), z: 16, core: 2. Of those that a mesh axis runs over, the one named last changes fastest.
Arguments:
- sources: bfloat16 [32768, 512], P('src'), may hold values from -400 to 400
- log_src: float32 [32768], P('src'), may hold values from -1 to 1
- targets: bfloat16 [32768, 512], P(('src', 'tgt')), may hold values from -6 to 6
- potential: float32 [32768], P(('src', 'tgt')), may hold values from -5 to 5
- log_tgt: float32 [32768], P(('src', 'tgt')), may hold values from -1 to 1
Outputs:
- src_pot: float32 [32768], P('src')
- tgt_pot: float32 [32768], P(('src', 'tgt'))
- mapped: bfloat16 [32768, 512], P('src', 'tgt')
All inputs are finite; a program needn't handle non-finite values.
Results may differ from a plain program's by a relative error of at most 0.0144.
Values may be sent and summed in bfloat16 or wider, within the bound.
No kernel may reach another device: no remote copies, remote signals or barrier semaphores. Data moves between devices by JAX's collectives and lax.ppermute only.
A program may use at most 64 MiB of HBM per device.

v0:
```python
import math

import jax
import jax.numpy as jnp
from jax import lax
from jax.sharding import Mesh
from jax.sharding import PartitionSpec as P

SRC = ("src_0", "src_1")
SRC_TGT = ("src_0", "src_1", "tgt")


def gathered_by_axis(array, axes, dim):
    if not axes:
        return array
    nearer = lax.all_gather(array, axes[-1], axis=dim, tiled=True)
    return gathered_by_axis(nearer, axes[:-1], dim)


def from_everyone(array, axis):
    copies = jnp.broadcast_to(array, (lax.axis_size(axis), *array.shape))
    return lax.all_to_all(copies, axis, split_axis=0, concat_axis=0, tiled=True)


def collected_together(array, axis):
    leaves = jax.tree.leaves(array)
    sequence = sorted(range(len(leaves)), key=lambda k: -leaves[k].size)
    width = (1, *leaves[sequence[0]].shape)[-1]
    lines = [
        jnp.pad(leaves[k].reshape(-1), (0, -leaves[k].size % width)).reshape(-1, width)
        for k in sequence
    ]
    both, at, found = (from_everyone(jnp.concatenate(lines), axis), 0, {})
    for k, line in zip(sequence, lines):
        piece = both[:, at : at + len(line)].reshape(len(both), -1)
        found[k] = piece[:, : leaves[k].size].reshape(-1, *leaves[k].shape)
        at += len(line)
    numbers = iter(range(len(leaves)))
    return jax.tree.map(lambda _: found[next(numbers)], array)


def folded_in_pairs(pieces, combine):
    while len(jax.tree.leaves(pieces)[0]) > 1:
        pieces = jax.vmap(combine)(
            *(jax.tree.map(lambda part: part[side::2], pieces) for side in (0, 1))
        )
    return jax.tree.map(lambda part: part[0], pieces)


def merged(array, axis, combine):
    pieces = collected_together(array, axis)
    return folded_in_pairs(pieces, combine)


def once_a_type(array, axis):
    leaves, found = (jax.tree.leaves(array), {})
    for initial, a in enumerate(leaves):
        if initial not in found:
            alike = [k for k, b in enumerate(leaves) if b.dtype == a.dtype]
            got = (
                collected_together([leaves[k] for k in alike], axis)
                if len(alike) > 1
                else [from_everyone(a, axis)]
            )
            for k, b in zip(alike, got):
                found[k] = b
    numbers = iter(range(len(leaves)))
    return jax.tree.map(lambda _: found[next(numbers)], array)


def combined_all(array, axis, combine):
    pieces = once_a_type(array, axis)
    return folded_in_pairs(pieces, combine)


def over_copies(array, axis):
    everything = from_everyone(array, axis)
    return jnp.sum(everything, axis=0)


def split_up(array, dim, size):
    before, after = (array.shape[:dim], array.shape[dim + 1 :])
    return jnp.moveaxis(array.reshape(*before, size, -1, *after), dim, 0)


def sent_and_summed(array, axis, dim):
    parts = split_up(array, dim, lax.axis_size(axis))
    arrived = lax.all_to_all(parts, axis, split_axis=0, concat_axis=0, tiled=True)
    return arrived.astype(jnp.float32).sum(axis=0)


def lse_pair(first, second):
    top = jnp.maximum(first[0], second[0])
    return (top, first[1] * jnp.exp(first[0] - top) + second[1] * jnp.exp(second[0] - top))


def scores_of(sources, piece, scale):
    product = lax.dot_general(
        sources, piece, (((1,), (1,)), ((), ())), preferred_element_type=jnp.float32
    )
    return product * scale


def body(sources, log_src, targets, potential, log_tgt):
    scale = 1.0 / math.sqrt(sources.shape[1])
    own = targets.shape[0]
    here = lax.axis_index(SRC) * own
    whole, pot_all, logt_all = (
        gathered_by_axis(targets, SRC, 0),
        gathered_by_axis(potential.astype(jnp.bfloat16), SRC, 0).astype(potential.dtype),
        gathered_by_axis(log_tgt.astype(jnp.bfloat16), SRC, 0).astype(log_tgt.dtype),
    )
    scores = scores_of(sources, whole, scale)
    shifted = scores + pot_all[None, :]
    row_top = jnp.max(shifted, axis=1)
    row_total = jnp.sum(jnp.exp(shifted - row_top[:, None]), axis=1)
    row_top, row_total = merged((row_top, row_total), "tgt", lse_pair)
    src_pot = log_src - (row_top + jnp.log(row_total))
    lifted = scores + src_pot[:, None]
    col_top = jnp.max(lifted, axis=0)
    col_total = jnp.sum(jnp.exp(lifted - col_top[None, :]), axis=0)
    peak, total = combined_all((col_top, col_total), SRC, lse_pair)
    tgt_all = logt_all - (peak + jnp.log(total))
    tgt_pot = lax.dynamic_slice_in_dim(tgt_all, here, own)
    weight = jnp.exp(scores + src_pot[:, None] + tgt_all[None, :])
    mass_part = jnp.sum(weight, axis=1)
    moved = jnp.dot(weight.astype(jnp.bfloat16), whole, preferred_element_type=jnp.float32)
    mass = over_copies(mass_part, "tgt")
    moved_mine = sent_and_summed(moved.astype(jnp.bfloat16), "tgt", 1)
    mapped = (moved_mine / mass[:, None]).astype(jnp.bfloat16)
    return (src_pot, tgt_pot, mapped)


def solution(mesh):
    torus = Mesh(mesh.devices.reshape(16, 2, mesh.shape["tgt"]), ("src_0", "src_1", "tgt"))
    return jax.shard_map(
        body,
        mesh=torus,
        in_specs=(P(SRC, None), P(SRC), P(SRC_TGT, None), P(SRC_TGT), P(SRC_TGT)),
        out_specs=(P(SRC), P(SRC_TGT), P(SRC, "tgt")),
        check_vma=False,
    )
```

profile of v0, /device:TPU:1, one launch (start us, length us, event | category | flops | bytes accessed | tf_op | source)
XLA Modules:
  0.0 228.5 jit_solution(12730165857021716889)
XLA Ops:
  7.2 7.9 %all_gather.18 = bf16[128,512]{1,0:T(8,128)(2,1)} all-gather(bf16[64,512]{1,0:T(8,128)(2,1)} %param.7), channel_id=1, replica_groups=mesh['src_0'=16,'src_1'=2,'tgt'=16] {'src_1'}, dimensions={0}, use_global_device_ids=true | all-gather | bytes 196608 | tf_op jit(solution)/shard_map/all_gather | solution.py:16
  15.2 0.7 convert_element_type.24
  15.9 0.7 convert_element_type.26
  16.5 1.3 dynamic-slice
  18.9 5.3 %all-reduce.2 = (bf16[128]{0:T(256)(128)(2,1)S(1)}, bf16[128]{0:T(256)(128)(2,1)S(1)}) all-reduce(bf16[128]{0:T(256)(128)(2,1)S(1)} %dynamic-update-slice, bf16[128]{0:T(256)(128)(2,1)S(1)} %dynamic-update-slice.1), channel_id=1, replica_groups=mesh['src_0'=16,'src_1'=2,'tgt'=16] {'src_1'}, use_global_device_ids=true, to_apply=%add | all-reduce | flops 256 | bytes 1024
  24.2 28.8 %all-gather = bf16[16,1,128]{2,1,0:T(2,128)(2,1)S(1)} all-gather(bf16[1,1,128]{2,1,0:T(2,128)(2,1)S(1)} %bitcast.41), channel_id=1, replica_groups=mesh['src_0'=16,'src_1'=2,'tgt'=16] {'src_0'}, dimensions={0}, use_global_device_ids=true | all-gather | bytes 4352 | tf_op jit(solution)/shard_map/all_gather | solution.py:16
  52.9 29.8 %all-gather.4.cloned.1.call-done = bf16[2048,512]{1,0:T(8,128)(2,1)} async-done(((bf16[128,512]{1,0:T(8,128)(2,1)}), bf16[2048,512]{1,0:T(8,128)(2,1)}) %all-gather.4.cloned.1.call-update) | async-done | bytes 2097168 | tf_op jit(solution)/shard_map/all_gather | solution.py:16
  82.7 4.1 %add_reduce_fusion = (f32[1024]{0:T(1024)S(1)}, f32[1024,2048]{1,0:T(8,128)S(1)}) fusion(f32[2048]{0:T(1024)S(1)} %bitcast.34, bf16[1024,512]{1,0:T(8,128)(2,1)S(1)} %copy-done, bf16[2048,512]{1,0:T(8,128)(2,1)} %all-gather.4.cloned.1.call-done), kind=kOutput, calls=%fused_computation.3 | convolution fusion | flops 2153774080 | bytes 11546624 | tf_op jit(solution)/shard_map/dot_general | solution.py:98
  86.8 3.2 %copy-done.1 = f32[1024,2048]{1,0:T(8,128)} copy-done((f32[1024,2048]{1,0:T(8,128)}, f32[1024,2048]{1,0:T(8,128)S(1)}, u32[]{:S(2)}) %copy-start.1) | copy-done | bytes 8388632
  90.0 2.2 exponential_reduce_fusion.1
  92.3 21.1 %all_to_all.21 = f32[16,2,1024]{2,1,0:T(2,128)S(1)} all-to-all(f32[16,2,1024]{2,1,0:T(2,128)S(1)} %broadcast_in_dim.6), channel_id=1, replica_groups=mesh['src_0'=16,'src_1'=2,'tgt'=16] {'tgt'}, dimensions={0} | all-to-all | bytes 262144 | tf_op jit(solution)/shard_map/all_to_all | solution.py:22
  114.0 4.4 %fusion.2 = f32[2048]{0:T(1024)S(1)} fusion(f32[1024,2048]{1,0:T(8,128)} %copy-done.1, f32[1024]{0:T(1024)S(1)} %sub.86), kind=kLoop, calls=%fused_computation.7 | loop fusion | flops 6289408 | bytes 8400896 | tf_op jit(solution)/shard_map/reduce_max | solution.py:120
  118.4 1.2 copy-done.2
  119.7 2.3 exponential_reduce_fusion
  122.0 1.0 broadcast_in_dim.7
  123.0 10.1 %all-to-all-start.1 = ((f32[32,2,2048]{2,1,0:T(2,128)}), f32[32,2,2048]{2,1,0:T(2,128)S(1)}, u32[]{:S(2)}, u32[]{:S(2)}) async-start(f32[32,2,2048]{2,1,0:T(2,128)} %broadcast_in_dim.7), calls=%async_computation.1 | async-start | bytes 1048576 | tf_op jit(solution)/shard_map/all_to_all | solution.py:22
  133.1 41.4 %all-gather.1 = bf16[16,1,128]{2,1,0:T(2,128)(2,1)S(1)} all-gather(bf16[1,1,128]{2,1,0:T(2,128)(2,1)S(1)} %bitcast.40), channel_id=1, replica_groups=mesh['src_0'=16,'src_1'=2,'tgt'=16] {'src_0'}, dimensions={0}, use_global_device_ids=true | all-gather | bytes 4352 | tf_op jit(solution)/shard_map/all_gather | solution.py:16
  176.0 4.7 %fusion = f32[1024]{0:T(1024)S(1)} fusion(f32[1024,2048]{1,0:T(8,128)} %copy-done.1, f32[2048]{0:T(1024)S(1)} %sub.99, f32[1024]{0:T(1024)S(1)} %sub.86), kind=kLoop, calls=%fused_computation.4 | loop fusion | flops 8387584 | bytes 8404992 | tf_op jit(solution)/shard_map/reduce_sum | solution.py:126
  180.7 0.7 broadcast_in_dim.8
  181.4 10.8 %all-to-all-start.3 = ((f32[16,1,1024]{2,1,0:T(1,128)}), f32[16,1,1024]{2,1,0:T(1,128)S(1)}, u32[]{:S(2)}, u32[]{:S(2)}) async-start(f32[16,1,1024]{2,1,0:T(1,128)} %broadcast_in_dim.8), calls=%async_computation.3 | async-start | bytes 131072 | tf_op jit(solution)/shard_map/all_to_all | solution.py:22
  192.2 7.1 %fusion.8 = bf16[1024,512]{0,1:T(8,128)(2,1)} fusion(bf16[2048,512]{1,0:T(8,128)(2,1)S(1)} %copy-done.5, f32[1024,2048]{1,0:T(8,128)} %copy-done.1, f32[2048]{0:T(1024)S(1)} %sub.99, f32[1024]{0:T(1024)S(1)} %sub.86), kind=kOutput, calls=%fused_computation.13 | convolution fusion | flops 2156396544 | bytes 11546624 | tf_op jit(solution)/shard_map/dot_general | solution.py:127
  199.3 5.8 %all-to-all-start.2 = ((bf16[16,1024,32]{1,2,0:T(8,128)(2,1)}), bf16[16,1024,32]{1,2,0:T(8,128)(2,1)S(1)}, u32[]{:S(2)}, u32[]{:S(2)}) async-start(bf16[16,1024,32]{1,2,0:T(8,128)(2,1)} %bitcast.14), calls=%async_computation.2 | async-start | bytes 2097152 | tf_op jit(solution)/shard_map/all_to_all | solution.py:88
  205.7 15.1 %all-to-all-done.2 = bf16[16,1024,32]{1,2,0:T(8,128)(2,1)S(1)} async-done(((bf16[16,1024,32]{1,2,0:T(8,128)(2,1)}), bf16[16,1024,32]{1,2,0:T(8,128)(2,1)S(1)}, u32[]{:S(2)}, u32[]{:S(2)}) %all-to-all-start.2) | async-done | bytes 1048608 | tf_op jit(solution)/shard_map/all_to_all | solution.py:88
  221.0 0.6 divide_convert_fusion
  (70 shorter events, 3.3 us)
Async XLA Ops:
  7.2 75.6 %copy-start = (bf16[1024,512]{1,0:T(8,128)(2,1)S(1)}, bf16[1024,512]{1,0:T(8,128)(2,1)}, u32[]{:S(2)}) copy-start(bf16[1024,512]{1,0:T(8,128)(2,1)} %param.5) | copy-start | bytes 3145732
  7.2 75.6 %all-gather.4.cloned.1.call-start = ((), (), s32[]{:S(2)}) async-start(), calls=%async_computation.4 | async-start | bytes 2228224 | tf_op jit(solution)/shard_map/all_gather | solution.py:16
  86.8 3.2 %copy-start.1 = (f32[1024,2048]{1,0:T(8,128)}, f32[1024,2048]{1,0:T(8,128)S(1)}, u32[]{:S(2)}) copy-start(f32[1024,2048]{1,0:T(8,128)S(1)} %get-tuple-element.24) | copy-start | bytes 25165828
  86.8 27.1 %copy-start.4 = (f32[1024]{0:T(1024)S(1)}, f32[1024]{0:T(1024)}, u32[]{:S(2)}) copy-start(f32[1024]{0:T(1024)} %param.6) | copy-start | bytes 12292
  113.9 5.8 %copy-start.2 = (f32[1024,2048]{1,0:T(8,128)S(1)}, f32[1024,2048]{1,0:T(8,128)}, u32[]{:S(2)}) copy-start(f32[1024,2048]{1,0:T(8,128)} %copy-done.1) | copy-start | bytes 25165828
  114.0 78.2 %copy-start.3 = (f32[1024]{0:T(1024)}, f32[1024]{0:T(1024)S(1)}, u32[]{:S(2)}) copy-start(f32[1024]{0:T(1024)S(1)} %sub.86) | copy-start | bytes 12292
  123.0 51.6 %all-to-all-start.1 = ((f32[32,2,2048]{2,1,0:T(2,128)}), f32[32,2,2048]{2,1,0:T(2,128)S(1)}, u32[]{:S(2)}, u32[]{:S(2)}) async-start(f32[32,2,2048]{2,1,0:T(2,128)} %broadcast_in_dim.7), calls=%async_computation.1 | async-start | bytes 1048576 | tf_op jit(solution)/shard_map/all_to_all | solution.py:22
  175.6 16.6 %copy-start.5 = (bf16[2048,512]{1,0:T(8,128)(2,1)S(1)}, bf16[2048,512]{1,0:T(8,128)(2,1)}, u32[]{:S(2)}) copy-start(bf16[2048,512]{1,0:T(8,128)(2,1)} %all-gather.4.cloned.1.call-done) | copy-start | bytes 6291460
  181.4 17.9 %all-to-all-start.3 = ((f32[16,1,1024]{2,1,0:T(1,128)}), f32[16,1,1024]{2,1,0:T(1,128)S(1)}, u32[]{:S(2)}, u32[]{:S(2)}) async-start(f32[16,1,1024]{2,1,0:T(1,128)} %broadcast_in_dim.8), calls=%async_computation.3 | async-start | bytes 131072 | tf_op jit(solution)/shard_map/all_to_all | solution.py:22
  199.3 21.5 %all-to-all-start.2 = ((bf16[16,1024,32]{1,2,0:T(8,128)(2,1)}), bf16[16,1024,32]{1,2,0:T(8,128)(2,1)S(1)}, u32[]{:S(2)}, u32[]{:S(2)}) async-start(bf16[16,1024,32]{1,2,0:T(8,128)(2,1)} %bitcast.14), calls=%async_computation.2 | async-start | bytes 2097152 | tf_op jit(solution)/shard_map/all_to_all | solution.py:88
Sparse Core Ops, SparseCore 0:
  15.3 67.3 all-gather.3
where the time goes:
time: 229 us
  blocking collectives  104 us (45%)
  waiting for transfers between devices  44.9 us (20%)
  starting transfers between devices  26.8 us (12%)
  other arithmetic  16.2 us (7%)
  between operations  15 us (7%)
  matrix products  11.1 us (5%)
  local copies, waits for them, and re-layouts  10 us (4%)
    all_gather x3, blocking collectives, gathered_by_axis(): nearer = lax.all_gather(array, axes[-1], axis=dim, tiled=True)  78.1 us
    all_gather x1, waiting for transfers between devices, gathered_by_axis(): nearer = lax.all_gather(array, axes[-1], axis=dim, tiled=True)  29.8 us
    all_to_all x1, blocking collectives, from_everyone(): return lax.all_to_all(copies, axis, split_axis=0, concat_axis=0, tiled=True)  21.1 us
    all_to_all x2, starting transfers between devices, from_everyone(): return lax.all_to_all(copies, axis, split_axis=0, concat_axis=0, tiled=True)  20.9 us
    all_to_all x1, waiting for transfers between devices, sent_and_summed(): lax.all_to_all(parts, axis, split_axis=0, concat_axis=0, tiled=True)  15.1 us
    dot_general x1, matrix products, body(): jnp.dot(weight.astype(jnp.bfloat16), whole, preferred_element_type=jnp.fl...  7.07 us
    unnamed x19, local copies, waits for them, and re-layouts  6.37 us
    all_to_all x1, starting transfers between devices, sent_and_summed(): lax.all_to_all(parts, axis, split_axis=0, concat_axis=0, tiled=True)  5.79 us
  transfers between devices with their start and end apart: 4, of which 2 were waited for; matrix products, arithmetic and copies ran while one was open for 5% of the time, Pallas kernels for 0%

commit v1 on v0

v1 whole, which is shorter than its diff:
```python
import math

import jax
import jax.numpy as jnp
from jax import lax
from jax.experimental import pallas as pl
from jax.experimental.pallas import tpu as pltpu
from jax.sharding import Mesh
from jax.sharding import PartitionSpec as P

AXES = ("z", "yh", "yl", "x", "c")
PLANE = ("yh", "yl", "x", "c")
CHIPS = ("yh", "yl", "x")
LOG2E = math.log2(math.e)
LN2 = math.log(2.0)
B = 64
A8 = 8
OFF1 = (0, 4, 11, 2, 6, 9)
OFF2 = (14, 1, 3, 7, 5, 12, 15, 8, 13, 10)
OFF = OFF1 + OFF2


def from_z(array, d):
    n = lax.axis_size("z")
    return lax.ppermute(array, "z", [((i + d) % n, i) for i in range(n)])


def thirds(v):
    hi = lax.reduce_precision(v, 8, 7)
    lo = lax.reduce_precision(v - hi, 8, 7)
    return [hi, lo, v - hi - lo]


def joined(messages):
    ks = [m.shape[0] // (B + A8) for m in messages]
    rows = [m[: k * B] for m, k in zip(messages, ks)]
    extra = [m[k * B :] for m, k in zip(messages, ks)]
    return jnp.concatenate(rows + extra, axis=0)


def eye(n):
    return lax.broadcasted_iota(jnp.int32, (n, n), 0) == lax.broadcasted_iota(jnp.int32, (n, n), 1)


def to_col(row):
    n = row.shape[1]
    return jnp.sum(jnp.where(eye(n), jnp.broadcast_to(row, (n, n)), 0.0), axis=1, keepdims=True)


def to_row(col):
    n = col.shape[0]
    return jnp.sum(jnp.where(eye(n), jnp.broadcast_to(col, (n, n)), 0.0), axis=0, keepdims=True)


CH = 512


def scores_kernel(picks, last, n_msg, scale2, scal, src, *refs):
    msgs = refs[:n_msg]
    rest = refs[n_msg:]
    if last:
        lse_in, s_out, tgt_out, lt_out, lse_out, tg, pot = rest
    else:
        s_out, tgt_out, lt_out, lse_out, tg, pot = rest
    n = pl.program_id(0)

    @pl.when(n == 0)
    def _():
        core = scal[1]
        lt_out[...] = jnp.zeros_like(lt_out)
        for p, (m, k) in enumerate(picks):
            total = msgs[m].shape[0] // (B + A8)
            rows = msgs[m][k * B : (k + 1) * B, :]
            tg[p * B : (p + 1) * B, :] = rows
            ex = msgs[m][total * B + k * A8 : total * B + (k + 1) * A8, 0:128].astype(jnp.float32)
            po = (ex[0:1] + ex[1:2] + ex[2:3]) * LOG2E
            lt_out[p : p + 1, :] = ex[3:4] + ex[4:5] + ex[5:6]
            pot[p * B : (p + 1) * B, :] = jnp.broadcast_to(to_col(po[:, :B]), (B, 128))
        for q in range(tg.shape[0] // 128):
            flipped = tg[q * 128 : (q + 1) * 128, :].astype(jnp.float32).T.astype(jnp.bfloat16)
            for t in range(16):
                at = pl.multiple_of((((t % 2) ^ core) * 8 + t // 2) * 32, 32)
                tgt_out[pl.ds(at, 32), q * 128 : (q + 1) * 128] = flipped[t * 32 : (t + 1) * 32, :]

    s = lax.dot_general(tg[...], src[...], (((1,), (1,)), ((), ())), preferred_element_type=jnp.float32) * scale2
    s_out[...] = s
    shifted = s + jnp.concatenate([pot[...]] * (CH // 128), axis=1)
    top = jnp.max(shifted, axis=0, keepdims=True)
    tot = jnp.sum(jnp.exp2(shifted - top), axis=0, keepdims=True)
    lse = top + jnp.log2(tot)
    if last:
        a = lse_in[...]
        hi = jnp.maximum(a, lse)
        lse = hi + jnp.log2(jnp.exp2(a - hi) + jnp.exp2(lse - hi))
        for i in range(CH // 128):
            piece = lse[:, i * 128 : (i + 1) * 128]
            lse_out[:, pl.ds(n * (CH // 128) + i, 1), :] = jnp.broadcast_to(piece[None], (lse_out.shape[0], 1, 128))
    else:
        lse_out[...] = lse


def scores_call(scal, src, msgs, picks, scale2, lse_in=None):
    t = len(picks) * B
    ns, f = src.shape
    last = lse_in is not None
    whole = lambda m: pl.BlockSpec(m.shape, lambda n, sc: (0,) * m.ndim)
    in_specs = [pl.BlockSpec((CH, f), lambda n, sc: (n, 0))] + [whole(m) for m in msgs]
    if last:
        in_specs.append(pl.BlockSpec((1, CH), lambda n, sc: (0, n)))
        lse_shape = jax.ShapeDtypeStruct((32, ns // 128, 128), jnp.float32)
        lse_spec = pl.BlockSpec((32, ns // 128, 128), lambda n, sc: (0, 0, 0))
    else:
        lse_shape = jax.ShapeDtypeStruct((1, ns), jnp.float32)
        lse_spec = pl.BlockSpec((1, CH), lambda n, sc: (0, n))
    lt_rows = -(-len(picks) // 8) * 8
    args = [scal, src, *msgs] + ([lse_in] if last else [])
    return pl.pallas_call(
        lambda *a: scores_kernel(picks, last, len(msgs), scale2, *a),
        name="scores_last" if last else "scores_first",
        grid_spec=pltpu.PrefetchScalarGridSpec(
            num_scalar_prefetch=1,
            grid=(ns // CH,),
            in_specs=in_specs,
            out_specs=[
                pl.BlockSpec((t, CH), lambda n, sc: (0, n)),
                pl.BlockSpec((f, t), lambda n, sc: (0, 0)),
                pl.BlockSpec((lt_rows, 128), lambda n, sc: (0, 0)),
                lse_spec,
            ],
            scratch_shapes=[pltpu.VMEM((t, f), jnp.bfloat16), pltpu.VMEM((t, 128), jnp.float32)],
        ),
        out_shape=[
            jax.ShapeDtypeStruct((t, ns), jnp.float32),
            jax.ShapeDtypeStruct((f, t), jnp.bfloat16),
            jax.ShapeDtypeStruct((lt_rows, 128), jnp.float32),
            lse_shape,
        ],
        cost_estimate=pl.CostEstimate(flops=2 * t * ns * f, bytes_accessed=4 * t * ns, transcendentals=t * ns),
    )(*args)


def merged_lse(parts):
    top = jnp.max(parts, axis=0)
    return top + jnp.log2(jnp.sum(jnp.exp2(parts - top[None]), axis=0))


def cols_kernel(scal, parts, log_src, s1, s2, pot_out, sp_out, msg_out, held):
    i = pl.program_id(0)

    @pl.when(i == 0)
    def _():
        sp = log_src[...] * LOG2E - merged_lse(parts[...])
        for r in range(sp.shape[0]):
            sp_out[:, r * 128 : (r + 1) * 128] = sp[r : r + 1, :]
        half = sp.shape[0] // 2
        pot_out[...] = jnp.where(scal[0] == 0, sp[:half], sp[half:]) * LN2
        held[...] = jnp.zeros_like(held)

    def step(s_ref):
        lifted = s_ref[...] + sp_out[...]
        top = jnp.max(lifted, axis=1, keepdims=True)
        lse = top + jnp.log2(jnp.sum(jnp.exp2(lifted - top), axis=1, keepdims=True))
        row = to_row(lse)
        row = jnp.concatenate([row, row], axis=1)
        slot = scal[2 + i]
        at = slot // 2
        half = lax.broadcasted_iota(jnp.int32, (1, 128), 1) // B
        held[pl.ds(at, 1), :] = jnp.where(half == slot % 2, row, held[pl.ds(at, 1), :])

    @pl.when(i < len(OFF1))
    def _():
        step(s1)

    @pl.when(i >= len(OFF1))
    def _():
        step(s2)

    @pl.when(i == len(OFF) - 1)
    def _():
        msg_out[...] = jnp.broadcast_to(held[...][None], msg_out.shape)


def cols_call(scal, parts, log_src, s1, s2):
    ns = s1.shape[1]
    n1, n2 = len(OFF1), len(OFF2)
    return pl.pallas_call(
        cols_kernel,
        name="cols",
        grid_spec=pltpu.PrefetchScalarGridSpec(
            num_scalar_prefetch=1,
            grid=(n1 + n2,),
            in_specs=[
                pl.BlockSpec(parts.shape, lambda i, sc: (0, 0, 0)),
                pl.BlockSpec(log_src.shape, lambda i, sc: (0, 0)),
                pl.BlockSpec((B, ns), lambda i, sc: (jnp.minimum(i, n1 - 1), 0)),
                pl.BlockSpec((B, ns), lambda i, sc: (jnp.maximum(i - n1, 0), 0)),
            ],
            out_specs=[
                pl.BlockSpec((8, 128), lambda i, sc: (0, 0)),
                pl.BlockSpec((1, ns), lambda i, sc: (0, 0)),
                pl.BlockSpec((16, 8, 128), lambda i, sc: (0, 0, 0)),
            ],
            scratch_shapes=[pltpu.VMEM((8, 128), jnp.float32)],
        ),
        out_shape=[
            jax.ShapeDtypeStruct((8, 128), jnp.float32),
            jax.ShapeDtypeStruct((1, ns), jnp.float32),
            jax.ShapeDtypeStruct((16, 8, 128), jnp.float32),
        ],
    )(scal, parts, log_src, s1, s2)


def moved_kernel(scal, parts, lt1, lt2, sp, s1, s2, t1, t2, pot_out, mine_out, theirs_out, mass_out, tp1, tp2, lse):
    n = pl.program_id(0)

    @pl.when(n == 0)
    def _():
        lse[...] = merged_lse(parts[...])
        for p in range(len(OFF)):
            slot = scal[2 + p]
            row = lse[pl.ds(slot // 2, 1), :]
            row = jnp.where(slot % 2 == 0, row[:, :B], row[:, B:])
            first = p < len(OFF1)
            lt, tp, q = (lt1, tp1, p) if first else (lt2, tp2, p - len(OFF1))
            tpot = lt[q : q + 1, 0:B] * LOG2E - row
            if p == 0:
                pot_out[...] = tpot * LN2
            tp[q * B : (q + 1) * B, :] = jnp.broadcast_to(to_col(tpot), (B, 128))

    rep = CH // 128
    w1 = jnp.exp2(s1[...] + sp[...] + jnp.concatenate([tp1[...]] * rep, axis=1))
    w2 = jnp.exp2(s2[...] + sp[...] + jnp.concatenate([tp2[...]] * rep, axis=1))
    mass = jnp.sum(w1, axis=0, keepdims=True) + jnp.sum(w2, axis=0, keepdims=True)
    moved = jnp.dot(t1[...], w1.astype(jnp.bfloat16), preferred_element_type=jnp.float32)
    moved = moved + jnp.dot(t2[...], w2.astype(jnp.bfloat16), preferred_element_type=jnp.float32)
    half = moved.shape[0] // 2
    mass_out[...] = mass
    mine_out[...] = moved[:half].astype(jnp.bfloat16)
    theirs_out[0:half, :] = moved[half:].astype(jnp.bfloat16)
    hi = mass.astype(jnp.bfloat16)
    lo = (mass - hi.astype(jnp.float32)).astype(jnp.bfloat16)
    pad = jnp.zeros((6, mass.shape[1]), jnp.float32)
    theirs_out[half : half + 8, :] = jnp.concatenate([hi.astype(jnp.float32), lo.astype(jnp.float32), pad], axis=0).astype(jnp.bfloat16)


def moved_call(scal, parts, lt1, lt2, sp, s1, s2, t1, t2):
    ns = s1.shape[1]
    f = t1.shape[0]
    const2 = lambda a: pl.BlockSpec(a.shape, lambda n, sc: (0, 0))
    return pl.pallas_call(
        moved_kernel,
        name="moved",
        grid_spec=pltpu.PrefetchScalarGridSpec(
            num_scalar_prefetch=1,
            grid=(ns // CH,),
            in_specs=[
                pl.BlockSpec(parts.shape, lambda n, sc: (0, 0, 0)),
                const2(lt1),
                const2(lt2),
                pl.BlockSpec((1, CH), lambda n, sc: (0, n)),
                pl.BlockSpec((s1.shape[0], CH), lambda n, sc: (0, n)),
                pl.BlockSpec((s2.shape[0], CH), lambda n, sc: (0, n)),
                const2(t1),
                const2(t2),
            ],
            out_specs=[
                pl.BlockSpec((1, B), lambda n, sc: (0, 0)),
                pl.BlockSpec((f // 2, CH), lambda n, sc: (0, n)),
                pl.BlockSpec((f // 2 + 8, CH), lambda n, sc: (0, n)),
                pl.BlockSpec((1, CH), lambda n, sc: (0, n)),
            ],
            scratch_shapes=[
                pltpu.VMEM((s1.shape[0], 128), jnp.float32),
                pltpu.VMEM((s2.shape[0], 128), jnp.float32),
                pltpu.VMEM((8, 128), jnp.float32),
            ],
        ),
        out_shape=[
            jax.ShapeDtypeStruct((1, B), jnp.float32),
            jax.ShapeDtypeStruct((f // 2, ns), jnp.bfloat16),
            jax.ShapeDtypeStruct((f // 2 + 8, ns), jnp.bfloat16),
            jax.ShapeDtypeStruct((1, ns), jnp.float32),
        ],
    )(scal, parts, lt1, lt2, sp, s1, s2, t1, t2)


def pack_kernel(mine, theirs, mass, out):
    g = pl.program_id(0)
    f32 = jnp.float32
    both = mine[...].astype(f32) + theirs[pl.ds(pl.multiple_of(g * 32, 32), 32), :].astype(f32)
    extra = theirs[256:264, :].astype(f32)
    total = mass[...] + extra[0:1] + extra[1:2]
    hi = total.astype(jnp.bfloat16).astype(f32)
    lo = total - hi
    for h in range(2):
        for q in range(8):
            at = (h * 8 + q) * 128
            out[h, 0, q * 32 : (q + 1) * 32, :] = both[:, at : at + 128].astype(jnp.bfloat16)
        rows = [v[:, (h * 8 + q) * 128 : (h * 8 + q + 1) * 128] for v in (hi, lo) for q in range(8)]
        out[h, 0, 256:272, :] = jnp.concatenate(rows, axis=0).astype(jnp.bfloat16)


def pack_call(mine, theirs, mass):
    ns = mine.shape[1]
    return pl.pallas_call(
        pack_kernel,
        name="pack",
        grid=(8,),
        in_specs=[
            pl.BlockSpec((32, ns), lambda g: (g, 0)),
            pl.BlockSpec(theirs.shape, lambda g: (0, 0)),
            pl.BlockSpec(mass.shape, lambda g: (0, 0)),
        ],
        out_specs=pl.BlockSpec((2, 1, 272, 128), lambda g: (0, g, 0, 0)),
        out_shape=jax.ShapeDtypeStruct((2, 8, 272, 128), jnp.bfloat16),
    )(mine, theirs, mass)


def finish_kernel(parts, out):
    total = jnp.sum(parts[...].astype(jnp.float32), axis=0)
    for q in range(8):
        mass = total[256 + q : 257 + q, :] + total[264 + q : 265 + q, :]
        image = total[q * 32 : (q + 1) * 32, :] / mass
        out[q * 128 : (q + 1) * 128, :] = image.T.astype(jnp.bfloat16)


def finish_call(parts):
    return pl.pallas_call(
        finish_kernel,
        name="finish",
        out_shape=jax.ShapeDtypeStruct((1024, 32), jnp.bfloat16),
    )(parts)


def body(sources, log_src, targets, potential, log_tgt):
    bf = jnp.bfloat16
    f = sources.shape[1]
    scale2 = LOG2E / math.sqrt(f)
    z, yh, c = lax.axis_index("z"), lax.axis_index("yh"), lax.axis_index("c")
    scal = jnp.concatenate([jnp.stack([yh, c]), (z + jnp.array(OFF, jnp.int32)) % 16]).astype(jnp.int32)

    extra = jnp.stack(thirds(potential) + thirds(log_tgt) + [jnp.zeros_like(potential)] * 2)
    extra = jnp.pad(extra, ((0, 0), (0, f - B))).astype(bf)
    own = jnp.concatenate([targets, extra], axis=0)
    ls = jnp.pad(jnp.stack(thirds(log_src.reshape(2, 512)), axis=1), ((0, 0), (0, 5), (0, 0))).astype(bf)
    halves = jnp.concatenate([sources.reshape(2, 512, f), ls], axis=1)
    sent = lax.dynamic_index_in_dim(halves, c, 0, keepdims=False)
    ra = from_z(own, 4)
    la = from_z(own, -5)
    near = lax.ppermute(sent, ("yh", "yl"), [(0, 3), (3, 0), (1, 2), (2, 1)])
    rb = from_z(joined([own, ra]), 2)
    lb = from_z(joined([la, own]), -2)
    swapped = lax.ppermute(near, "c", [(0, 1), (1, 0)])
    rc = from_z(joined([own, rb, ra, la]), 1)
    lc = from_z(joined([own, lb, la]), -1)
    first = jnp.where(c == 0, near, swapped)
    second = jnp.where(c == 0, swapped, near)
    other = jnp.concatenate([first[:512], second[:512]], axis=0)
    whole = [first[512:].astype(jnp.float32), second[512:].astype(jnp.float32)]
    other_log = jnp.concatenate([w[0] + w[1] + w[2] for w in whole])
    src = jnp.concatenate([jnp.where(yh == 0, sources, other), jnp.where(yh == 0, other, sources)], axis=0)
    log_all = jnp.concatenate([jnp.where(yh == 0, log_src, other_log), jnp.where(yh == 0, other_log, log_src)])
    log_all = log_all.reshape(16, 128)

    s1, t1, lt1, lse1 = scores_call(scal, src, [own, ra, la, rb, lb], [(0, 0), (1, 0), (2, 0), (3, 0), (3, 1), (4, 0)], scale2)
    s2, t2, lt2, rows = scores_call(
        scal, src, [lb, rc, lc], [(0, 1)] + [(1, k) for k in range(5)] + [(2, k) for k in range(4)], scale2, lse1
    )
    row_parts = lax.all_to_all(rows, PLANE, split_axis=0, concat_axis=0, tiled=True)
    src_pot, sp, cols = cols_call(scal, row_parts, log_all, s1, s2)
    col_parts = lax.all_to_all(cols, "z", split_axis=0, concat_axis=0, tiled=True)
    tgt_pot, mine, theirs, mass = moved_call(scal, col_parts, lt1, lt2, sp, s1, s2, t1, t2)
    theirs = lax.ppermute(theirs, "c", [(0, 1), (1, 0)])
    packed = pack_call(mine, theirs, mass).reshape(16, 272, 128)
    parts = lax.all_to_all(packed, CHIPS, split_axis=0, concat_axis=0, tiled=True)
    mapped = finish_call(parts)
    return (src_pot.reshape(-1), tgt_pot.reshape(-1), mapped)


def solution(mesh):
    torus = Mesh(mesh.devices.reshape(16, 2, 2, 4, 2), AXES)
    src, every = ("z", "yh"), ("z", "yh", "yl", "x", "c")
    return jax.shard_map(
        body,
        mesh=torus,
        in_specs=(P(src, None), P(src), P(every, None), P(every), P(every)),
        out_specs=(P(src), P(every), P(src, ("yl", "x", "c"))),
        check_vma=False,
    )
```

time: 229 us -> 170 us (0.74)
  blocking collectives: 104 us -> 39.6 us
  Pallas kernels: 0 us -> 43.7 us
  starting transfers between devices: 26.8 us -> 50.8 us
  waiting for transfers between devices: 44.9 us -> 22.1 us
  between operations: 15 us -> 1.02 us
  matrix products: 11.1 us -> 0 us
  other arithmetic: 16.2 us -> 7.26 us
  local copies, waits for them, and re-layouts: 10 us -> 4.47 us
    all_gather x3 -> x0, blocking collectives: 78.1 us -> none  [gathered_by_axis(): nearer = lax.all_gather(array, axes[-1], axis=dim, tiled=True)]
    pallas_call x0 -> x6, Pallas kernels: none -> 43.7 us  [the longest x2 13.4 us: scores_call(): pl.pallas_call(lambda *a: scores_kernel(picks, last, len(msgs), scale2, *...]
    ppermute x0 -> x9, starting transfers between devices: none -> 42.5 us  [the longest x6 28 us: from_z(): return lax.ppermute(array, 'z', [((i + d) % n, i) for i in range(n)])]
    all_gather x1 -> x0, waiting for transfers between devices: 29.8 us -> none  [gathered_by_axis(): nearer = lax.all_gather(array, axes[-1], axis=dim, tiled=True)]
    all_to_all x1 -> x2, blocking collectives: 21.1 us -> 39.6 us  [the longest x1 21.7 us: body(): lax.all_to_all(packed, CHIPS, split_axis=0, concat_axis=0, tiled=True)]
    all_to_all x3 -> x1, starting transfers between devices: 26.7 us -> 8.23 us  [body(): lax.all_to_all(rows, PLANE, split_axis=0, concat_axis=0, tiled=True)]
    ppermute x0 -> x9, waiting for transfers between devices: none -> 13.8 us  [the longest x6 11.3 us: from_z(): return lax.ppermute(array, 'z', [((i + d) % n, i) for i in range(n)])]
    dot_general x2 -> x0, matrix products: 11.1 us -> none  [the longest x1 7.07 us: body(): jnp.dot(weight.astype(jnp.bfloat16), whole, preferred_element_type=jnp.fl...]
  transfers between devices with their start and end apart: 4 -> 10, of which waited for: 2 -> 5; matrix products, arithmetic and copies ran while one was open for 5% -> 3% of each run, Pallas kernels for 0% -> 3%
where the time goes in v1:
time: 170 us; the launch traced here: 169 us
  starting transfers between devices  50.8 us (30%)
  Pallas kernels  43.7 us (26%)
  blocking collectives  39.6 us (23%)
  waiting for transfers between devices  22.1 us (13%)
  other arithmetic  7.26 us (4%)
  local copies, waits for them, and re-layouts  4.47 us (3%)
    ppermute x6, starting transfers between devices, from_z(): return lax.ppermute(array, 'z', [((i + d) % n, i) for i in range(n)])  28 us
    all_to_all x1, blocking collectives, body(): lax.all_to_all(packed, CHIPS, split_axis=0, concat_axis=0, tiled=True)  21.7 us
    all_to_all x1, blocking collectives, body(): lax.all_to_all(cols, 'z', split_axis=0, concat_axis=0, tiled=True)  17.9 us
    pallas_call x2, Pallas kernels, scores_call(): pl.pallas_call(lambda *a: scores_kernel(picks, last, len(msgs), scale2, *...  13.4 us
    pallas_call x1, Pallas kernels, cols_call(): pl.pallas_call(cols_kernel, name='cols', grid_spec=pltpu.PrefetchScalarGr...  13.1 us
    ppermute x6, waiting for transfers between devices, from_z(): return lax.ppermute(array, 'z', [((i + d) % n, i) for i in range(n)])  11.3 us
    pallas_call x1, Pallas kernels, moved_call(): pl.pallas_call(moved_kernel, name='moved', grid_spec=pltpu.PrefetchScalar...  9.16 us
    all_to_all x1, waiting for transfers between devices, body(): lax.all_to_all(rows, PLANE, split_axis=0, concat_axis=0, tiled=True)  8.25 us
  transfers between devices with their start and end apart: 10, of which 5 were waited for; matrix products, arithmetic and copies ran while one was open for 3% of the time, Pallas kernels for 3%

profile of v1, /device:TPU:1, one launch (start us, length us, event | category | flops | bytes accessed | tf_op | source)
XLA Modules:
  0.0 169.0 jit_solution(1540760914855212103)
XLA Ops:
  2.2 13.3 %collective-permute-start.4 = (bf16[72,512]{1,0:T(8,128)(2,1)S(1)}, bf16[72,512]{1,0:T(8,128)(2,1)S(1)}, u32[]{:S(2)}, u32[]{:S(2)}) collective-permute-start(bf16[72,512]{1,0:T(8,128)(2,1)S(1)} %pad_maximum_fusion.4.a_2_), channel_id=1, source_target_pairs={{128,0},{160,32},{192,64},{224,96},{256,128},{288,160},{320,192},{... | collective-permute-start | bytes 221192 | tf_op jit(solution)/shard_map/ppermute | solution.py:25
  15.5 1.9 %collective-permute-start.2 = (bf16[72,512]{1,0:T(8,128)(2,1)S(1)}, bf16[72,512]{1,0:T(8,128)(2,1)S(1)}, u32[]{:S(2)}, u32[]{:S(2)}) collective-permute-start(bf16[72,512]{1,0:T(8,128)(2,1)S(1)} %pad_maximum_fusion.4.a_2_), channel_id=1, source_target_pairs={{352,0},{384,32},{416,64},{448,96},{480,128},{0,160},{32,192},{64,... | collective-permute-start | bytes 221192 | tf_op jit(solution)/shard_map/ppermute | solution.py:25
  19.3 4.6 %collective-permute-start = (bf16[520,512]{1,0:T(8,128)(2,1)S(1)}, bf16[520,512]{1,0:T(8,128)(2,1)S(1)}, u32[]{:S(2)}, u32[]{:S(2)}) collective-permute-start(bf16[520,512]{1,0:T(8,128)(2,1)S(1)} %fusion.1), channel_id=1, source_target_pairs={{0,24},{24,0},{8,16},{16,8},{1,25},{25,1},{9,17},{17,9},{2,26},{26... | collective-permute-start | bytes 1597448 | tf_op jit(solution)/shard_map/ppermute | solution.py:350
  24.6 5.3 %collective-permute-done.2.a_4_ = bf16[72,512]{1,0:T(8,128)(2,1)S(1)} collective-permute-done((bf16[72,512]{1,0:T(8,128)(2,1)S(1)}, bf16[72,512]{1,0:T(8,128)(2,1)S(1)}, u32[]{:S(2)}, u32[]{:S(2)}) %collective-permute-start.2) | collective-permute-done | bytes 73760 | tf_op jit(solution)/shard_map/ppermute | solution.py:25
  30.0 3.4 %collective-permute-start.5 = (bf16[144,512]{1,0:T(8,128)(2,1)S(1)}, bf16[144,512]{1,0:T(8,128)(2,1)S(1)}, u32[]{:S(2)}, u32[]{:S(2)}) collective-permute-start(bf16[144,512]{1,0:T(8,128)(2,1)S(1)} %get-tuple-element.44), channel_id=1, source_target_pairs={{64,0},{96,32},{128,64},{160,96},{192,128},{224,160},{256,192},{28... | collective-permute-start | bytes 442376 | tf_op jit(solution)/shard_map/ppermute | solution.py:25
  34.1 2.8 %collective-permute-start.3 = (bf16[144,512]{1,0:T(8,128)(2,1)S(1)}, bf16[144,512]{1,0:T(8,128)(2,1)S(1)}, u32[]{:S(2)}, u32[]{:S(2)}) collective-permute-start(bf16[144,512]{1,0:T(8,128)(2,1)S(1)} %get-tuple-element.45), channel_id=1, source_target_pairs={{448,0},{480,32},{0,64},{32,96},{64,128},{96,160},{128,192},{160,2... | collective-permute-start | bytes 442376 | tf_op jit(solution)/shard_map/ppermute | solution.py:25
  36.9 2.6 %collective-permute-done.5.a_5_ = bf16[144,512]{1,0:T(8,128)(2,1)S(1)} collective-permute-done((bf16[144,512]{1,0:T(8,128)(2,1)S(1)}, bf16[144,512]{1,0:T(8,128)(2,1)S(1)}, u32[]{:S(2)}, u32[]{:S(2)}) %collective-permute-start.5) | collective-permute-done | bytes 147488 | tf_op jit(solution)/shard_map/ppermute | solution.py:25
  39.6 3.3 %collective-permute-done.3.a_6_.a_2_ = bf16[144,512]{1,0:T(8,128)(2,1)S(1)} collective-permute-done((bf16[144,512]{1,0:T(8,128)(2,1)S(1)}, bf16[144,512]{1,0:T(8,128)(2,1)S(1)}, u32[]{:S(2)}, u32[]{:S(2)}) %collective-permute-start.3) | collective-permute-done | bytes 147488 | tf_op jit(solution)/shard_map/ppermute | solution.py:25
  43.0 5.9 %collective-permute-start.1 = (bf16[520,512]{1,0:T(8,128)(2,1)S(1)}, bf16[520,512]{1,0:T(8,128)(2,1)S(1)}, u32[]{:S(2)}, u32[]{:S(2)}) collective-permute-start(bf16[520,512]{1,0:T(8,128)(2,1)S(1)} %collective-permute-done), channel_id=1, source_target_pairs={{0,1},{1,0},{2,3},{3,2},{4,5},{5,4},{6,7},{7,6},{8,9},{9,8},{10,11... | collective-permute-start | bytes 1597448 | tf_op jit(solution)/shard_map/ppermute | solution.py:353
  49.0 2.4 %collective-permute-start.7 = (bf16[288,512]{1,0:T(8,128)(2,1)S(1)}, bf16[288,512]{1,0:T(8,128)(2,1)S(1)}, u32[]{:S(2)}, u32[]{:S(2)}) collective-permute-start(bf16[288,512]{1,0:T(8,128)(2,1)S(1)} %get-tuple-element.40), channel_id=1, source_target_pairs={{480,0},{0,32},{32,64},{64,96},{96,128},{128,160},{160,192},{192,2... | collective-permute-start | bytes 884744 | tf_op jit(solution)/shard_map/ppermute | solution.py:25
  51.3 4.3 %collective-permute-start.6 = (bf16[360,512]{1,0:T(8,128)(2,1)S(1)}, bf16[360,512]{1,0:T(8,128)(2,1)S(1)}, u32[]{:S(2)}, u32[]{:S(2)}) collective-permute-start(bf16[360,512]{1,0:T(8,128)(2,1)S(1)} %get-tuple-element.41), channel_id=1, source_target_pairs={{32,0},{64,32},{96,64},{128,96},{160,128},{192,160},{224,192},{256... | collective-permute-start | bytes 1105928 | tf_op jit(solution)/shard_map/ppermute | solution.py:25
  57.7 5.9 %scores_first.1 = (f32[384,2048]{1,0:T(8,128)}, bf16[512,384]{1,0:T(8,128)(2,1)}, f32[8,128]{1,0:T(8,128)}, f32[1,2048]{1,0:T(1,128)}) custom-call(s32[18]{0:T(128)} %pad_add_fusion.a_0_.scal, bf16[2048,512]{1,0:T(8,128)(2,1)} %pad_maximum_fusion.a_1_, bf16[72,512]{1,0:T(8,128)(2,1)} %copy-done.8, bf16[72,512]{1,0:T(8,128)(2,1)} %copy-done.5, ...), custom_call_target="tpu_custom_call" | custom-call | flops 805306368 | bytes 3145728 | tf_op jit(solution)/shard_map/scores_first/pallas_call | solution.py:117
  64.5 7.5 %scores_last.1 = (f32[640,2048]{1,0:T(8,128)}, bf16[512,640]{1,0:T(8,128)(2,1)}, f32[16,128]{1,0:T(8,128)}, f32[32,16,128]{2,1,0:T(8,128)}) custom-call(s32[18]{0:T(128)} %pad_add_fusion.a_0_.scal, bf16[2048,512]{1,0:T(8,128)(2,1)} %pad_maximum_fusion.a_1_, bf16[144,512]{1,0:T(8,128)(2,1)} %copy-done.6, bf16[360,512]{1,0:T(8,128)(2,1)} %copy-done.10, ...), custom_call_target="tpu_custom_call" | custom-call | flops 1342177280 | bytes 5242880 | tf_op jit(solution)/shard_map/scores_last/pallas_call | solution.py:117
  72.0 8.2 %all-to-all-start = ((f32[32,16,128]{2,1,0:T(8,128)}), f32[32,16,128]{2,1,0:T(8,128)S(1)}, u32[]{:S(2)}, u32[]{:S(2)}) async-start(f32[32,16,128]{2,1,0:T(8,128)} %get-tuple-element.19), calls=%async_computation | async-start | bytes 524288 | tf_op jit(solution)/shard_map/all_to_all | solution.py:369
  80.9 8.2 %all-to-all-done.parts = f32[32,16,128]{2,1,0:T(8,128)S(1)} async-done(((f32[32,16,128]{2,1,0:T(8,128)}), f32[32,16,128]{2,1,0:T(8,128)S(1)}, u32[]{:S(2)}, u32[]{:S(2)}) %all-to-all-start) | async-done | bytes 262176 | tf_op jit(solution)/shard_map/all_to_all | solution.py:369
  89.9 13.1 %cols.1 = (f32[8,128]{1,0:T(8,128)}, f32[1,2048]{1,0:T(1,128)}, f32[16,8,128]{2,1,0:T(8,128)}) custom-call(s32[18]{0:T(128)} %pad_add_fusion.a_0_.scal, f32[32,16,128]{2,1,0:T(8,128)} %copy-done.2, f32[16,128]{1,0:T(8,128)} %pad_maximum_fusion.5.log_src, f32[384,2048]{1,0:T(8,128)} %get-tuple-element.20.s1, f32[640,2048]{1,0:T(8,128)} %get-tuple-element.21.s2), custom_call_target="tpu_custom_call" | custom-call | tf_op jit(solution)/shard_map/cols/pallas_call | solution.py:186
  102.9 17.9 %all_to_all.15.parts = f32[16,8,128]{2,1,0:T(8,128)} all-to-all(f32[16,8,128]{2,1,0:T(8,128)} %get-tuple-element.23), channel_id=1, replica_groups=mesh['z'=16,'yh'=2,'yl'=2,'x'=4,'c'=2] {'z'}, dimensions={0} | all-to-all | bytes 131072 | tf_op jit(solution)/shard_map/all_to_all | solution.py:371
  120.9 9.2 %moved.1 = (f32[1,64]{1,0:T(1,128)}, bf16[256,2048]{1,0:T(8,128)(2,1)}, bf16[264,2048]{1,0:T(8,128)(2,1)}, f32[1,2048]{1,0:T(1,128)}) custom-call(s32[18]{0:T(128)} %pad_add_fusion.a_0_.scal, f32[16,8,128]{2,1,0:T(8,128)} %all_to_all.15.parts, f32[8,128]{1,0:T(8,128)} %get-tuple-element.24.lt1, f32[16,128]{1,0:T(8,128)} %get-tuple-element.25.lt2, ...), custom_call_target="tpu_custom_call" | custom-call | tf_op jit(solution)/shard_map/moved/pallas_call | solution.py:250
  130.0 4.0 %collective-permute-start.8 = (bf16[264,2048]{1,0:T(8,128)(2,1)}, bf16[264,2048]{1,0:T(8,128)(2,1)S(1)}, u32[]{:S(2)}, u32[]{:S(2)}) collective-permute-start(bf16[264,2048]{1,0:T(8,128)(2,1)} %get-tuple-element.31), channel_id=1, source_target_pairs={{0,1},{1,0},{2,3},{3,2},{4,5},{5,4},{6,7},{7,6},{8,9},{9,8},{10,11... | collective-permute-start | bytes 3244040 | tf_op jit(solution)/shard_map/ppermute | solution.py:373
  134.0 2.5 %collective-permute-done.8.theirs = bf16[264,2048]{1,0:T(8,128)(2,1)S(1)} collective-permute-done((bf16[264,2048]{1,0:T(8,128)(2,1)}, bf16[264,2048]{1,0:T(8,128)(2,1)S(1)}, u32[]{:S(2)}, u32[]{:S(2)}) %collective-permute-start.8) | collective-permute-done | bytes 1081376 | tf_op jit(solution)/shard_map/ppermute | solution.py:373
  137.5 5.9 %pack.1 = bf16[2,8,272,128]{3,2,1,0:T(8,128)(2,1)} custom-call(bf16[256,2048]{1,0:T(8,128)(2,1)} %get-tuple-element.30.mine, bf16[264,2048]{1,0:T(8,128)(2,1)} %copy-done.1, f32[1,2048]{1,0:T(1,128)} %get-tuple-element.32.mass), custom_call_target="tpu_custom_call" | custom-call | tf_op jit(solution)/shard_map/pack/pallas_call | solution.py:305
  143.4 21.7 %all_to_all.16.parts = bf16[16,272,128]{2,1,0:T(8,128)(2,1)} all-to-all(bf16[16,272,128]{2,1,0:T(8,128)(2,1)} %bitcast.27), channel_id=1, replica_groups=mesh['z'=16,'yh'=2,'yl'=2,'x'=4,'c'=2] {'yh','yl','x'}, dimensions={0} | all-to-all | bytes 2228224 | tf_op jit(solution)/shard_map/all_to_all | solution.py:375
  165.1 2.2 %finish.1 = bf16[1024,32]{1,0:T(8,128)(2,1)} custom-call(bf16[16,272,128]{2,1,0:T(8,128)(2,1)} %all_to_all.16.parts), custom_call_target="tpu_custom_call" | custom-call | tf_op jit(solution)/shard_map/finish/pallas_call | solution.py:328
  167.3 1.7 %copy.9 = bf16[1024,32]{0,1:T(8,128)(2,1)} copy(bf16[1024,32]{1,0:T(8,128)(2,1)} %finish.1) | data formatting | bytes 131072
  (64 shorter events, 10.1 us)
Async XLA Ops:
  0.6 29.4 %copy-start.3 = (bf16[64,512]{1,0:T(8,128)(2,1)S(1)}, bf16[64,512]{1,0:T(8,128)(2,1)}, u32[]{:S(2)}) copy-start(bf16[64,512]{1,0:T(8,128)(2,1)} %param.8) | copy-start | bytes 196612
  2.2 53.5 %copy-start.8 = (bf16[72,512]{1,0:T(8,128)(2,1)}, bf16[72,512]{1,0:T(8,128)(2,1)S(1)}, u32[]{:S(2)}) copy-start(bf16[72,512]{1,0:T(8,128)(2,1)S(1)} %pad_maximum_fusion.4.a_2_) | copy-start | bytes 221188
  2.2 22.4 %collective-permute-start.4 = (bf16[72,512]{1,0:T(8,128)(2,1)S(1)}, bf16[72,512]{1,0:T(8,128)(2,1)S(1)}, u32[]{:S(2)}, u32[]{:S(2)}) collective-permute-start(bf16[72,512]{1,0:T(8,128)(2,1)S(1)} %pad_maximum_fusion.4.a_2_), channel_id=1, source_target_pairs={{128,0},{160,32},{192,64},{224,96},{256,128},{288,160},{320,192},{... | collective-permute-start | bytes 221192 | tf_op jit(solution)/shard_map/ppermute | solution.py:25
  15.5 14.5 %collective-permute-start.2 = (bf16[72,512]{1,0:T(8,128)(2,1)S(1)}, bf16[72,512]{1,0:T(8,128)(2,1)S(1)}, u32[]{:S(2)}, u32[]{:S(2)}) collective-permute-start(bf16[72,512]{1,0:T(8,128)(2,1)S(1)} %pad_maximum_fusion.4.a_2_), channel_id=1, source_target_pairs={{352,0},{384,32},{416,64},{448,96},{480,128},{0,160},{32,192},{64,... | collective-permute-start | bytes 221192 | tf_op jit(solution)/shard_map/ppermute | solution.py:25
  19.3 23.7 %collective-permute-start = (bf16[520,512]{1,0:T(8,128)(2,1)S(1)}, bf16[520,512]{1,0:T(8,128)(2,1)S(1)}, u32[]{:S(2)}, u32[]{:S(2)}) collective-permute-start(bf16[520,512]{1,0:T(8,128)(2,1)S(1)} %fusion.1), channel_id=1, source_target_pairs={{0,24},{24,0},{8,16},{16,8},{1,25},{25,1},{9,17},{17,9},{2,26},{26... | collective-permute-start | bytes 1597448 | tf_op jit(solution)/shard_map/ppermute | solution.py:350
  24.6 31.2 %copy-start.5 = (bf16[72,512]{1,0:T(8,128)(2,1)}, bf16[72,512]{1,0:T(8,128)(2,1)S(1)}, u32[]{:S(2)}) copy-start(bf16[72,512]{1,0:T(8,128)(2,1)S(1)} %collective-permute-done.4.a_3_) | copy-start | bytes 221188
  30.0 25.8 %copy-start.4 = (bf16[72,512]{1,0:T(8,128)(2,1)}, bf16[72,512]{1,0:T(8,128)(2,1)S(1)}, u32[]{:S(2)}) copy-start(bf16[72,512]{1,0:T(8,128)(2,1)S(1)} %collective-permute-done.2.a_4_) | copy-start | bytes 221188
  30.0 9.5 %collective-permute-start.5 = (bf16[144,512]{1,0:T(8,128)(2,1)S(1)}, bf16[144,512]{1,0:T(8,128)(2,1)S(1)}, u32[]{:S(2)}, u32[]{:S(2)}) collective-permute-start(bf16[144,512]{1,0:T(8,128)(2,1)S(1)} %get-tuple-element.44), channel_id=1, source_target_pairs={{64,0},{96,32},{128,64},{160,96},{192,128},{224,160},{256,192},{28... | collective-permute-start | bytes 442376 | tf_op jit(solution)/shard_map/ppermute | solution.py:25
  34.1 8.8 %collective-permute-start.3 = (bf16[144,512]{1,0:T(8,128)(2,1)S(1)}, bf16[144,512]{1,0:T(8,128)(2,1)S(1)}, u32[]{:S(2)}, u32[]{:S(2)}) collective-permute-start(bf16[144,512]{1,0:T(8,128)(2,1)S(1)} %get-tuple-element.45), channel_id=1, source_target_pairs={{448,0},{480,32},{0,64},{32,96},{64,128},{96,160},{128,192},{160,2... | collective-permute-start | bytes 442376 | tf_op jit(solution)/shard_map/ppermute | solution.py:25
  39.5 16.2 %copy-start.7 = (bf16[144,512]{1,0:T(8,128)(2,1)}, bf16[144,512]{1,0:T(8,128)(2,1)S(1)}, u32[]{:S(2)}) copy-start(bf16[144,512]{1,0:T(8,128)(2,1)S(1)} %collective-permute-done.5.a_5_) | copy-start | bytes 442372
  42.9 12.9 %copy-start.6 = (bf16[144,512]{1,0:T(8,128)(2,1)}, bf16[144,512]{1,0:T(8,128)(2,1)S(1)}, u32[]{:S(2)}) copy-start(bf16[144,512]{1,0:T(8,128)(2,1)S(1)} %collective-permute-done.3.a_6_.a_2_) | copy-start | bytes 442372
  43.0 12.6 %collective-permute-start.1 = (bf16[520,512]{1,0:T(8,128)(2,1)S(1)}, bf16[520,512]{1,0:T(8,128)(2,1)S(1)}, u32[]{:S(2)}, u32[]{:S(2)}) collective-permute-start(bf16[520,512]{1,0:T(8,128)(2,1)S(1)} %collective-permute-done), channel_id=1, source_target_pairs={{0,1},{1,0},{2,3},{3,2},{4,5},{5,4},{6,7},{7,6},{8,9},{9,8},{10,11... | collective-permute-start | bytes 1597448 | tf_op jit(solution)/shard_map/ppermute | solution.py:353
  49.0 14.7 %collective-permute-start.7 = (bf16[288,512]{1,0:T(8,128)(2,1)S(1)}, bf16[288,512]{1,0:T(8,128)(2,1)S(1)}, u32[]{:S(2)}, u32[]{:S(2)}) collective-permute-start(bf16[288,512]{1,0:T(8,128)(2,1)S(1)} %get-tuple-element.40), channel_id=1, source_target_pairs={{480,0},{0,32},{32,64},{64,96},{96,128},{128,160},{160,192},{192,2... | collective-permute-start | bytes 884744 | tf_op jit(solution)/shard_map/ppermute | solution.py:25
  51.3 4.5 %copy-start = (bf16[1024,512]{1,0:T(8,128)(2,1)S(1)}, bf16[1024,512]{1,0:T(8,128)(2,1)}, u32[]{:S(2)}) copy-start(bf16[1024,512]{1,0:T(8,128)(2,1)} %param.6) | copy-start | bytes 3145732
  51.3 12.3 %collective-permute-start.6 = (bf16[360,512]{1,0:T(8,128)(2,1)S(1)}, bf16[360,512]{1,0:T(8,128)(2,1)S(1)}, u32[]{:S(2)}, u32[]{:S(2)}) collective-permute-start(bf16[360,512]{1,0:T(8,128)(2,1)S(1)} %get-tuple-element.41), channel_id=1, source_target_pairs={{32,0},{64,32},{96,64},{128,96},{160,128},{192,160},{224,192},{256... | collective-permute-start | bytes 1105928 | tf_op jit(solution)/shard_map/ppermute | solution.py:25
  63.6 0.7 copy-start.11
  63.7 0.9 copy-start.10
  64.5 15.8 %copy-start.9 = (f32[1024]{0:T(1024)S(1)}, f32[1024]{0:T(1024)}, u32[]{:S(2)}) copy-start(f32[1024]{0:T(1024)} %param.7) | copy-start | bytes 12292
  72.0 17.1 %all-to-all-start = ((f32[32,16,128]{2,1,0:T(8,128)}), f32[32,16,128]{2,1,0:T(8,128)S(1)}, u32[]{:S(2)}, u32[]{:S(2)}) async-start(f32[32,16,128]{2,1,0:T(8,128)} %get-tuple-element.19), calls=%async_computation | async-start | bytes 524288 | tf_op jit(solution)/shard_map/all_to_all | solution.py:369
  89.2 0.7 copy-start.2
  130.0 6.5 %collective-permute-start.8 = (bf16[264,2048]{1,0:T(8,128)(2,1)}, bf16[264,2048]{1,0:T(8,128)(2,1)S(1)}, u32[]{:S(2)}, u32[]{:S(2)}) collective-permute-start(bf16[264,2048]{1,0:T(8,128)(2,1)} %get-tuple-element.31), channel_id=1, source_target_pairs={{0,1},{1,0},{2,3},{3,2},{4,5},{5,4},{6,7},{7,6},{8,9},{9,8},{10,11... | collective-permute-start | bytes 3244040 | tf_op jit(solution)/shard_map/ppermute | solution.py:373
  136.5 1.0 copy-start.1

commit v2 on v1

v2 whole, which is shorter than its diff:
```python
import math

import jax
import jax.numpy as jnp
from jax import lax
from jax.experimental import pallas as pl
from jax.experimental.pallas import tpu as pltpu
from jax.sharding import Mesh
from jax.sharding import PartitionSpec as P

AXES = ("z", "yh", "yl", "x", "c")
PLANE = ("yh", "yl", "x", "c")
CHIPS = ("yh", "yl", "x")
LOG2E = math.log2(math.e)
LN2 = math.log(2.0)
B = 64
A8 = 8
OFF1 = (0, 4, 11, 2, 6, 9)
OFF2 = (14, 1, 3, 7, 5, 12, 15, 8, 13, 10)
OFF = OFF1 + OFF2
PICKS = ((0, 0), (1, 0), (2, 0), (3, 0), (3, 1), (4, 0), (4, 1)) + tuple((5, k) for k in range(5)) + tuple((6, k) for k in range(4))
PICKS1 = PICKS[:6]
PICKS2 = tuple((m - 4, k) for m, k in PICKS[6:])


def from_z(array, d):
    n = lax.axis_size("z")
    return lax.ppermute(array, "z", [((i + d) % n, i) for i in range(n)])


def thirds(v):
    hi = lax.reduce_precision(v, 8, 7)
    lo = lax.reduce_precision(v - hi, 8, 7)
    return [hi, lo, v - hi - lo]


def joined(messages):
    ks = [m.shape[0] // (B + A8) for m in messages]
    rows = [m[: k * B] for m, k in zip(messages, ks)]
    extra = [m[k * B :] for m, k in zip(messages, ks)]
    return jnp.concatenate(rows + extra, axis=0)


def eye(n):
    return lax.broadcasted_iota(jnp.int32, (n, n), 0) == lax.broadcasted_iota(jnp.int32, (n, n), 1)


def to_col(row):
    n = row.shape[1]
    return jnp.sum(jnp.where(eye(n), jnp.broadcast_to(row, (n, n)), 0.0), axis=1, keepdims=True)


def to_row(col):
    n = col.shape[0]
    return jnp.sum(jnp.where(eye(n), jnp.broadcast_to(col, (n, n)), 0.0), axis=0, keepdims=True)


CH = 512
MIB = 1 << 20


def params(mib):
    return pltpu.CompilerParams(vmem_limit_bytes=mib * MIB)


SMEM = pl.BlockSpec(memory_space=pltpu.SMEM)
WHOLE = pl.BlockSpec(memory_space=pltpu.VMEM)


def block_of(msgs, m, k):
    total = msgs[m].shape[0] // (B + A8)
    extra = msgs[m][total * B + k * A8 : total * B + (k + 1) * A8, 0:128]
    return msgs[m].at[k * B : (k + 1) * B], extra.astype(jnp.float32)


def scores_kernel(picks, last, n_msg, scale2, src, *refs):
    msgs = refs[:n_msg]
    rest = refs[n_msg:]
    if last:
        lse_in, s_out, lse_out, tg, pot = rest
    else:
        s_out, lse_out, tg, pot = rest
    t = tg.shape[0]
    for p, (m, k) in enumerate(picks):
        rows, ex = block_of(msgs, m, k)
        tg[p * B : (p + 1) * B, :] = rows[...]
        po = (ex[0:1] + ex[1:2] + ex[2:3]) * LOG2E
        pot[p * B : (p + 1) * B, :] = jnp.broadcast_to(to_col(po[:, :B]), (B, 128))

    for n in range(src.shape[0] // CH):
        at = slice(n * CH, (n + 1) * CH)
        s_out[:, at] = (
            lax.dot_general(tg[...], src[at, :], (((1,), (1,)), ((), ())), preferred_element_type=jnp.float32) * scale2
        )

        def shifted(r):
            return s_out[r : r + 32, at] + jnp.concatenate([pot[r : r + 32, :]] * (CH // 128), axis=1)

        top = jnp.full((8, CH), -jnp.inf, jnp.float32)
        for r in range(0, t, 32):
            top = jnp.maximum(top, jnp.max(shifted(r).reshape(4, 8, CH), axis=0))
        top = jnp.max(top, axis=0, keepdims=True)
        tot = jnp.zeros((8, CH), jnp.float32)
        for r in range(0, t, 32):
            tot = tot + jnp.sum(jnp.exp2(shifted(r) - top).reshape(4, 8, CH), axis=0)
        lse = top + jnp.log2(jnp.sum(tot, axis=0, keepdims=True))
        if last:
            a = lse_in[:, at]
            hi = jnp.maximum(a, lse)
            lse = hi + jnp.log2(jnp.exp2(a - hi) + jnp.exp2(lse - hi))
            for i in range(CH // 128):
                piece = lse[:, i * 128 : (i + 1) * 128]
                q = n * (CH // 128) + i
                lse_out[:, q : q + 1, :] = jnp.broadcast_to(piece[None], (lse_out.shape[0], 1, 128))
        else:
            lse_out[:, at] = lse


def scores_call(src, msgs, picks, scale2, lse_in=None):
    t = len(picks) * B
    ns, f = src.shape
    last = lse_in is not None
    lse_shape = (32, ns // 128, 128) if last else (1, ns)
    args = [src, *msgs] + ([lse_in] if last else [])
    return pl.pallas_call(
        lambda *a: scores_kernel(picks, last, len(msgs), scale2, *a),
        name="scores_last" if last else "scores_first",
        in_specs=[WHOLE] * len(args),
        out_specs=[WHOLE] * 2,
        scratch_shapes=[pltpu.VMEM((t, f), jnp.bfloat16), pltpu.VMEM((t, 128), jnp.float32)],
        out_shape=[jax.ShapeDtypeStruct((t, ns), jnp.float32), jax.ShapeDtypeStruct(lse_shape, jnp.float32)],
        compiler_params=params(20),
        cost_estimate=pl.CostEstimate(flops=2 * t * ns * f, bytes_accessed=4 * t * ns, transcendentals=t * ns),
    )(*args)


def prepare_kernel(scal, *refs):
    msgs, (_, tgt_out, lt_out, tg) = refs[:-4], refs[-4:]
    core = scal[1]
    for p, (m, k) in enumerate(PICKS):
        rows, ex = block_of(msgs, m, k)
        tg[p * B : (p + 1) * B, :] = rows[...]
        lt_out[p : p + 1, :] = (ex[3:4] + ex[4:5] + ex[5:6]) * LOG2E
    for q in range(tg.shape[0] // 128):
        flipped = tg[q * 128 : (q + 1) * 128, :].T
        for t in range(16):
            at = pl.multiple_of((((t % 2) ^ core) * 8 + t // 2) * 32, 32)
            tgt_out[pl.ds(at, 32), q * 128 : (q + 1) * 128] = flipped[t * 32 : (t + 1) * 32, :]


def prepare_call(scal, msgs, after):
    t, f = len(OFF) * B, msgs[0].shape[1]
    return pl.pallas_call(
        prepare_kernel,
        name="prepare",
        in_specs=[SMEM] + [WHOLE] * len(msgs) + [pl.BlockSpec(memory_space=pl.ANY)],
        out_specs=[WHOLE] * 2,
        scratch_shapes=[pltpu.VMEM((t, f), jnp.bfloat16)],
        out_shape=[jax.ShapeDtypeStruct((f, t), jnp.bfloat16), jax.ShapeDtypeStruct((len(OFF), 128), jnp.float32)],
        compiler_params=params(16),
        cost_estimate=pl.CostEstimate(flops=2 * t * f * 1024, bytes_accessed=4 * t * f, transcendentals=0),
    )(scal, *msgs, after)


def merged_lse(parts):
    top = jnp.max(parts, axis=0)
    return top + jnp.log2(jnp.sum(jnp.exp2(parts - top[None]), axis=0))


def cols_kernel(scal, parts, log_src, s1, s2, pot_out, sp_out, msg_out, held):
    sp = log_src[...] * LOG2E - merged_lse(parts[...])
    for r in range(sp.shape[0]):
        sp_out[:, r * 128 : (r + 1) * 128] = sp[r : r + 1, :]
    mid = sp.shape[0] // 2
    pot_out[...] = jnp.where(scal[0] == 0, sp[:mid], sp[mid:]) * LN2
    held[...] = jnp.zeros_like(held)

    def step(s_ref, p, i):
        pieces = []
        for r in range(B // 8):
            lifted = s_ref[pl.ds(pl.multiple_of(p * B + r * 8, 8), 8), :] + sp_out[...]
            top = jnp.max(lifted, axis=1, keepdims=True)
            pieces.append(top + jnp.log2(jnp.sum(jnp.exp2(lifted - top), axis=1, keepdims=True)))
        row = to_row(jnp.concatenate(pieces, axis=0))
        row = jnp.concatenate([row, row], axis=1)
        slot = scal[2 + i]
        at = slot // 2
        half = lax.broadcasted_iota(jnp.int32, (1, 128), 1) // B
        held[pl.ds(at, 1), :] = jnp.where(half == slot % 2, row, held[pl.ds(at, 1), :])

    @pl.loop(0, len(OFF1))
    def _(p):
        step(s1, p, p)

    @pl.loop(0, len(OFF2))
    def _(p):
        step(s2, p, p + len(OFF1))

    msg_out[...] = jnp.broadcast_to(held[...][None], msg_out.shape)


def cols_call(scal, parts, log_src, s1, s2):
    ns = s1.shape[1]
    return pl.pallas_call(
        cols_kernel,
        name="cols",
        in_specs=[SMEM] + [WHOLE] * 4,
        out_specs=[WHOLE] * 3,
        scratch_shapes=[pltpu.VMEM((8, 128), jnp.float32)],
        out_shape=[
            jax.ShapeDtypeStruct((8, 128), jnp.float32),
            jax.ShapeDtypeStruct((1, ns), jnp.float32),
            jax.ShapeDtypeStruct((16, 8, 128), jnp.float32),
        ],
        compiler_params=params(16),
    )(scal, parts, log_src, s1, s2)


def moved_kernel(scal, parts, lt, sp, s1, s2, tgt, pot_out, mine_out, theirs_out, mass_out, tp, lse, *wide):
    lse[...] = merged_lse(parts[...])
    for p in range(len(OFF)):
        slot = scal[2 + p]
        row = lse[pl.ds(slot // 2, 1), :]
        row = jnp.where(slot % 2 == 0, row[:, :B], row[:, B:])
        tpot = lt[p : p + 1, 0:B] - row
        if p == 0:
            pot_out[...] = tpot * LN2
        tp[p * B : (p + 1) * B, :] = jnp.broadcast_to(to_col(tpot), (B, 128))

    t1 = s1.shape[0]
    half = tgt.shape[0] // 2
    for n in range(sp.shape[1] // CH):
        at = slice(n * CH, (n + 1) * CH)
        w = wide[n % len(wide)]
        spn = sp[:, at]
        mass = jnp.zeros((8, CH), jnp.float32)
        for r in range(0, tp.shape[0], 32):
            s_ref, q = (s1, r) if r < t1 else (s2, r - t1)
            e = jnp.exp2(s_ref[q : q + 32, at] + spn + jnp.concatenate([tp[r : r + 32, :]] * (CH // 128), axis=1))
            mass = mass + jnp.sum(e.reshape(4, 8, CH), axis=0)
            w[r : r + 32, :] = e.astype(jnp.bfloat16)
        mass = jnp.sum(mass, axis=0, keepdims=True)
        mass_out[:, at] = mass
        theirs_out[0:half, at] = jnp.dot(tgt[half:, :], w[...], preferred_element_type=jnp.float32).astype(jnp.bfloat16)
        mine_out[:, at] = jnp.dot(tgt[:half, :], w[...], preferred_element_type=jnp.float32).astype(jnp.bfloat16)
        hi = mass.astype(jnp.bfloat16).astype(jnp.float32)
        pad = jnp.zeros((6, CH), jnp.float32)
        theirs_out[half : half + 8, at] = jnp.concatenate([hi, mass - hi, pad], axis=0).astype(jnp.bfloat16)


def moved_call(scal, parts, lt, sp, s1, s2, tgt):
    ns = s1.shape[1]
    f, t = tgt.shape
    return pl.pallas_call(
        moved_kernel,
        name="moved",
        in_specs=[SMEM] + [WHOLE] * 6,
        out_specs=[WHOLE] * 4,
        scratch_shapes=[pltpu.VMEM((t, 128), jnp.float32), pltpu.VMEM((8, 128), jnp.float32)]
        + [pltpu.VMEM((t, CH), jnp.bfloat16)] * 2,
        out_shape=[
            jax.ShapeDtypeStruct((1, B), jnp.float32),
            jax.ShapeDtypeStruct((f // 2, ns), jnp.bfloat16),
            jax.ShapeDtypeStruct((f // 2 + 8, ns), jnp.bfloat16),
            jax.ShapeDtypeStruct((1, ns), jnp.float32),
        ],
        compiler_params=params(20),
    )(scal, parts, lt, sp, s1, s2, tgt)


def pack_kernel(mine, theirs, mass, out):
    f32 = jnp.float32
    extra = theirs[256:264, :].astype(f32)
    total = mass[...] + extra[0:1] + extra[1:2]
    hi = total.astype(jnp.bfloat16).astype(f32)
    lo = total - hi
    for h in range(2):
        rows = [v[:, (h * 8 + q) * 128 : (h * 8 + q + 1) * 128] for v in (hi, lo) for q in range(8)]
        rows = jnp.concatenate(rows, axis=0).astype(jnp.bfloat16)
        for g in range(8):
            for q in range(8):
                at = (slice(g * 32, (g + 1) * 32), slice((h * 8 + q) * 128, (h * 8 + q + 1) * 128))
                both = mine[at].astype(f32) + theirs[at].astype(f32)
                out[h * 8 + g, q * 32 : (q + 1) * 32, :] = both.astype(jnp.bfloat16)
            out[h * 8 + g, 256:272, :] = rows


def pack_call(mine, theirs, mass):
    return pl.pallas_call(
        pack_kernel,
        name="pack",
        in_specs=[WHOLE] * 3,
        out_specs=WHOLE,
        out_shape=jax.ShapeDtypeStruct((16, 272, 128), jnp.bfloat16),
        compiler_params=params(8),
    )(mine, theirs, mass)


def finish_kernel(parts, out):
    f32 = jnp.float32

    def added(at):
        total = parts[0, at, :].astype(f32)
        for k in range(1, parts.shape[0]):
            total = total + parts[k, at, :].astype(f32)
        return total

    mass = added(slice(256, 272))
    mass = mass[:8] + mass[8:]
    for q in range(8):
        image = added(slice(q * 32, (q + 1) * 32)) / mass[q : q + 1, :]
        out[:, q * 128 : (q + 1) * 128] = image.astype(jnp.bfloat16)


def finish_call(parts):
    return pl.pallas_call(
        finish_kernel,
        name="finish",
        in_specs=[WHOLE],
        out_specs=WHOLE,
        out_shape=jax.ShapeDtypeStruct((32, 1024), jnp.bfloat16),
        compiler_params=params(8),
    )(parts)


def body(sources, log_src, targets, potential, log_tgt):
    bf = jnp.bfloat16
    f = sources.shape[1]
    scale2 = LOG2E / math.sqrt(f)
    z, yh, c = lax.axis_index("z"), lax.axis_index("yh"), lax.axis_index("c")
    scal = jnp.concatenate([jnp.stack([yh, c]), (z + jnp.array(OFF, jnp.int32)) % 16]).astype(jnp.int32)

    extra = jnp.stack(thirds(potential) + thirds(log_tgt) + [jnp.zeros_like(potential)] * 2)
    extra = jnp.pad(extra, ((0, 0), (0, f - B))).astype(bf)
    own = jnp.concatenate([targets, extra], axis=0)
    ls = jnp.pad(jnp.stack(thirds(log_src.reshape(2, 512)), axis=1), ((0, 0), (0, 5), (0, 0))).astype(bf)
    halves = jnp.concatenate([sources.reshape(2, 512, f), ls], axis=1)
    sent = lax.dynamic_index_in_dim(halves, c, 0, keepdims=False)
    ra = from_z(own, 4)
    la = from_z(own, -5)
    near = lax.ppermute(sent, ("yh", "yl"), [(0, 3), (3, 0), (1, 2), (2, 1)])
    rb = from_z(joined([own, ra]), 2)
    lb = from_z(joined([la, own]), -2)
    swapped = lax.ppermute(near, "c", [(0, 1), (1, 0)])
    rc = from_z(joined([own, rb, ra, la]), 1)
    lc = from_z(joined([own, lb, la]), -1)
    first = jnp.where(c == 0, near, swapped)
    second = jnp.where(c == 0, swapped, near)
    other = jnp.concatenate([first[:512], second[:512]], axis=0)
    whole = [first[512:].astype(jnp.float32), second[512:].astype(jnp.float32)]
    other_log = jnp.concatenate([w[0] + w[1] + w[2] for w in whole])
    src = jnp.concatenate([jnp.where(yh == 0, sources, other), jnp.where(yh == 0, other, sources)], axis=0)
    log_all = jnp.concatenate([jnp.where(yh == 0, log_src, other_log), jnp.where(yh == 0, other_log, log_src)])
    log_all = log_all.reshape(16, 128)

    s1, lse1 = scores_call(src, [own, ra, la, rb, lb], PICKS1, scale2)
    s2, rows = scores_call(src, [lb, rc, lc], PICKS2, scale2, lse1)
    row_parts = lax.all_to_all(rows, PLANE, split_axis=0, concat_axis=0, tiled=True)
    tgt, lt = prepare_call(scal, [own, ra, la, rb, lb, rc, lc], rows)
    src_pot, sp, cols = cols_call(scal, row_parts, log_all, s1, s2)
    col_parts = lax.all_to_all(cols, "z", split_axis=0, concat_axis=0, tiled=True)
    tgt_pot, mine, theirs, mass = moved_call(scal, col_parts, lt, sp, s1, s2, tgt)
    theirs = lax.ppermute(theirs, "c", [(0, 1), (1, 0)])
    packed = pack_call(mine, theirs, mass)
    parts = lax.all_to_all(packed, CHIPS, split_axis=0, concat_axis=0, tiled=True)
    mapped = finish_call(parts).T
    return (src_pot.reshape(-1), tgt_pot.reshape(-1), mapped)


def solution(mesh):
    torus = Mesh(mesh.devices.reshape(16, 2, 2, 4, 2), AXES)
    src, every = ("z", "yh"), ("z", "yh", "yl", "x", "c")
    return jax.shard_map(
        body,
        mesh=torus,
        in_specs=(P(src, None), P(src), P(every, None), P(every), P(every)),
        out_specs=(P(src), P(every), P(src, ("yl", "x", "c"))),
        check_vma=False,
    )
```

time: 170 us -> 152 us (0.89)
  Pallas kernels: 43.7 us -> 16.4 us
  blocking collectives: 39.6 us -> 20 us
  local copies, waits for them, and re-layouts: 4.47 us -> 19.3 us
  waiting for transfers between devices: 22.1 us -> 29 us
  starting transfers between devices: 50.8 us -> 57.6 us
    all_to_all x1 -> x0, blocking collectives: 17.9 us -> none  [body(): lax.all_to_all(cols, 'z', split_axis=0, concat_axis=0, tiled=True)]
    pallas_call x4 -> x5, Pallas kernels: 30.3 us -> 12.8 us  [the longest x1 7.37 us: cols_call(): pl.pallas_call(cols_kernel, name='cols', in_specs=[SMEM] + [WHOLE] * 4, o...]
    unnamed x34 -> x61, local copies, waits for them, and re-layouts: 4.33 us -> 19.2 us
    pallas_call x2, Pallas kernels: 13.4 us -> 3.6 us  [scores_call(): pl.pallas_call(lambda *a: scores_kernel(picks, last, len(msgs), scale2, *...]
    all_to_all x0 -> x1, starting transfers between devices: none -> 6.31 us  [body(): lax.all_to_all(cols, 'z', split_axis=0, concat_axis=0, tiled=True)]
    ppermute x6, waiting for transfers between devices: 11.3 us -> 15.7 us  [from_z(): return lax.ppermute(array, 'z', [((i + d) % n, i) for i in range(n)])]
    all_to_all x0 -> x1, waiting for transfers between devices: none -> 3.44 us  [body(): lax.all_to_all(cols, 'z', split_axis=0, concat_axis=0, tiled=True)]
    all_to_all x1, blocking collectives: 21.7 us -> 20 us  [body(): lax.all_to_all(packed, CHIPS, split_axis=0, concat_axis=0, tiled=True)]
  transfers between devices with their start and end apart: 10 -> 11, of which waited for: 5 -> 8; matrix products, arithmetic and copies ran while one was open for 3% -> 4% of each run, Pallas kernels for 3% -> 1%
where the time goes in v2:
time: 152 us; the launch traced here: 151 us
  starting transfers between devices  57.6 us (38%)
  waiting for transfers between devices  29 us (19%)
  blocking collectives  20 us (13%)
  local copies, waits for them, and re-layouts  19.3 us (13%)
  Pallas kernels  16.4 us (11%)
  other arithmetic  7.82 us (5%)
    ppermute x6, starting transfers between devices, from_z(): return lax.ppermute(array, 'z', [((i + d) % n, i) for i in range(n)])  28 us
    all_to_all x1, blocking collectives, body(): lax.all_to_all(packed, CHIPS, split_axis=0, concat_axis=0, tiled=True)  20 us
    unnamed x61, local copies, waits for them, and re-layouts  19.2 us
    ppermute x6, waiting for transfers between devices, from_z(): return lax.ppermute(array, 'z', [((i + d) % n, i) for i in range(n)])  15.7 us
    all_to_all x1, starting transfers between devices, body(): lax.all_to_all(rows, PLANE, split_axis=0, concat_axis=0, tiled=True)  8.77 us
    all_to_all x1, waiting for transfers between devices, body(): lax.all_to_all(rows, PLANE, split_axis=0, concat_axis=0, tiled=True)  7.55 us
    pallas_call x1, Pallas kernels, cols_call(): pl.pallas_call(cols_kernel, name='cols', in_specs=[SMEM] + [WHOLE] * 4, o...  7.37 us
    all_to_all x1, starting transfers between devices, body(): lax.all_to_all(cols, 'z', split_axis=0, concat_axis=0, tiled=True)  6.31 us
  transfers between devices with their start and end apart: 11, of which 8 were waited for; matrix products, arithmetic and copies ran while one was open for 4% of the time, Pallas kernels for 1%

profile of v2, /device:TPU:1, one launch (start us, length us, event | category | flops | bytes accessed | tf_op | source)
XLA Modules:
  0.0 151.1 jit_solution(6720583398106658628)
XLA Ops:
  2.2 13.3 %collective-permute-start.4 = (bf16[72,512]{1,0:T(8,128)(2,1)S(1)}, bf16[72,512]{1,0:T(8,128)(2,1)S(1)}, u32[]{:S(2)}, u32[]{:S(2)}) collective-permute-start(bf16[72,512]{1,0:T(8,128)(2,1)S(1)} %pad_maximum_fusion.4.a_1_.refs_0_), channel_id=1, source_target_pairs={{128,0},{160,32},{192,64},{224,96},{256,128},{288,160},{320,192},{... | collective-permute-start | bytes 221192 | tf_op jit(solution)/shard_map/ppermute | solution.py:28
  19.3 4.6 %collective-permute-start = (bf16[520,512]{1,0:T(8,128)(2,1)S(1)}, bf16[520,512]{1,0:T(8,128)(2,1)S(1)}, u32[]{:S(2)}, u32[]{:S(2)}) collective-permute-start(bf16[520,512]{1,0:T(8,128)(2,1)S(1)} %fusion.1), channel_id=1, source_target_pairs={{0,24},{24,0},{8,16},{16,8},{1,25},{25,1},{9,17},{17,9},{2,26},{26... | collective-permute-start | bytes 1597448 | tf_op jit(solution)/shard_map/ppermute | solution.py:341
  24.6 5.4 %collective-permute-done.2.a_3_.refs_2_ = bf16[72,512]{1,0:T(8,128)(2,1)S(1)} collective-permute-done((bf16[72,512]{1,0:T(8,128)(2,1)S(1)}, bf16[72,512]{1,0:T(8,128)(2,1)S(1)}, u32[]{:S(2)}, u32[]{:S(2)}) %collective-permute-start.2) | collective-permute-done | bytes 73760 | tf_op jit(solution)/shard_map/ppermute | solution.py:28
  30.0 3.4 %collective-permute-start.5 = (bf16[144,512]{1,0:T(8,128)(2,1)S(1)}, bf16[144,512]{1,0:T(8,128)(2,1)S(1)}, u32[]{:S(2)}, u32[]{:S(2)}) collective-permute-start(bf16[144,512]{1,0:T(8,128)(2,1)S(1)} %get-tuple-element.37), channel_id=1, source_target_pairs={{64,0},{96,32},{128,64},{160,96},{192,128},{224,160},{256,192},{28... | collective-permute-start | bytes 442376 | tf_op jit(solution)/shard_map/ppermute | solution.py:28
  34.1 2.8 %collective-permute-start.3 = (bf16[144,512]{1,0:T(8,128)(2,1)S(1)}, bf16[144,512]{1,0:T(8,128)(2,1)S(1)}, u32[]{:S(2)}, u32[]{:S(2)}) collective-permute-start(bf16[144,512]{1,0:T(8,128)(2,1)S(1)} %get-tuple-element.38), channel_id=1, source_target_pairs={{448,0},{480,32},{0,64},{32,96},{64,128},{96,160},{128,192},{160,2... | collective-permute-start | bytes 442376 | tf_op jit(solution)/shard_map/ppermute | solution.py:28
  36.9 2.6 %collective-permute-done.5.a_4_.refs_3_ = bf16[144,512]{1,0:T(8,128)(2,1)S(1)} collective-permute-done((bf16[144,512]{1,0:T(8,128)(2,1)S(1)}, bf16[144,512]{1,0:T(8,128)(2,1)S(1)}, u32[]{:S(2)}, u32[]{:S(2)}) %collective-permute-start.5) | collective-permute-done | bytes 147488 | tf_op jit(solution)/shard_map/ppermute | solution.py:28
  39.6 3.3 %collective-permute-done.3.a_5_.a_1_.refs_4_ = bf16[144,512]{1,0:T(8,128)(2,1)S(1)} collective-permute-done((bf16[144,512]{1,0:T(8,128)(2,1)S(1)}, bf16[144,512]{1,0:T(8,128)(2,1)S(1)}, u32[]{:S(2)}, u32[]{:S(2)}) %collective-permute-start.3) | collective-permute-done | bytes 147488 | tf_op jit(solution)/shard_map/ppermute | solution.py:28
  43.0 5.9 %collective-permute-start.1 = (bf16[520,512]{1,0:T(8,128)(2,1)S(1)}, bf16[520,512]{1,0:T(8,128)(2,1)S(1)}, u32[]{:S(2)}, u32[]{:S(2)}) collective-permute-start(bf16[520,512]{1,0:T(8,128)(2,1)S(1)} %collective-permute-done), channel_id=1, source_target_pairs={{0,1},{1,0},{2,3},{3,2},{4,5},{5,4},{6,7},{7,6},{8,9},{9,8},{10,11... | collective-permute-start | bytes 1597448 | tf_op jit(solution)/shard_map/ppermute | solution.py:344
  48.9 2.4 %collective-permute-start.7 = (bf16[288,512]{1,0:T(8,128)(2,1)S(1)}, bf16[288,512]{1,0:T(8,128)(2,1)S(1)}, u32[]{:S(2)}, u32[]{:S(2)}) collective-permute-start(bf16[288,512]{1,0:T(8,128)(2,1)S(1)} %get-tuple-element.33), channel_id=1, source_target_pairs={{480,0},{0,32},{32,64},{64,96},{96,128},{128,160},{160,192},{192,2... | collective-permute-start | bytes 884744 | tf_op jit(solution)/shard_map/ppermute | solution.py:28
  51.3 4.3 %collective-permute-start.6 = (bf16[360,512]{1,0:T(8,128)(2,1)S(1)}, bf16[360,512]{1,0:T(8,128)(2,1)S(1)}, u32[]{:S(2)}, u32[]{:S(2)}) collective-permute-start(bf16[360,512]{1,0:T(8,128)(2,1)S(1)} %get-tuple-element.34), channel_id=1, source_target_pairs={{32,0},{64,32},{96,64},{128,96},{160,128},{192,160},{224,192},{256... | collective-permute-start | bytes 1105928 | tf_op jit(solution)/shard_map/ppermute | solution.py:28
  60.6 2.6 %collective-permute-done.6.a_2_.refs_5_ = bf16[360,512]{1,0:T(8,128)(2,1)S(1)} collective-permute-done((bf16[360,512]{1,0:T(8,128)(2,1)S(1)}, bf16[360,512]{1,0:T(8,128)(2,1)S(1)}, u32[]{:S(2)}, u32[]{:S(2)}) %collective-permute-start.6) | collective-permute-done | bytes 368672 | tf_op jit(solution)/shard_map/ppermute | solution.py:28
  63.2 2.3 %scores_last.1 = (f32[640,2048]{1,0:T(8,128)S(1)}, f32[32,16,128]{2,1,0:T(8,128)S(1)}) custom-call(bf16[2048,512]{1,0:T(8,128)(2,1)S(1)} %pad_maximum_fusion.a_0_, bf16[144,512]{1,0:T(8,128)(2,1)S(1)} %collective-permute-done.3.a_5_.a_1_.refs_4_, bf16[360,512]{1,0:T(8,128)(2,1)S(1)} %collective-permute-done.6.a_2_.refs_5_, ...), custom_call_target="tpu_custom_call" | custom-call | flops 1342177280 | bytes 5242880 | tf_op jit(solution)/shard_map/scores_last/pallas_call | solution.py:125
  65.5 2.3 %copy-done = f32[640,2048]{1,0:T(8,128)} copy-done((f32[640,2048]{1,0:T(8,128)}, f32[640,2048]{1,0:T(8,128)S(1)}, u32[]{:S(2)}) %copy-start) | copy-done | bytes 5242904
  68.6 8.8 %all-to-all-start = ((f32[32,16,128]{2,1,0:T(8,128)}), f32[32,16,128]{2,1,0:T(8,128)S(1)}, u32[]{:S(2)}, u32[]{:S(2)}) async-start(f32[32,16,128]{2,1,0:T(8,128)} %copy-done.5), calls=%async_computation | async-start | bytes 524288 | tf_op jit(solution)/shard_map/all_to_all | solution.py:358
  78.7 7.5 %all-to-all-done.parts = f32[32,16,128]{2,1,0:T(8,128)S(1)} async-done(((f32[32,16,128]{2,1,0:T(8,128)}), f32[32,16,128]{2,1,0:T(8,128)S(1)}, u32[]{:S(2)}, u32[]{:S(2)}) %all-to-all-start) | async-done | bytes 262176 | tf_op jit(solution)/shard_map/all_to_all | solution.py:358
  86.2 2.5 %copy-done.1 = f32[640,2048]{1,0:T(8,128)S(1)} copy-done((f32[640,2048]{1,0:T(8,128)S(1)}, f32[640,2048]{1,0:T(8,128)}, u32[]{:S(2)}) %copy-start.1) | copy-done | bytes 5242904
  90.1 7.4 %cols.1 = (f32[8,128]{1,0:T(8,128)}, f32[1,2048]{1,0:T(1,128)S(1)}, f32[16,8,128]{2,1,0:T(8,128)S(1)}) custom-call(s32[18]{0:T(128)S(1)} %copy-done.17, f32[32,16,128]{2,1,0:T(8,128)S(1)} %all-to-all-done.parts, f32[16,128]{1,0:T(8,128)S(1)} %copy-done.14, f32[384,2048]{1,0:T(8,128)S(1)} %get-tuple-element.18.s1, f32[640,2048]{1,0:T(8,128)S(1)} %copy-done.1), custom_call_target="tpu_custom_call" | custom-call | tf_op jit(solution)/shard_map/cols/pallas_call | solution.py:204
  98.7 6.3 %all-to-all-start.1 = ((f32[16,8,128]{2,1,0:T(8,128)}), f32[16,8,128]{2,1,0:T(8,128)S(1)}, u32[]{:S(2)}, u32[]{:S(2)}) async-start(f32[16,8,128]{2,1,0:T(8,128)} %copy-done.13), calls=%async_computation.1 | async-start | bytes 131072 | tf_op jit(solution)/shard_map/all_to_all | solution.py:361
  113.2 3.4 %all-to-all-done.1.parts = f32[16,8,128]{2,1,0:T(8,128)S(1)} async-done(((f32[16,8,128]{2,1,0:T(8,128)}), f32[16,8,128]{2,1,0:T(8,128)S(1)}, u32[]{:S(2)}, u32[]{:S(2)}) %all-to-all-start.1) | async-done | bytes 65568 | tf_op jit(solution)/shard_map/all_to_all | solution.py:361
  116.7 2.5 %copy-done.2 = f32[640,2048]{1,0:T(8,128)S(1)} copy-done((f32[640,2048]{1,0:T(8,128)S(1)}, f32[640,2048]{1,0:T(8,128)}, u32[]{:S(2)}) %copy-start.2) | copy-done | bytes 5242904
  120.4 3.4 %moved.1 = (f32[1,64]{1,0:T(1,128)}, bf16[256,2048]{1,0:T(8,128)(2,1)S(1)}, bf16[264,2048]{1,0:T(8,128)(2,1)S(1)}, f32[1,2048]{1,0:T(1,128)S(1)}) custom-call(s32[18]{0:T(128)S(1)} %copy-done.19, f32[16,8,128]{2,1,0:T(8,128)S(1)} %all-to-all-done.1.parts, f32[16,128]{1,0:T(8,128)S(1)} %get-tuple-element.22.lt, f32[1,2048]{1,0:T(1,128)S(1)} %copy-done.16, ...), custom_call_target="tpu_custom_call" | custom-call | tf_op jit(solution)/shard_map/moved/pallas_call | solution.py:254
  123.8 4.0 %collective-permute-start.8 = (bf16[264,2048]{1,0:T(8,128)(2,1)S(1)}, bf16[264,2048]{1,0:T(8,128)(2,1)S(1)}, u32[]{:S(2)}, u32[]{:S(2)}) collective-permute-start(bf16[264,2048]{1,0:T(8,128)(2,1)S(1)} %get-tuple-element.27), channel_id=1, source_target_pairs={{0,1},{1,0},{2,3},{3,2},{4,5},{5,4},{6,7},{7,6},{8,9},{9,8},{10,11... | collective-permute-start | bytes 3244040 | tf_op jit(solution)/shard_map/ppermute | solution.py:363
  127.8 2.3 %collective-permute-done.8.theirs = bf16[264,2048]{1,0:T(8,128)(2,1)S(1)} collective-permute-done((bf16[264,2048]{1,0:T(8,128)(2,1)S(1)}, bf16[264,2048]{1,0:T(8,128)(2,1)S(1)}, u32[]{:S(2)}, u32[]{:S(2)}) %collective-permute-start.8) | collective-permute-done | bytes 1081376 | tf_op jit(solution)/shard_map/ppermute | solution.py:363
  130.4 20.0 %all_to_all.15.parts = bf16[16,272,128]{2,1,0:T(8,128)(2,1)S(1)} all-to-all(bf16[16,272,128]{2,1,0:T(8,128)(2,1)S(1)} %pack.1), channel_id=1, replica_groups=mesh['z'=16,'yh'=2,'yl'=2,'x'=4,'c'=2] {'yh','yl','x'}, dimensions={0} | all-to-all | bytes 2228224 | tf_op jit(solution)/shard_map/all_to_all | solution.py:365
  (93 shorter events, 26.8 us)
Async XLA Ops:
  0.6 29.4 %copy-start.25 = (bf16[64,512]{1,0:T(8,128)(2,1)S(1)}, bf16[64,512]{1,0:T(8,128)(2,1)}, u32[]{:S(2)}) copy-start(bf16[64,512]{1,0:T(8,128)(2,1)} %param.8) | copy-start | bytes 196612
  2.2 54.7 %copy-start.11 = (bf16[72,512]{1,0:T(8,128)(2,1)}, bf16[72,512]{1,0:T(8,128)(2,1)S(1)}, u32[]{:S(2)}) copy-start(bf16[72,512]{1,0:T(8,128)(2,1)S(1)} %pad_maximum_fusion.4.a_1_.refs_0_) | copy-start | bytes 221188
  2.2 22.4 %collective-permute-start.4 = (bf16[72,512]{1,0:T(8,128)(2,1)S(1)}, bf16[72,512]{1,0:T(8,128)(2,1)S(1)}, u32[]{:S(2)}, u32[]{:S(2)}) collective-permute-start(bf16[72,512]{1,0:T(8,128)(2,1)S(1)} %pad_maximum_fusion.4.a_1_.refs_0_), channel_id=1, source_target_pairs={{128,0},{160,32},{192,64},{224,96},{256,128},{288,160},{320,192},{... | collective-permute-start | bytes 221192 | tf_op jit(solution)/shard_map/ppermute | solution.py:28
  15.5 14.5 %collective-permute-start.2 = (bf16[72,512]{1,0:T(8,128)(2,1)S(1)}, bf16[72,512]{1,0:T(8,128)(2,1)S(1)}, u32[]{:S(2)}, u32[]{:S(2)}) collective-permute-start(bf16[72,512]{1,0:T(8,128)(2,1)S(1)} %pad_maximum_fusion.4.a_1_.refs_0_), channel_id=1, source_target_pairs={{352,0},{384,32},{416,64},{448,96},{480,128},{0,160},{32,192},{64,... | collective-permute-start | bytes 221192 | tf_op jit(solution)/shard_map/ppermute | solution.py:28
  19.3 23.7 %collective-permute-start = (bf16[520,512]{1,0:T(8,128)(2,1)S(1)}, bf16[520,512]{1,0:T(8,128)(2,1)S(1)}, u32[]{:S(2)}, u32[]{:S(2)}) collective-permute-start(bf16[520,512]{1,0:T(8,128)(2,1)S(1)} %fusion.1), channel_id=1, source_target_pairs={{0,24},{24,0},{8,16},{16,8},{1,25},{25,1},{9,17},{17,9},{2,26},{26... | collective-permute-start | bytes 1597448 | tf_op jit(solution)/shard_map/ppermute | solution.py:341
  30.0 9.5 %collective-permute-start.5 = (bf16[144,512]{1,0:T(8,128)(2,1)S(1)}, bf16[144,512]{1,0:T(8,128)(2,1)S(1)}, u32[]{:S(2)}, u32[]{:S(2)}) collective-permute-start(bf16[144,512]{1,0:T(8,128)(2,1)S(1)} %get-tuple-element.37), channel_id=1, source_target_pairs={{64,0},{96,32},{128,64},{160,96},{192,128},{224,160},{256,192},{28... | collective-permute-start | bytes 442376 | tf_op jit(solution)/shard_map/ppermute | solution.py:28
  34.1 8.8 %collective-permute-start.3 = (bf16[144,512]{1,0:T(8,128)(2,1)S(1)}, bf16[144,512]{1,0:T(8,128)(2,1)S(1)}, u32[]{:S(2)}, u32[]{:S(2)}) collective-permute-start(bf16[144,512]{1,0:T(8,128)(2,1)S(1)} %get-tuple-element.38), channel_id=1, source_target_pairs={{448,0},{480,32},{0,64},{32,96},{64,128},{96,160},{128,192},{160,2... | collective-permute-start | bytes 442376 | tf_op jit(solution)/shard_map/ppermute | solution.py:28
  39.5 17.4 %copy-start.7 = (bf16[144,512]{1,0:T(8,128)(2,1)}, bf16[144,512]{1,0:T(8,128)(2,1)S(1)}, u32[]{:S(2)}) copy-start(bf16[144,512]{1,0:T(8,128)(2,1)S(1)} %collective-permute-done.5.a_4_.refs_3_) | copy-start | bytes 442372
  42.9 20.3 %copy-start.9 = (bf16[144,512]{1,0:T(8,128)(2,1)}, bf16[144,512]{1,0:T(8,128)(2,1)S(1)}, u32[]{:S(2)}) copy-start(bf16[144,512]{1,0:T(8,128)(2,1)S(1)} %collective-permute-done.3.a_5_.a_1_.refs_4_) | copy-start | bytes 442372
  43.0 12.6 %collective-permute-start.1 = (bf16[520,512]{1,0:T(8,128)(2,1)S(1)}, bf16[520,512]{1,0:T(8,128)(2,1)S(1)}, u32[]{:S(2)}, u32[]{:S(2)}) collective-permute-start(bf16[520,512]{1,0:T(8,128)(2,1)S(1)} %collective-permute-done), channel_id=1, source_target_pairs={{0,1},{1,0},{2,3},{3,2},{4,5},{5,4},{6,7},{7,6},{8,9},{9,8},{10,11... | collective-permute-start | bytes 1597448 | tf_op jit(solution)/shard_map/ppermute | solution.py:344
  48.9 11.7 %collective-permute-start.7 = (bf16[288,512]{1,0:T(8,128)(2,1)S(1)}, bf16[288,512]{1,0:T(8,128)(2,1)S(1)}, u32[]{:S(2)}, u32[]{:S(2)}) collective-permute-start(bf16[288,512]{1,0:T(8,128)(2,1)S(1)} %get-tuple-element.33), channel_id=1, source_target_pairs={{480,0},{0,32},{32,64},{64,96},{96,128},{128,160},{160,192},{192,2... | collective-permute-start | bytes 884744 | tf_op jit(solution)/shard_map/ppermute | solution.py:28
  51.3 4.5 %copy-start.24 = (bf16[1024,512]{1,0:T(8,128)(2,1)S(1)}, bf16[1024,512]{1,0:T(8,128)(2,1)}, u32[]{:S(2)}) copy-start(bf16[1024,512]{1,0:T(8,128)(2,1)} %param.6) | copy-start | bytes 3145732
  51.3 11.9 %collective-permute-start.6 = (bf16[360,512]{1,0:T(8,128)(2,1)S(1)}, bf16[360,512]{1,0:T(8,128)(2,1)S(1)}, u32[]{:S(2)}, u32[]{:S(2)}) collective-permute-start(bf16[360,512]{1,0:T(8,128)(2,1)S(1)} %get-tuple-element.34), channel_id=1, source_target_pairs={{32,0},{64,32},{96,64},{128,96},{160,128},{192,160},{224,192},{256... | collective-permute-start | bytes 1105928 | tf_op jit(solution)/shard_map/ppermute | solution.py:28
  60.6 4.9 %copy-start.22 = (bf16[288,512]{1,0:T(8,128)(2,1)}, bf16[288,512]{1,0:T(8,128)(2,1)S(1)}, u32[]{:S(2)}) copy-start(bf16[288,512]{1,0:T(8,128)(2,1)S(1)} %collective-permute-done.7.a_3_.refs_6_) | copy-start | bytes 884740
  63.2 2.3 %copy-start.20 = (bf16[360,512]{1,0:T(8,128)(2,1)}, bf16[360,512]{1,0:T(8,128)(2,1)S(1)}, u32[]{:S(2)}) copy-start(bf16[360,512]{1,0:T(8,128)(2,1)S(1)} %collective-permute-done.6.a_2_.refs_5_) | copy-start | bytes 1105924
  65.5 2.3 %copy-start = (f32[640,2048]{1,0:T(8,128)}, f32[640,2048]{1,0:T(8,128)S(1)}, u32[]{:S(2)}) copy-start(f32[640,2048]{1,0:T(8,128)S(1)} %get-tuple-element.19.s2) | copy-start | bytes 15728644
  68.6 17.7 %all-to-all-start = ((f32[32,16,128]{2,1,0:T(8,128)}), f32[32,16,128]{2,1,0:T(8,128)S(1)}, u32[]{:S(2)}, u32[]{:S(2)}) async-start(f32[32,16,128]{2,1,0:T(8,128)} %copy-done.5), calls=%async_computation | async-start | bytes 524288 | tf_op jit(solution)/shard_map/all_to_all | solution.py:358
  86.2 2.5 %copy-start.1 = (f32[640,2048]{1,0:T(8,128)S(1)}, f32[640,2048]{1,0:T(8,128)}, u32[]{:S(2)}) copy-start(f32[640,2048]{1,0:T(8,128)} %copy-done) | copy-start | bytes 15728644
  98.7 18.0 %copy-start.19 = (s32[18]{0:T(128)S(1)}, s32[18]{0:T(128)}, u32[]{:S(2)}) copy-start(s32[18]{0:T(128)} %pad_add_fusion.scal) | copy-start | bytes 220
  98.7 18.0 %copy-start.16 = (f32[1,2048]{1,0:T(1,128)S(1)}, f32[1,2048]{1,0:T(1,128)}, u32[]{:S(2)}) copy-start(f32[1,2048]{1,0:T(1,128)} %copy-done.15) | copy-start | bytes 24580
  98.7 18.0 %all-to-all-start.1 = ((f32[16,8,128]{2,1,0:T(8,128)}), f32[16,8,128]{2,1,0:T(8,128)S(1)}, u32[]{:S(2)}, u32[]{:S(2)}) async-start(f32[16,8,128]{2,1,0:T(8,128)} %copy-done.13), calls=%async_computation.1 | async-start | bytes 131072 | tf_op jit(solution)/shard_map/all_to_all | solution.py:361
  116.7 2.5 %copy-start.2 = (f32[640,2048]{1,0:T(8,128)S(1)}, f32[640,2048]{1,0:T(8,128)}, u32[]{:S(2)}) copy-start(f32[640,2048]{1,0:T(8,128)} %copy-done) | copy-start | bytes 15728644
  119.1 1.2 copy-start.4
  123.8 6.3 %collective-permute-start.8 = (bf16[264,2048]{1,0:T(8,128)(2,1)S(1)}, bf16[264,2048]{1,0:T(8,128)(2,1)S(1)}, u32[]{:S(2)}, u32[]{:S(2)}) collective-permute-start(bf16[264,2048]{1,0:T(8,128)(2,1)S(1)} %get-tuple-element.27), channel_id=1, source_target_pairs={{0,1},{1,0},{2,3},{3,2},{4,5},{5,4},{6,7},{7,6},{8,9},{9,8},{10,11... | collective-permute-start | bytes 3244040 | tf_op jit(solution)/shard_map/ppermute | solution.py:363
  (13 other events, 10.6 us)

commit v3 on v2

--- a/solution.py
+++ b/solution.py
@@ -7,6 +7,7 @@
 from jax.experimental.pallas import tpu as pltpu
 from jax.sharding import Mesh
 from jax.sharding import PartitionSpec as P
+
 
 AXES = ("z", "yh", "yl", "x", "c")
 PLANE = ("yh", "yl", "x", "c")
@@ -20,7 +21,7 @@
 OFF = OFF1 + OFF2
 PICKS = ((0, 0), (1, 0), (2, 0), (3, 0), (3, 1), (4, 0), (4, 1)) + tuple((5, k) for k in range(5)) + tuple((6, k) for k in range(4))
 PICKS1 = PICKS[:6]
-PICKS2 = tuple((m - 4, k) for m, k in PICKS[6:])
+PICKS2 = PICKS[6:]
 
 
 def from_z(array, d):
@@ -34,11 +35,46 @@
     return [hi, lo, v - hi - lo]
 
 
-def joined(messages):
-    ks = [m.shape[0] // (B + A8) for m in messages]
-    rows = [m[: k * B] for m, k in zip(messages, ks)]
-    extra = [m[k * B :] for m, k in zip(messages, ks)]
-    return jnp.concatenate(rows + extra, axis=0)
+def own_kernel(targets, potential, log_tgt, out):
+    f32, bf = jnp.float32, jnp.bfloat16
+    rows = []
+    for ref in (potential, log_tgt):
+        v = ref[...]
+        hi = v.astype(bf).astype(f32)
+        lo = (v - hi).astype(bf).astype(f32)
+        rows += [hi, lo, v - hi - lo]
+    extra = jnp.concatenate(rows + [jnp.zeros((2, B), f32)], axis=0).astype(bf)
+    out[0:B, :] = targets[...]
+    out[B : B + A8, :] = jnp.concatenate([extra, jnp.zeros((A8, out.shape[1] - B), bf)], axis=1)
+
+
+def own_call(targets, potential, log_tgt):
+    return pl.pallas_call(
+        own_kernel,
+        name="own",
+        in_specs=[WHOLE] * 3,
+        out_specs=WHOLE,
+        out_shape=jax.ShapeDtypeStruct((B + A8, targets.shape[1]), targets.dtype),
+        compiler_params=params(4),
+    )(targets, potential.reshape(1, B), log_tgt.reshape(1, B))
+
+
+def joined(picks, msgs):
+    def kernel(*refs):
+        out = refs[-1]
+        for p, (m, k) in enumerate(picks):
+            total = refs[m].shape[0] // (B + A8)
+            out[p * B : (p + 1) * B, :] = refs[m][k * B : (k + 1) * B, :]
+            at = len(picks) * B + p * A8
+            out[at : at + A8, :] = refs[m][total * B + k * A8 : total * B + (k + 1) * A8, :]
+
+    return pl.pallas_call(
+        kernel,
+        in_specs=[WHOLE] * len(msgs),
+        out_specs=WHOLE,
+        out_shape=jax.ShapeDtypeStruct((len(picks) * (B + A8), msgs[0].shape[1]), msgs[0].dtype),
+        compiler_params=params(4),
+    )(*msgs)
 
 
 def eye(n):
@@ -77,7 +113,7 @@
     msgs = refs[:n_msg]
     rest = refs[n_msg:]
     if last:
-        lse_in, s_out, lse_out, tg, pot = rest
+        lse_in, scal, s_out, lse_out, tgt_out, lt_out, tg, pot = rest
     else:
         s_out, lse_out, tg, pot = rest
     t = tg.shape[0]
@@ -115,51 +151,44 @@
         else:
             lse_out[:, at] = lse
 
-
-def scores_call(src, msgs, picks, scale2, lse_in=None):
+    if last:
+        core = scal[1]
+        pieces = []
+        for p, (m, k) in enumerate(PICKS):
+            rows, ex = block_of(msgs, m, k)
+            lt_out[p : p + 1, :] = (ex[3:4] + ex[4:5] + ex[5:6]) * LOG2E
+            pieces.append(rows[...])
+        for q in range(len(pieces) // 2):
+            flipped = jnp.concatenate(pieces[2 * q : 2 * q + 2], axis=0).T
+            for f in range(16):
+                to = pl.multiple_of((((f % 2) ^ core) * 8 + f // 2) * 32, 32)
+                tgt_out[pl.ds(to, 32), q * 128 : (q + 1) * 128] = flipped[f * 32 : (f + 1) * 32, :]
+
+
+def scores_call(src, msgs, picks, scale2, lse_in=None, scal=None):
     t = len(picks) * B
     ns, f = src.shape
     last = lse_in is not None
-    lse_shape = (32, ns // 128, 128) if last else (1, ns)
+    shapes = [jax.ShapeDtypeStruct((t, ns), jnp.float32)]
+    if last:
+        shapes += [
+            jax.ShapeDtypeStruct((32, ns // 128, 128), jnp.float32),
+            jax.ShapeDtypeStruct((f, len(OFF) * B), jnp.bfloat16),
+            jax.ShapeDtypeStruct((len(OFF), 128), jnp.float32),
+        ]
+    else:
+        shapes.append(jax.ShapeDtypeStruct((1, ns), jnp.float32))
     args = [src, *msgs] + ([lse_in] if last else [])
     return pl.pallas_call(
         lambda *a: scores_kernel(picks, last, len(msgs), scale2, *a),
         name="scores_last" if last else "scores_first",
-        in_specs=[WHOLE] * len(args),
-        out_specs=[WHOLE] * 2,
+        in_specs=[WHOLE] * len(args) + ([SMEM] if last else []),
+        out_specs=[WHOLE] * len(shapes),
         scratch_shapes=[pltpu.VMEM((t, f), jnp.bfloat16), pltpu.VMEM((t, 128), jnp.float32)],
-        out_shape=[jax.ShapeDtypeStruct((t, ns), jnp.float32), jax.ShapeDtypeStruct(lse_shape, jnp.float32)],
+        out_shape=shapes,
         compiler_params=params(20),
         cost_estimate=pl.CostEstimate(flops=2 * t * ns * f, bytes_accessed=4 * t * ns, transcendentals=t * ns),
-    )(*args)
-
-
-def prepare_kernel(scal, *refs):
-    msgs, (_, tgt_out, lt_out, tg) = refs[:-4], refs[-4:]
-    core = scal[1]
-    for p, (m, k) in enumerate(PICKS):
-        rows, ex = block_of(msgs, m, k)
-        tg[p * B : (p + 1) * B, :] = rows[...]
-        lt_out[p : p + 1, :] = (ex[3:4] + ex[4:5] + ex[5:6]) * LOG2E
-    for q in range(tg.shape[0] // 128):
-        flipped = tg[q * 128 : (q + 1) * 128, :].T
-        for t in range(16):
-            at = pl.multiple_of((((t % 2) ^ core) * 8 + t // 2) * 32, 32)
-            tgt_out[pl.ds(at, 32), q * 128 : (q + 1) * 128] = flipped[t * 32 : (t + 1) * 32, :]
-
-
-def prepare_call(scal, msgs, after):
-    t, f = len(OFF) * B, msgs[0].shape[1]
-    return pl.pallas_call(
-        prepare_kernel,
-        name="prepare",
-        in_specs=[SMEM] + [WHOLE] * len(msgs) + [pl.BlockSpec(memory_space=pl.ANY)],
-        out_specs=[WHOLE] * 2,
-        scratch_shapes=[pltpu.VMEM((t, f), jnp.bfloat16)],
-        out_shape=[jax.ShapeDtypeStruct((f, t), jnp.bfloat16), jax.ShapeDtypeStruct((len(OFF), 128), jnp.float32)],
-        compiler_params=params(16),
-        cost_estimate=pl.CostEstimate(flops=2 * t * f * 1024, bytes_accessed=4 * t * f, transcendentals=0),
-    )(scal, *msgs, after)
+    )(*args, *([scal] if last else []))
 
 
 def merged_lse(parts):
@@ -178,7 +207,7 @@
     def step(s_ref, p, i):
         pieces = []
         for r in range(B // 8):
-            lifted = s_ref[pl.ds(pl.multiple_of(p * B + r * 8, 8), 8), :] + sp_out[...]
+            lifted = s_ref[p * B + r * 8 : p * B + r * 8 + 8, :] + sp_out[...]
             top = jnp.max(lifted, axis=1, keepdims=True)
             pieces.append(top + jnp.log2(jnp.sum(jnp.exp2(lifted - top), axis=1, keepdims=True)))
         row = to_row(jnp.concatenate(pieces, axis=0))
@@ -188,12 +217,9 @@
         half = lax.broadcasted_iota(jnp.int32, (1, 128), 1) // B
         held[pl.ds(at, 1), :] = jnp.where(half == slot % 2, row, held[pl.ds(at, 1), :])
 
-    @pl.loop(0, len(OFF1))
-    def _(p):
+    for p in range(len(OFF1)):
         step(s1, p, p)
-
-    @pl.loop(0, len(OFF2))
-    def _(p):
+    for p in range(len(OFF2)):
         step(s2, p, p + len(OFF1))
 
     msg_out[...] = jnp.broadcast_to(held[...][None], msg_out.shape)
@@ -330,20 +356,19 @@
     z, yh, c = lax.axis_index("z"), lax.axis_index("yh"), lax.axis_index("c")
     scal = jnp.concatenate([jnp.stack([yh, c]), (z + jnp.array(OFF, jnp.int32)) % 16]).astype(jnp.int32)
 
-    extra = jnp.stack(thirds(potential) + thirds(log_tgt) + [jnp.zeros_like(potential)] * 2)
-    extra = jnp.pad(extra, ((0, 0), (0, f - B))).astype(bf)
-    own = jnp.concatenate([targets, extra], axis=0)
+    own = own_call(targets, potential, log_tgt)
     ls = jnp.pad(jnp.stack(thirds(log_src.reshape(2, 512)), axis=1), ((0, 0), (0, 5), (0, 0))).astype(bf)
     halves = jnp.concatenate([sources.reshape(2, 512, f), ls], axis=1)
-    sent = lax.dynamic_index_in_dim(halves, c, 0, keepdims=False)
+    mine = lax.dynamic_index_in_dim(halves, c, 0, keepdims=False)
     ra = from_z(own, 4)
     la = from_z(own, -5)
-    near = lax.ppermute(sent, ("yh", "yl"), [(0, 3), (3, 0), (1, 2), (2, 1)])
-    rb = from_z(joined([own, ra]), 2)
-    lb = from_z(joined([la, own]), -2)
+    near = lax.ppermute(mine, ("yh", "yl"), [(0, 3), (3, 0), (1, 2), (2, 1)])
+    rb = from_z(joined([(0, 0), (1, 0)], [own, ra]), 2)
+    lb = from_z(joined([(1, 0), (0, 0)], [own, la]), -2)
     swapped = lax.ppermute(near, "c", [(0, 1), (1, 0)])
-    rc = from_z(joined([own, rb, ra, la]), 1)
-    lc = from_z(joined([own, lb, la]), -1)
+    own_c, swapped = lax.optimization_barrier((own, swapped))
+    rc = from_z(joined([(0, 0), (1, 0), (1, 1), (2, 0), (3, 0)], [own_c, rb, ra, la]), 1)
+    lc = from_z(joined([(0, 0), (1, 0), (1, 1), (2, 0)], [own_c, lb, la]), -1)
     first = jnp.where(c == 0, near, swapped)
     second = jnp.where(c == 0, swapped, near)
     other = jnp.concatenate([first[:512], second[:512]], axis=0)
@@ -353,10 +378,11 @@
     log_all = jnp.concatenate([jnp.where(yh == 0, log_src, other_log), jnp.where(yh == 0, other_log, log_src)])
     log_all = log_all.reshape(16, 128)
 
-    s1, lse1 = scores_call(src, [own, ra, la, rb, lb], PICKS1, scale2)
-    s2, rows = scores_call(src, [lb, rc, lc], PICKS2, scale2, lse1)
+    msgs = [own, ra, la, rb, lb, rc, lc]
+    s1, lse1 = scores_call(src, msgs[:5], PICKS1, scale2)
+    s2, rows, tgt, lt = scores_call(src, msgs, PICKS2, scale2, lse1, scal)
+    rows, log_all = lax.optimization_barrier((rows, log_all))
     row_parts = lax.all_to_all(rows, PLANE, split_axis=0, concat_axis=0, tiled=True)
-    tgt, lt = prepare_call(scal, [own, ra, la, rb, lb, rc, lc], rows)
     src_pot, sp, cols = cols_call(scal, row_parts, log_all, s1, s2)
     col_parts = lax.all_to_all(cols, "z", split_axis=0, concat_axis=0, tiled=True)
     tgt_pot, mine, theirs, mass = moved_call(scal, col_parts, lt, sp, s1, s2, tgt)

time: 152 us -> 150 us (0.987)
  blocking collectives: 20 us -> 57.7 us
  local copies, waits for them, and re-layouts: 19.3 us -> 2.23 us
  waiting for transfers between devices: 29 us -> 19.6 us
  starting transfers between devices: 57.6 us -> 52.1 us
  other arithmetic: 7.82 us -> 3.19 us
  Pallas kernels: 16.4 us -> 13.7 us
    all_to_all x0 -> x2, blocking collectives: none -> 37.7 us  [the longest x1 20.5 us: body(): lax.all_to_all(cols, 'z', split_axis=0, concat_axis=0, tiled=True)]
    unnamed x61 -> x10, local copies, waits for them, and re-layouts: 19.2 us -> 2.16 us
    all_to_all x2 -> x0, starting transfers between devices: 15.1 us -> none  [the longest x1 8.77 us: body(): lax.all_to_all(rows, PLANE, split_axis=0, concat_axis=0, tiled=True)]
    all_to_all x2 -> x0, waiting for transfers between devices: 11 us -> none  [the longest x1 7.55 us: body(): lax.all_to_all(rows, PLANE, split_axis=0, concat_axis=0, tiled=True)]
    ppermute x1, waiting for transfers between devices: 0.01 us -> 8.41 us  [body(): near = lax.ppermute(mine, ('yh', 'yl'), [(0, 3), (3, 0), (1, 2), (2, 1)])]
    ppermute x6, starting transfers between devices: 28 us -> 35.5 us  [from_z(): return lax.ppermute(array, 'z', [((i + d) % n, i) for i in range(n)])]
    ppermute x6, waiting for transfers between devices: 15.7 us -> 8.85 us  [from_z(): return lax.ppermute(array, 'z', [((i + d) % n, i) for i in range(n)])]
    pallas_call x1, Pallas kernels: 7.37 us -> 4.49 us  [cols_call(): pl.pallas_call(cols_kernel, name='cols', in_specs=[SMEM] + [WHOLE] * 4, o...]
  transfers between devices with their start and end apart: 11 -> 9, of which waited for: 8 -> 7; matrix products, arithmetic and copies ran while one was open for 4% -> 1% of each run, Pallas kernels for 1% -> 1%
where the time goes in v3:
time: 150 us; the launch traced here: 149 us
  blocking collectives  57.7 us (38%)
  starting transfers between devices  52.1 us (35%)
  waiting for transfers between devices  19.6 us (13%)
  Pallas kernels  13.7 us (9%)
  other arithmetic  3.19 us (2%)
  local copies, waits for them, and re-layouts  2.23 us (1%)
    ppermute x6, starting transfers between devices, from_z(): return lax.ppermute(array, 'z', [((i + d) % n, i) for i in range(n)])  35.5 us
    all_to_all x1, blocking collectives, body(): lax.all_to_all(cols, 'z', split_axis=0, concat_axis=0, tiled=True)  20.5 us
    all_to_all x1, blocking collectives, body(): lax.all_to_all(packed, CHIPS, split_axis=0, concat_axis=0, tiled=True)  20 us
    all_to_all x1, blocking collectives, body(): lax.all_to_all(rows, PLANE, split_axis=0, concat_axis=0, tiled=True)  17.2 us
    ppermute x6, waiting for transfers between devices, from_z(): return lax.ppermute(array, 'z', [((i + d) % n, i) for i in range(n)])  8.85 us
    ppermute x1, waiting for transfers between devices, body(): near = lax.ppermute(mine, ('yh', 'yl'), [(0, 3), (3, 0), (1, 2), (2, 1)])  8.41 us
    ppermute x1, starting transfers between devices, body(): swapped = lax.ppermute(near, 'c', [(0, 1), (1, 0)])  7.23 us
    ppermute x1, starting transfers between devices, body(): near = lax.ppermute(mine, ('yh', 'yl'), [(0, 3), (3, 0), (1, 2), (2, 1)])  5.46 us
  transfers between devices with their start and end apart: 9, of which 7 were waited for; matrix products, arithmetic and copies ran while one was open for 1% of the time, Pallas kernels for 1%

profile of v3, /device:TPU:1, one launch (start us, length us, event | category | flops | bytes accessed | tf_op | source)
XLA Modules:
  0.0 149.4 jit_solution(8595957830555552702)
XLA Ops:
  1.4 1.1 fusion.1
  2.5 5.5 %collective-permute-start = (bf16[520,512]{1,0:T(8,128)(2,1)S(1)}, bf16[520,512]{1,0:T(8,128)(2,1)S(1)}, u32[]{:S(2)}, u32[]{:S(2)}) collective-permute-start(bf16[520,512]{1,0:T(8,128)(2,1)S(1)} %fusion.1), channel_id=1, source_target_pairs={{0,24},{24,0},{8,16},{16,8},{1,25},{25,1},{9,17},{17,9},{2,26},{26... | collective-permute-start | bytes 1597448 | tf_op jit(solution)/shard_map/ppermute | solution.py:365
  7.9 8.4 %collective-permute-done = bf16[520,512]{1,0:T(8,128)(2,1)S(1)} collective-permute-done((bf16[520,512]{1,0:T(8,128)(2,1)S(1)}, bf16[520,512]{1,0:T(8,128)(2,1)S(1)}, u32[]{:S(2)}, u32[]{:S(2)}) %collective-permute-start) | collective-permute-done | bytes 532512 | tf_op jit(solution)/shard_map/ppermute | solution.py:365
  16.3 7.2 %collective-permute-start.1 = (bf16[520,512]{1,0:T(8,128)(2,1)S(1)}, bf16[520,512]{1,0:T(8,128)(2,1)S(1)}, u32[]{:S(2)}, u32[]{:S(2)}) collective-permute-start(bf16[520,512]{1,0:T(8,128)(2,1)S(1)} %collective-permute-done), channel_id=1, source_target_pairs={{0,1},{1,0},{2,3},{3,2},{4,5},{5,4},{6,7},{7,6},{8,9},{9,8},{10,11... | collective-permute-start | bytes 1597448 | tf_op jit(solution)/shard_map/ppermute | solution.py:368
  23.6 0.8 copy-done
  25.7 9.5 %collective-permute-start.3 = (bf16[72,512]{1,0:T(8,128)(2,1)S(1)}, bf16[72,512]{1,0:T(8,128)(2,1)S(1)}, u32[]{:S(2)}, u32[]{:S(2)}) collective-permute-start(bf16[72,512]{1,0:T(8,128)(2,1)S(1)} %own.1.refs_0_.a_1_), channel_id=1, source_target_pairs={{352,0},{384,32},{416,64},{448,96},{480,128},{0,160},{32,192},{64,... | collective-permute-start | bytes 221192 | tf_op jit(solution)/shard_map/ppermute | solution.py:29
  35.2 4.2 %collective-permute-start.2 = (bf16[72,512]{1,0:T(8,128)(2,1)S(1)}, bf16[72,512]{1,0:T(8,128)(2,1)S(1)}, u32[]{:S(2)}, u32[]{:S(2)}) collective-permute-start(bf16[72,512]{1,0:T(8,128)(2,1)S(1)} %own.1.refs_0_.a_1_), channel_id=1, source_target_pairs={{128,0},{160,32},{192,64},{224,96},{256,128},{288,160},{320,192},{... | collective-permute-start | bytes 221192 | tf_op jit(solution)/shard_map/ppermute | solution.py:29
  40.2 1.6 %collective-permute-done.3.refs_1_.refs_3_.refs_2_.a_3_ = bf16[72,512]{1,0:T(8,128)(2,1)S(1)} collective-permute-done((bf16[72,512]{1,0:T(8,128)(2,1)S(1)}, bf16[72,512]{1,0:T(8,128)(2,1)S(1)}, u32[]{:S(2)}, u32[]{:S(2)}) %collective-permute-start.3) | collective-permute-done | bytes 73760 | tf_op jit(solution)/shard_map/ppermute | solution.py:29
  41.8 5.2 %collective-permute-start.5 = (bf16[144,512]{1,0:T(8,128)(2,1)S(1)}, bf16[144,512]{1,0:T(8,128)(2,1)S(1)}, u32[]{:S(2)}, u32[]{:S(2)}) collective-permute-start(bf16[144,512]{1,0:T(8,128)(2,1)S(1)} %shard_map.86), channel_id=1, source_target_pairs={{448,0},{480,32},{0,64},{32,96},{64,128},{96,160},{128,192},{160,2... | collective-permute-start | bytes 442376 | tf_op jit(solution)/shard_map/ppermute | solution.py:29
  47.0 1.7 %collective-permute-done.2.refs_1_.refs_2_.a_2_ = bf16[72,512]{1,0:T(8,128)(2,1)S(1)} collective-permute-done((bf16[72,512]{1,0:T(8,128)(2,1)S(1)}, bf16[72,512]{1,0:T(8,128)(2,1)S(1)}, u32[]{:S(2)}, u32[]{:S(2)}) %collective-permute-start.2) | collective-permute-done | bytes 73760 | tf_op jit(solution)/shard_map/ppermute | solution.py:29
  48.7 3.6 %collective-permute-start.4 = (bf16[144,512]{1,0:T(8,128)(2,1)S(1)}, bf16[144,512]{1,0:T(8,128)(2,1)S(1)}, u32[]{:S(2)}, u32[]{:S(2)}) collective-permute-start(bf16[144,512]{1,0:T(8,128)(2,1)S(1)} %shard_map.85), channel_id=1, source_target_pairs={{64,0},{96,32},{128,64},{160,96},{192,128},{224,160},{256,192},{28... | collective-permute-start | bytes 442376 | tf_op jit(solution)/shard_map/ppermute | solution.py:29
  52.9 8.1 %collective-permute-start.7 = (bf16[288,512]{1,0:T(8,128)(2,1)S(1)}, bf16[288,512]{1,0:T(8,128)(2,1)S(1)}, u32[]{:S(2)}, u32[]{:S(2)}) collective-permute-start(bf16[288,512]{1,0:T(8,128)(2,1)S(1)} %shard_map.88), channel_id=1, source_target_pairs={{480,0},{0,32},{32,64},{64,96},{96,128},{128,160},{160,192},{192,2... | collective-permute-start | bytes 884744 | tf_op jit(solution)/shard_map/ppermute | solution.py:29
  61.1 4.9 %collective-permute-start.6 = (bf16[360,512]{1,0:T(8,128)(2,1)S(1)}, bf16[360,512]{1,0:T(8,128)(2,1)S(1)}, u32[]{:S(2)}, u32[]{:S(2)}) collective-permute-start(bf16[360,512]{1,0:T(8,128)(2,1)S(1)} %shard_map.87), channel_id=1, source_target_pairs={{32,0},{64,32},{96,64},{128,96},{160,128},{192,160},{224,192},{256... | collective-permute-start | bytes 1105928 | tf_op jit(solution)/shard_map/ppermute | solution.py:29
  66.5 1.3 scores_first.1
  67.8 2.7 %collective-permute-done.7.a_7_ = bf16[288,512]{1,0:T(8,128)(2,1)S(1)} collective-permute-done((bf16[288,512]{1,0:T(8,128)(2,1)S(1)}, bf16[288,512]{1,0:T(8,128)(2,1)S(1)}, u32[]{:S(2)}, u32[]{:S(2)}) %collective-permute-start.7) | collective-permute-done | bytes 294944 | tf_op jit(solution)/shard_map/ppermute | solution.py:29
  70.5 2.5 %collective-permute-done.6.a_6_ = bf16[360,512]{1,0:T(8,128)(2,1)S(1)} collective-permute-done((bf16[360,512]{1,0:T(8,128)(2,1)S(1)}, bf16[360,512]{1,0:T(8,128)(2,1)S(1)}, u32[]{:S(2)}, u32[]{:S(2)}) %collective-permute-start.6) | collective-permute-done | bytes 368672 | tf_op jit(solution)/shard_map/ppermute | solution.py:29
  73.1 3.1 %scores_last.1 = (f32[640,2048]{1,0:T(8,128)S(1)}, f32[32,16,128]{2,1,0:T(8,128)S(1)}, bf16[512,1024]{1,0:T(8,128)(2,1)S(1)}, f32[16,128]{1,0:T(8,128)S(1)}) custom-call(bf16[2048,512]{1,0:T(8,128)(2,1)S(1)} %pad_maximum_fusion.a_0_, bf16[72,512]{1,0:T(8,128)(2,1)S(1)} %own.1.refs_0_.a_1_, bf16[72,512]{1,0:T(8,128)(2,1)S(1)} %collective-permute-done.2.refs_1_.refs_2_.a_2_, ...), custom_call_target="tpu_custom_call" | custom-call | flops 1342177280 | bytes 5242880 | tf_op jit(solution)/shard_map/scores_last/pallas_call | solution.py:182
  76.1 17.2 %all_to_all.15.parts = f32[32,16,128]{2,1,0:T(8,128)S(1)} all-to-all(f32[32,16,128]{2,1,0:T(8,128)S(1)} %get-tuple-element.24), channel_id=1, replica_groups=mesh['z'=16,'yh'=2,'yl'=2,'x'=4,'c'=2] {'yh','yl','x','c'}, dimensions={0} | all-to-all | bytes 524288 | tf_op jit(solution)/shard_map/all_to_all | solution.py:385
  93.4 4.5 %cols.1 = (f32[8,128]{1,0:T(8,128)}, f32[1,2048]{1,0:T(1,128)S(1)}, f32[16,8,128]{2,1,0:T(8,128)S(1)}) custom-call(s32[18]{0:T(128)S(1)} %pad_add_fusion.a_9_.scal, f32[32,16,128]{2,1,0:T(8,128)S(1)} %all_to_all.15.parts, f32[16,128]{1,0:T(8,128)S(1)} %pad_maximum_fusion.2.log_src, f32[384,2048]{1,0:T(8,128)S(1)} %get-tuple-element.26.s1, ...), custom_call_target="tpu_custom_call" | custom-call | tf_op jit(solution)/shard_map/cols/pallas_call | solution.py:230
  97.9 20.5 %all_to_all.16.parts = f32[16,8,128]{2,1,0:T(8,128)S(1)} all-to-all(f32[16,8,128]{2,1,0:T(8,128)S(1)} %get-tuple-element.29), channel_id=1, replica_groups=mesh['z'=16,'yh'=2,'yl'=2,'x'=4,'c'=2] {'z'}, dimensions={0} | all-to-all | bytes 131072 | tf_op jit(solution)/shard_map/all_to_all | solution.py:387
  118.3 3.7 %moved.1 = (f32[1,64]{1,0:T(1,128)}, bf16[256,2048]{1,0:T(8,128)(2,1)S(1)}, bf16[264,2048]{1,0:T(8,128)(2,1)S(1)}, f32[1,2048]{1,0:T(1,128)S(1)}) custom-call(s32[18]{0:T(128)S(1)} %pad_add_fusion.a_9_.scal, f32[16,8,128]{2,1,0:T(8,128)S(1)} %all_to_all.16.parts, f32[16,128]{1,0:T(8,128)S(1)} %get-tuple-element.30.lt, f32[1,2048]{1,0:T(1,128)S(1)} %get-tuple-element.31.sp, ...), custom_call_target="tpu_custom_call" | custom-call | tf_op jit(solution)/shard_map/moved/pallas_call | solution.py:280
  122.1 4.0 %collective-permute-start.8 = (bf16[264,2048]{1,0:T(8,128)(2,1)S(1)}, bf16[264,2048]{1,0:T(8,128)(2,1)S(1)}, u32[]{:S(2)}, u32[]{:S(2)}) collective-permute-start(bf16[264,2048]{1,0:T(8,128)(2,1)S(1)} %get-tuple-element.35), channel_id=1, source_target_pairs={{0,1},{1,0},{2,3},{3,2},{4,5},{5,4},{6,7},{7,6},{8,9},{9,8},{10,11... | collective-permute-start | bytes 3244040 | tf_op jit(solution)/shard_map/ppermute | solution.py:389
  126.1 2.3 %collective-permute-done.8.theirs = bf16[264,2048]{1,0:T(8,128)(2,1)S(1)} collective-permute-done((bf16[264,2048]{1,0:T(8,128)(2,1)S(1)}, bf16[264,2048]{1,0:T(8,128)(2,1)S(1)}, u32[]{:S(2)}, u32[]{:S(2)}) %collective-permute-start.8) | collective-permute-done | bytes 1081376 | tf_op jit(solution)/shard_map/ppermute | solution.py:389
  128.7 20.0 %all_to_all.17.parts = bf16[16,272,128]{2,1,0:T(8,128)(2,1)S(1)} all-to-all(bf16[16,272,128]{2,1,0:T(8,128)(2,1)S(1)} %pack.1), channel_id=1, replica_groups=mesh['z'=16,'yh'=2,'yl'=2,'x'=4,'c'=2] {'yh','yl','x'}, dimensions={0} | all-to-all | bytes 2228224 | tf_op jit(solution)/shard_map/all_to_all | solution.py:391
  (33 shorter events, 5.0 us)
Async XLA Ops:
  2.5 13.9 %collective-permute-start = (bf16[520,512]{1,0:T(8,128)(2,1)S(1)}, bf16[520,512]{1,0:T(8,128)(2,1)S(1)}, u32[]{:S(2)}, u32[]{:S(2)}) collective-permute-start(bf16[520,512]{1,0:T(8,128)(2,1)S(1)} %fusion.1), channel_id=1, source_target_pairs={{0,24},{24,0},{8,16},{16,8},{1,25},{25,1},{9,17},{17,9},{2,26},{26... | collective-permute-start | bytes 1597448 | tf_op jit(solution)/shard_map/ppermute | solution.py:365
  16.3 36.0 %collective-permute-start.1 = (bf16[520,512]{1,0:T(8,128)(2,1)S(1)}, bf16[520,512]{1,0:T(8,128)(2,1)S(1)}, u32[]{:S(2)}, u32[]{:S(2)}) collective-permute-start(bf16[520,512]{1,0:T(8,128)(2,1)S(1)} %collective-permute-done), channel_id=1, source_target_pairs={{0,1},{1,0},{2,3},{3,2},{4,5},{5,4},{6,7},{7,6},{8,9},{9,8},{10,11... | collective-permute-start | bytes 1597448 | tf_op jit(solution)/shard_map/ppermute | solution.py:368
  23.6 0.8 copy-start
  24.4 0.7 copy-start.1
  25.1 0.7 copy-start.2
  25.7 16.0 %collective-permute-start.3 = (bf16[72,512]{1,0:T(8,128)(2,1)S(1)}, bf16[72,512]{1,0:T(8,128)(2,1)S(1)}, u32[]{:S(2)}, u32[]{:S(2)}) collective-permute-start(bf16[72,512]{1,0:T(8,128)(2,1)S(1)} %own.1.refs_0_.a_1_), channel_id=1, source_target_pairs={{352,0},{384,32},{416,64},{448,96},{480,128},{0,160},{32,192},{64,... | collective-permute-start | bytes 221192 | tf_op jit(solution)/shard_map/ppermute | solution.py:29
  35.2 13.5 %collective-permute-start.2 = (bf16[72,512]{1,0:T(8,128)(2,1)S(1)}, bf16[72,512]{1,0:T(8,128)(2,1)S(1)}, u32[]{:S(2)}, u32[]{:S(2)}) collective-permute-start(bf16[72,512]{1,0:T(8,128)(2,1)S(1)} %own.1.refs_0_.a_1_), channel_id=1, source_target_pairs={{128,0},{160,32},{192,64},{224,96},{256,128},{288,160},{320,192},{... | collective-permute-start | bytes 221192 | tf_op jit(solution)/shard_map/ppermute | solution.py:29
  41.8 11.1 %collective-permute-start.5 = (bf16[144,512]{1,0:T(8,128)(2,1)S(1)}, bf16[144,512]{1,0:T(8,128)(2,1)S(1)}, u32[]{:S(2)}, u32[]{:S(2)}) collective-permute-start(bf16[144,512]{1,0:T(8,128)(2,1)S(1)} %shard_map.86), channel_id=1, source_target_pairs={{448,0},{480,32},{0,64},{32,96},{64,128},{96,160},{128,192},{160,2... | collective-permute-start | bytes 442376 | tf_op jit(solution)/shard_map/ppermute | solution.py:29
  48.7 12.3 %collective-permute-start.4 = (bf16[144,512]{1,0:T(8,128)(2,1)S(1)}, bf16[144,512]{1,0:T(8,128)(2,1)S(1)}, u32[]{:S(2)}, u32[]{:S(2)}) collective-permute-start(bf16[144,512]{1,0:T(8,128)(2,1)S(1)} %shard_map.85), channel_id=1, source_target_pairs={{64,0},{96,32},{128,64},{160,96},{192,128},{224,160},{256,192},{28... | collective-permute-start | bytes 442376 | tf_op jit(solution)/shard_map/ppermute | solution.py:29
  52.4 13.5 %copy-start.3 = (bf16[1024,512]{1,0:T(8,128)(2,1)S(1)}, bf16[1024,512]{1,0:T(8,128)(2,1)}, u32[]{:S(2)}) copy-start(bf16[1024,512]{1,0:T(8,128)(2,1)} %param.6) | copy-start | bytes 3145732
  52.9 17.6 %collective-permute-start.7 = (bf16[288,512]{1,0:T(8,128)(2,1)S(1)}, bf16[288,512]{1,0:T(8,128)(2,1)S(1)}, u32[]{:S(2)}, u32[]{:S(2)}) collective-permute-start(bf16[288,512]{1,0:T(8,128)(2,1)S(1)} %shard_map.88), channel_id=1, source_target_pairs={{480,0},{0,32},{32,64},{64,96},{96,128},{128,160},{160,192},{192,2... | collective-permute-start | bytes 884744 | tf_op jit(solution)/shard_map/ppermute | solution.py:29
  61.1 12.0 %collective-permute-start.6 = (bf16[360,512]{1,0:T(8,128)(2,1)S(1)}, bf16[360,512]{1,0:T(8,128)(2,1)S(1)}, u32[]{:S(2)}, u32[]{:S(2)}) collective-permute-start(bf16[360,512]{1,0:T(8,128)(2,1)S(1)} %shard_map.87), channel_id=1, source_target_pairs={{32,0},{64,32},{96,64},{128,96},{160,128},{192,160},{224,192},{256... | collective-permute-start | bytes 1105928 | tf_op jit(solution)/shard_map/ppermute | solution.py:29
  66.5 1.3 copy-start.4
  122.1 6.3 %collective-permute-start.8 = (bf16[264,2048]{1,0:T(8,128)(2,1)S(1)}, bf16[264,2048]{1,0:T(8,128)(2,1)S(1)}, u32[]{:S(2)}, u32[]{:S(2)}) collective-permute-start(bf16[264,2048]{1,0:T(8,128)(2,1)S(1)} %get-tuple-element.35), channel_id=1, source_target_pairs={{0,1},{1,0},{2,3},{3,2},{4,5},{5,4},{6,7},{7,6},{8,9},{9,8},{10,11... | collective-permute-start | bytes 3244040 | tf_op jit(solution)/shard_map/ppermute | solution.py:389

commit v4 on v3

v4 whole, which is shorter than its diff:
```python
import math

import jax
import jax.numpy as jnp
from jax import lax
from jax.experimental import pallas as pl
from jax.experimental.pallas import tpu as pltpu
from jax.sharding import Mesh
from jax.sharding import PartitionSpec as P


WHOLE = pl.BlockSpec(memory_space=pltpu.VMEM)
FAR = pl.BlockSpec(memory_space=pltpu.HBM)
AXES = ("z", "yh", "yl", "x", "c")
PLANE = ("yh", "yl", "x", "c")
CHIPS = ("yh", "yl", "x")
LOG2E = math.log2(math.e)
LN2 = math.log(2.0)
B = 64
A8 = 8
OFF1 = (0, 4, 11, 2, 6, 9)
OFF2 = (14, 1, 3, 7, 5, 12, 15, 8, 13, 10)
OFF = OFF1 + OFF2
PICKS = ((0, 0), (1, 0), (2, 0), (3, 0), (3, 1), (4, 0), (4, 1)) + tuple((5, k) for k in range(5)) + tuple((6, k) for k in range(4))
PICKS1 = PICKS[:6]
PICKS2 = PICKS[6:]


MIB = 1 << 20


def params(mib):
    return pltpu.CompilerParams(vmem_limit_bytes=mib * MIB)


def from_z(array, d):
    n = lax.axis_size("z")
    return lax.ppermute(array, "z", [((i + d) % n, i) for i in range(n)])


def split(v):
    hi = v.astype(jnp.bfloat16).astype(jnp.float32)
    lo = (v - hi).astype(jnp.bfloat16).astype(jnp.float32)
    return [hi, lo, v - hi - lo]


def far(array):
    return pltpu.with_memory_space_constraint(array, pltpu.HBM)


def own_kernel(targets, potential, log_tgt, out, pot, log, sems):
    f32, bf = jnp.float32, jnp.bfloat16
    copies = [
        pltpu.make_async_copy(targets, out.at[0:B], sems.at[0]),
        pltpu.make_async_copy(potential, pot, sems.at[1]),
        pltpu.make_async_copy(log_tgt, log, sems.at[2]),
    ]
    for copy in copies:
        copy.start()
    for copy in copies:
        copy.wait()
    rows = []
    for ref in (pot, log):
        rows += split(ref[...])
    extra = jnp.concatenate(rows + [jnp.zeros((2, B), f32)], axis=0).astype(bf)
    out[B : B + A8, :] = jnp.concatenate([extra, jnp.zeros((A8, out.shape[1] - B), bf)], axis=1)


def own_call(targets, potential, log_tgt):
    return pl.pallas_call(
        own_kernel,
        name="own",
        in_specs=[FAR] * 3,
        out_specs=WHOLE,
        out_shape=jax.ShapeDtypeStruct((B + A8, targets.shape[1]), targets.dtype),
        scratch_shapes=[pltpu.VMEM((1, B), jnp.float32)] * 2 + [pltpu.SemaphoreType.DMA((3,))],
        compiler_params=params(4),
    )(*[far(a) for a in (targets, potential.reshape(1, B), log_tgt.reshape(1, B))])


def near_kernel(sources, log_src, out, log, sems):
    copies = [
        pltpu.make_async_copy(sources, out.at[0 : sources.shape[0]], sems.at[0]),
        pltpu.make_async_copy(log_src, log, sems.at[1]),
    ]
    for copy in copies:
        copy.start()
    for copy in copies:
        copy.wait()
    f = out.shape[1]
    rows = [part[:, h * f : (h + 1) * f] for part in split(log[...]) for h in range(2)]
    out[sources.shape[0] :, :] = jnp.concatenate(rows + [jnp.zeros((2, f), jnp.float32)], axis=0).astype(out.dtype)


def near_call(sources, log_src):
    n, f = sources.shape
    return pl.pallas_call(
        near_kernel,
        name="near_message",
        in_specs=[FAR] * 2,
        out_specs=WHOLE,
        out_shape=jax.ShapeDtypeStruct((n + A8, f), sources.dtype),
        scratch_shapes=[pltpu.VMEM((1, n), jnp.float32), pltpu.SemaphoreType.DMA((2,))],
        compiler_params=params(4),
    )(far(sources), far(log_src.reshape(1, n)))


def joined(picks, msgs):
    def kernel(*refs):
        out = refs[-1]
        extra = []
        for p, (m, k) in enumerate(picks):
            out[p * B : (p + 1) * B, :] = refs[m][k * B : (k + 1) * B, :]
            extra.append(refs[m][refs[m].shape[0] - A8 :, k * B : (k + 1) * B])
        rest = out.shape[1] - len(picks) * B
        extra.append(jnp.zeros((A8, rest), out.dtype))
        out[len(picks) * B :, :] = jnp.concatenate(extra, axis=1)

    return pl.pallas_call(
        kernel,
        in_specs=[WHOLE] * len(msgs),
        out_specs=WHOLE,
        out_shape=jax.ShapeDtypeStruct((len(picks) * B + A8, msgs[0].shape[1]), msgs[0].dtype),
        compiler_params=params(4),
    )(*msgs)


def eye(n):
    return lax.broadcasted_iota(jnp.int32, (n, n), 0) == lax.broadcasted_iota(jnp.int32, (n, n), 1)


def to_col(row):
    n = row.shape[1]
    return jnp.sum(jnp.where(eye(n), jnp.broadcast_to(row, (n, n)), 0.0), axis=1, keepdims=True)


def to_row(col):
    n = col.shape[0]
    return jnp.sum(jnp.where(eye(n), jnp.broadcast_to(col, (n, n)), 0.0), axis=0, keepdims=True)


CH = 512


def block_of(msgs, m, k):
    extra = msgs[m][msgs[m].shape[0] - A8 :, k * B : (k + 1) * B]
    return msgs[m].at[k * B : (k + 1) * B], extra.astype(jnp.float32)


def scores_kernel(picks, last, n_msg, scale2, src, *refs):
    msgs = refs[:n_msg]
    rest = refs[n_msg:]
    if last:
        lse_in, s_out, lse_out, tgt_out, lt_out, tg, pot = rest
    else:
        near, log_src, s_out, lse_out, log_out, tg, pot = rest
        yh = lax.axis_index("yh")
        logs = near[near.shape[0] - A8 :, :].astype(jnp.float32)
        logs = logs[0:2] + logs[2:4] + logs[4:6]
        for q in range(8):
            mine = log_src[:, q * 128 : (q + 1) * 128]
            other = logs[q // 4 : q // 4 + 1, q % 4 * 128 : (q % 4 + 1) * 128]
            log_out[q : q + 1, :] = jnp.where(yh == 0, mine, other) * LOG2E
            log_out[q + 8 : q + 9, :] = jnp.where(yh == 0, other, mine) * LOG2E
    t = tg.shape[0]
    for p, (m, k) in enumerate(picks):
        rows, ex = block_of(msgs, m, k)
        tg[p * B : (p + 1) * B, :] = rows[...]
        po = (ex[0:1] + ex[1:2] + ex[2:3]) * LOG2E
        pot[p * B : (p + 1) * B, :] = jnp.broadcast_to(to_col(po), (B, 128))

    for n in range(src.shape[0] // CH):
        at = slice(n * CH, (n + 1) * CH)
        s_out[:, at] = (
            lax.dot_general(tg[...], src[at, :], (((1,), (1,)), ((), ())), preferred_element_type=jnp.float32) * scale2
        )

        def shifted(r):
            return s_out[r : r + 32, at] + jnp.concatenate([pot[r : r + 32, :]] * (CH // 128), axis=1)

        top = jnp.full((8, CH), -jnp.inf, jnp.float32)
        for r in range(0, t, 32):
            top = jnp.maximum(top, jnp.max(shifted(r).reshape(4, 8, CH), axis=0))
        top = jnp.max(top, axis=0, keepdims=True)
        tot = jnp.zeros((8, CH), jnp.float32)
        for r in range(0, t, 32):
            tot = tot + jnp.sum(jnp.exp2(shifted(r) - top).reshape(4, 8, CH), axis=0)
        lse = top + jnp.log2(jnp.sum(tot, axis=0, keepdims=True))
        if last:
            a = lse_in[:, at]
            hi = jnp.maximum(a, lse)
            lse = hi + jnp.log2(jnp.exp2(a - hi) + jnp.exp2(lse - hi))
            for i in range(CH // 128):
                piece = lse[:, i * 128 : (i + 1) * 128]
                q = n * (CH // 128) + i
                lse_out[:, q : q + 1, :] = jnp.broadcast_to(piece[None], (lse_out.shape[0], 1, 128))
        else:
            lse_out[:, at] = lse

    if last:
        core = lax.axis_index("c")
        pieces = []
        for p, (m, k) in enumerate(PICKS):
            rows, ex = block_of(msgs, m, k)
            lt_out[p : p + 1, 0:B] = (ex[3:4] + ex[4:5] + ex[5:6]) * LOG2E
            pieces.append(rows[...])
        for q in range(len(pieces) // 2):
            flipped = jnp.concatenate(pieces[2 * q : 2 * q + 2], axis=0).T
            for f in range(16):
                to = pl.multiple_of((((f % 2) ^ core) * 8 + f // 2) * 32, 32)
                tgt_out[pl.ds(to, 32), q * 128 : (q + 1) * 128] = flipped[f * 32 : (f + 1) * 32, :]


def scores_call(src, msgs, picks, scale2, *more, last):
    t = len(picks) * B
    ns, f = src.shape
    shapes = [jax.ShapeDtypeStruct((t, ns), jnp.float32)]
    if last:
        shapes += [
            jax.ShapeDtypeStruct((32, ns // 128, 128), jnp.float32),
            jax.ShapeDtypeStruct((f, len(OFF) * B), jnp.bfloat16),
            jax.ShapeDtypeStruct((len(OFF), 128), jnp.float32),
        ]
    else:
        shapes += [jax.ShapeDtypeStruct((1, ns), jnp.float32), jax.ShapeDtypeStruct((ns // 128, 128), jnp.float32)]
    args = [src, *msgs, *more]
    return pl.pallas_call(
        lambda *a: scores_kernel(picks, last, len(msgs), scale2, *a),
        name="scores_last" if last else "scores_first",
        in_specs=[WHOLE] * len(args),
        out_specs=[WHOLE] * len(shapes),
        scratch_shapes=[pltpu.VMEM((t, f), jnp.bfloat16), pltpu.VMEM((t, 128), jnp.float32)],
        out_shape=shapes,
        compiler_params=params(20),
        cost_estimate=pl.CostEstimate(flops=2 * t * ns * f, bytes_accessed=4 * t * ns, transcendentals=t * ns),
    )(*args)


def merged_lse(parts):
    top = jnp.max(parts, axis=0)
    return top + jnp.log2(jnp.sum(jnp.exp2(parts - top[None]), axis=0))


def slot_of(p):
    return (lax.axis_index("z") + OFF[p]) % 16


def cols_kernel(parts, log_src, s1, s2, sp_out, msg_out, held):
    sp = log_src[...] - merged_lse(parts[...])
    for r in range(sp.shape[0]):
        sp_out[:, r * 128 : (r + 1) * 128] = sp[r : r + 1, :]
    held[...] = jnp.zeros_like(held)

    def step(s_ref, p, i):
        pieces = []
        for r in range(B // 8):
            lifted = s_ref[p * B + r * 8 : p * B + r * 8 + 8, :] + sp_out[...]
            top = jnp.max(lifted, axis=1, keepdims=True)
            pieces.append(top + jnp.log2(jnp.sum(jnp.exp2(lifted - top), axis=1, keepdims=True)))
        row = to_row(jnp.concatenate(pieces, axis=0))
        row = jnp.concatenate([row, row], axis=1)
        slot = slot_of(i)
        at = slot // 2
        half = lax.broadcasted_iota(jnp.int32, (1, 128), 1) // B
        held[pl.ds(at, 1), :] = jnp.where(half == slot % 2, row, held[pl.ds(at, 1), :])

    for p in range(len(OFF1)):
        step(s1, p, p)
    for p in range(len(OFF2)):
        step(s2, p, p + len(OFF1))

    msg_out[...] = jnp.broadcast_to(held[...][None], msg_out.shape)


def cols_call(parts, log_src, s1, s2):
    ns = s1.shape[1]
    return pl.pallas_call(
        cols_kernel,
        name="cols",
        in_specs=[WHOLE] * 4,
        out_specs=[WHOLE] * 2,
        scratch_shapes=[pltpu.VMEM((8, 128), jnp.float32)],
        out_shape=[jax.ShapeDtypeStruct((1, ns), jnp.float32), jax.ShapeDtypeStruct((16, 8, 128), jnp.float32)],
        compiler_params=params(16),
    )(parts, log_src, s1, s2)


def moved_kernel(parts, lt, sp, s1, s2, tgt, pot_out, theirs_out, mass_out, wide, tp, lse):
    lse[...] = merged_lse(parts[...])
    for p in range(len(OFF)):
        slot = slot_of(p)
        row = lse[pl.ds(slot // 2, 1), :]
        row = jnp.where(slot % 2 == 0, row[:, :B], row[:, B:])
        tpot = lt[p : p + 1, 0:B] - row
        if p == 0:
            pot_out[:, 0:B] = tpot * LN2
        tp[p * B : (p + 1) * B, :] = jnp.broadcast_to(to_col(tpot), (B, 128))

    t1 = s1.shape[0]
    half = tgt.shape[0] // 2
    for n in range(sp.shape[1] // CH):
        at = slice(n * CH, (n + 1) * CH)
        spn = sp[:, at]
        mass = jnp.zeros((8, CH), jnp.float32)
        for r in range(0, tp.shape[0], 32):
            s_ref, q = (s1, r) if r < t1 else (s2, r - t1)
            e = jnp.exp2(s_ref[q : q + 32, at] + spn + jnp.concatenate([tp[r : r + 32, :]] * (CH // 128), axis=1))
            mass = mass + jnp.sum(e.reshape(4, 8, CH), axis=0)
            wide[r : r + 32, at] = e.astype(jnp.bfloat16)
        mass = jnp.sum(mass, axis=0, keepdims=True)
        mass_out[:, at] = mass
        part = jnp.dot(tgt[half:, :], wide[:, at], preferred_element_type=jnp.float32)
        theirs_out[0:half, at] = part.astype(jnp.bfloat16)
        hi = mass.astype(jnp.bfloat16).astype(jnp.float32)
        pad = jnp.zeros((6, CH), jnp.float32)
        theirs_out[half : half + 8, at] = jnp.concatenate([hi, mass - hi, pad], axis=0).astype(jnp.bfloat16)


def moved_call(parts, lt, sp, s1, s2, tgt):
    ns = s1.shape[1]
    f, t = tgt.shape
    return pl.pallas_call(
        moved_kernel,
        name="moved",
        in_specs=[WHOLE] * 6,
        out_specs=[WHOLE] * 4,
        scratch_shapes=[pltpu.VMEM((t, 128), jnp.float32), pltpu.VMEM((8, 128), jnp.float32)],
        out_shape=[
            jax.ShapeDtypeStruct((1, 128), jnp.float32),
            jax.ShapeDtypeStruct((f // 2 + 8, ns), jnp.bfloat16),
            jax.ShapeDtypeStruct((1, ns), jnp.float32),
            jax.ShapeDtypeStruct((t, ns), jnp.bfloat16),
        ],
        compiler_params=params(20),
    )(parts, lt, sp, s1, s2, tgt)


def mine_kernel(tgt, wide, out):
    for n in range(out.shape[1] // CH):
        at = slice(n * CH, (n + 1) * CH)
        part = jnp.dot(tgt[: out.shape[0], :], wide[:, at], preferred_element_type=jnp.float32)
        out[:, at] = part.astype(jnp.bfloat16)


def mine_call(tgt, wide):
    f, t = tgt.shape
    ns = wide.shape[1]
    return pl.pallas_call(
        mine_kernel,
        name="mine",
        in_specs=[WHOLE] * 2,
        out_specs=WHOLE,
        out_shape=jax.ShapeDtypeStruct((f // 2, ns), jnp.bfloat16),
        compiler_params=params(12),
        cost_estimate=pl.CostEstimate(flops=f * t * ns, bytes_accessed=2 * t * ns, transcendentals=0),
    )(tgt, wide)


def pack_kernel(mine, theirs, mass, out):
    f32 = jnp.float32
    extra = theirs[256:264, :].astype(f32)
    total = mass[...] + extra[0:1] + extra[1:2]
    hi = total.astype(jnp.bfloat16).astype(f32)
    lo = total - hi
    for h in range(2):
        rows = [v[:, (h * 8 + q) * 128 : (h * 8 + q + 1) * 128] for v in (hi, lo) for q in range(8)]
        rows = jnp.concatenate(rows, axis=0).astype(jnp.bfloat16)
        for g in range(8):
            for q in range(8):
                at = (slice(g * 32, (g + 1) * 32), slice((h * 8 + q) * 128, (h * 8 + q + 1) * 128))
                both = mine[at].astype(f32) + theirs[at].astype(f32)
                out[h * 8 + g, q * 32 : (q + 1) * 32, :] = both.astype(jnp.bfloat16)
            out[h * 8 + g, 256:272, :] = rows


def pack_call(mine, theirs, mass):
    return pl.pallas_call(
        pack_kernel,
        name="pack",
        in_specs=[WHOLE] * 3,
        out_specs=WHOLE,
        out_shape=jax.ShapeDtypeStruct((16, 272, 128), jnp.bfloat16),
        compiler_params=params(8),
    )(mine, theirs, mass)


def finish_kernel(parts, sp, tpot, out, src_pot, tgt_pot):
    f32 = jnp.float32

    def added(at):
        total = parts[0, at, :].astype(f32)
        for k in range(1, parts.shape[0]):
            total = total + parts[k, at, :].astype(f32)
        return total

    first = lax.axis_index("yh") == 0
    for q in range(8):
        rows = [sp[:, (h * 8 + q) * 128 : (h * 8 + q + 1) * 128] for h in range(2)]
        src_pot[q : q + 1, :] = jnp.where(first, rows[0], rows[1]) * LN2
    tgt_pot[...] = tpot[:, 0:B]
    mass = added(slice(256, 272))
    mass = mass[:8] + mass[8:]
    for q in range(8):
        image = added(slice(q * 32, (q + 1) * 32)) / mass[q : q + 1, :]
        out[:, q * 128 : (q + 1) * 128] = image.astype(jnp.bfloat16)


def finish_call(parts, sp, tpot):
    return pl.pallas_call(
        finish_kernel,
        name="finish",
        in_specs=[WHOLE] * 3,
        out_specs=[WHOLE] * 3,
        out_shape=[
            jax.ShapeDtypeStruct((32, 1024), jnp.bfloat16),
            jax.ShapeDtypeStruct((8, 128), jnp.float32),
            jax.ShapeDtypeStruct((1, B), jnp.float32),
        ],
        compiler_params=params(8),
    )(parts, sp, tpot)


def body(sources, log_src, targets, potential, log_tgt):
    f = sources.shape[1]
    scale2 = LOG2E / math.sqrt(f)
    yh = lax.axis_index("yh")

    own = own_call(targets, potential, log_tgt)
    ra = from_z(own, 4)
    la = from_z(own, -5)
    near = lax.ppermute(near_call(sources, log_src), ("yh", "yl"), [(0, 3), (3, 0), (1, 2), (2, 1)])
    rb = from_z(joined([(0, 0), (1, 0)], [own, ra]), 2)
    lb = from_z(joined([(1, 0), (0, 0)], [own, la]), -2)
    rc = from_z(joined([(0, 0), (1, 0), (1, 1), (2, 0), (3, 0)], [own, rb, ra, la]), 1)
    lc = from_z(joined([(0, 0), (1, 0), (1, 1), (2, 0)], [own, lb, la]), -1)
    other = near[: sources.shape[0]]
    src = jnp.concatenate([jnp.where(yh == 0, sources, other), jnp.where(yh == 0, other, sources)], axis=0)
    msgs = [own, ra, la, rb, lb, rc, lc]
    s1, lse1, log_all = scores_call(src, msgs[:5], PICKS1, scale2, near, log_src.reshape(1, -1), last=False)
    s2, rows, tgt, lt = scores_call(src, msgs, PICKS2, scale2, lse1, last=True)
    row_parts = lax.all_to_all(rows, PLANE, split_axis=0, concat_axis=0, tiled=True)
    sp, cols = cols_call(row_parts, log_all, s1, s2)
    col_parts = lax.all_to_all(cols, "z", split_axis=0, concat_axis=0, tiled=True)
    tpot, theirs, mass, wide = moved_call(col_parts, lt, sp, s1, s2, tgt)
    theirs = lax.ppermute(theirs, "c", [(0, 1), (1, 0)])
    packed = pack_call(mine_call(tgt, wide), theirs, mass)
    parts = lax.all_to_all(packed, CHIPS, split_axis=0, concat_axis=0, tiled=True)
    mapped, src_pot, tgt_pot = finish_call(parts, sp, tpot)
    return (src_pot.reshape(-1), tgt_pot.reshape(-1), mapped.T)


def solution(mesh):
    torus = Mesh(mesh.devices.reshape(16, 2, 2, 4, 2), AXES)
    src, every = ("z", "yh"), ("z", "yh", "yl", "x", "c")
    return jax.shard_map(
        body,
        mesh=torus,
        in_specs=(P(src, None), P(src), P(every, None), P(every), P(every)),
        out_specs=(P(src), P(every), P(src, ("yl", "x", "c"))),
        check_vma=False,
    )
```

time: 150 us -> 126 us (0.84)
  waiting for transfers between devices: 19.6 us -> 6.41 us
  starting transfers between devices: 52.1 us -> 46.9 us
  blocking collectives: 57.7 us -> 55.4 us
  local copies, waits for them, and re-layouts: 2.23 us -> 0.54 us
  other arithmetic: 3.19 us -> 1.51 us
    ppermute x2 -> x1, waiting for transfers between devices: 8.42 us -> 0.01 us  [body(): lax.ppermute(near_call(sources, log_src), ('yh', 'yl'), [(0, 3), (3, 0),...]
    ppermute x2 -> x1, starting transfers between devices: 12.7 us -> 5.46 us  [body(): lax.ppermute(near_call(sources, log_src), ('yh', 'yl'), [(0, 3), (3, 0),...]
    ppermute x6, waiting for transfers between devices: 8.85 us -> 5.38 us  [from_z(): return lax.ppermute(array, 'z', [((i + d) % n, i) for i in range(n)])]
    ppermute x6, starting transfers between devices: 35.5 us -> 37.5 us  [from_z(): return lax.ppermute(array, 'z', [((i + d) % n, i) for i in range(n)])]
    all_to_all x1, blocking collectives: 17.2 us -> 15.2 us  [body(): lax.all_to_all(rows, PLANE, split_axis=0, concat_axis=0, tiled=True)]
    unnamed x10 -> x2, local copies, waits for them, and re-layouts: 2.16 us -> 0.54 us
    pallas_call x4 -> x6, Pallas kernels: 9.04 us -> 9.87 us  [the longest x1 3.4 us: cols_call(): pl.pallas_call(cols_kernel, name='cols', in_specs=[WHOLE] * 4, out_specs=...]
  transfers between devices with their start and end apart: 9 -> 8, of which waited for: 7 -> 4; matrix products, arithmetic and copies ran while one was open for 1% -> 1% of each run, Pallas kernels for 1% -> 3%
where the time goes in v4:
time: 126 us
  blocking collectives  55.4 us (44%)
  starting transfers between devices  46.9 us (37%)
  Pallas kernels  14.2 us (11%)
  waiting for transfers between devices  6.41 us (5%)
  other arithmetic  1.51 us (1%)
    ppermute x6, starting transfers between devices, from_z(): return lax.ppermute(array, 'z', [((i + d) % n, i) for i in range(n)])  37.5 us
    all_to_all x1, blocking collectives, body(): lax.all_to_all(cols, 'z', split_axis=0, concat_axis=0, tiled=True)  20.2 us
    all_to_all x1, blocking collectives, body(): lax.all_to_all(packed, CHIPS, split_axis=0, concat_axis=0, tiled=True)  20 us
    all_to_all x1, blocking collectives, body(): lax.all_to_all(rows, PLANE, split_axis=0, concat_axis=0, tiled=True)  15.2 us
    ppermute x1, starting transfers between devices, body(): lax.ppermute(near_call(sources, log_src), ('yh', 'yl'), [(0, 3), (3, 0),...  5.46 us
    ppermute x6, waiting for transfers between devices, from_z(): return lax.ppermute(array, 'z', [((i + d) % n, i) for i in range(n)])  5.38 us
    ppermute x1, starting transfers between devices, body(): theirs = lax.ppermute(theirs, 'c', [(0, 1), (1, 0)])  3.99 us
    pallas_call x2, Pallas kernels, scores_call(): pl.pallas_call(lambda *a: scores_kernel(picks, last, len(msgs), scale2, *...  3.74 us
  transfers between devices with their start and end apart: 8, of which 4 were waited for; matrix products, arithmetic and copies ran while one was open for 1% of the time, Pallas kernels for 3%

profile of v4, /device:TPU:1, one launch (start us, length us, event | category | flops | bytes accessed | tf_op | source)
XLA Modules:
  0.0 125.8 jit_solution(7838762396043790671)
XLA Ops:
  0.6 1.3 %near_message.1 = bf16[1032,512]{1,0:T(8,128)(2,1)S(1)} custom-call(bf16[1024,512]{1,0:T(8,128)(2,1)} %sources.1, f32[1,1024]{1,0:T(1,128)} %bitcast.6), custom_call_target="tpu_custom_call" | custom-call | tf_op jit(solution)/shard_map/near_message/pallas_call | solution.py:97
  1.9 5.5 %collective-permute-start = (bf16[1032,512]{1,0:T(8,128)(2,1)S(1)}, bf16[1032,512]{1,0:T(8,128)(2,1)S(1)}, u32[]{:S(2)}, u32[]{:S(2)}) collective-permute-start(bf16[1032,512]{1,0:T(8,128)(2,1)S(1)} %near_message.1), channel_id=1, source_target_pairs={{0,24},{24,0},{8,16},{16,8},{1,25},{25,1},{9,17},{17,9},{2,26},{26... | collective-permute-start | bytes 3170312 | tf_op jit(solution)/shard_map/ppermute | solution.py:431
  7.4 0.9 own.1.refs_0_.a_1_
  8.3 10.2 %collective-permute-start.2 = (bf16[72,512]{1,0:T(8,128)(2,1)S(1)}, bf16[72,512]{1,0:T(8,128)(2,1)S(1)}, u32[]{:S(2)}, u32[]{:S(2)}) collective-permute-start(bf16[72,512]{1,0:T(8,128)(2,1)S(1)} %own.1.refs_0_.a_1_), channel_id=1, source_target_pairs={{352,0},{384,32},{416,64},{448,96},{480,128},{0,160},{32,192},{64,... | collective-permute-start | bytes 221192 | tf_op jit(solution)/shard_map/ppermute | solution.py:38
  18.4 4.2 %collective-permute-start.1 = (bf16[72,512]{1,0:T(8,128)(2,1)S(1)}, bf16[72,512]{1,0:T(8,128)(2,1)S(1)}, u32[]{:S(2)}, u32[]{:S(2)}) collective-permute-start(bf16[72,512]{1,0:T(8,128)(2,1)S(1)} %own.1.refs_0_.a_1_), channel_id=1, source_target_pairs={{128,0},{160,32},{192,64},{224,96},{256,128},{288,160},{320,192},{... | collective-permute-start | bytes 221192 | tf_op jit(solution)/shard_map/ppermute | solution.py:38
  22.7 1.7 %collective-permute-done.2.refs_1_.refs_3_.refs_2_.a_3_ = bf16[72,512]{1,0:T(8,128)(2,1)S(1)} collective-permute-done((bf16[72,512]{1,0:T(8,128)(2,1)S(1)}, bf16[72,512]{1,0:T(8,128)(2,1)S(1)}, u32[]{:S(2)}, u32[]{:S(2)}) %collective-permute-start.2) | collective-permute-done | bytes 73760 | tf_op jit(solution)/shard_map/ppermute | solution.py:38
  24.4 5.5 %collective-permute-start.4 = (bf16[136,512]{1,0:T(8,128)(2,1)S(1)}, bf16[136,512]{1,0:T(8,128)(2,1)S(1)}, u32[]{:S(2)}, u32[]{:S(2)}) collective-permute-start(bf16[136,512]{1,0:T(8,128)(2,1)S(1)} %shard_map.77), channel_id=1, source_target_pairs={{448,0},{480,32},{0,64},{32,96},{64,128},{96,160},{128,192},{160,2... | collective-permute-start | bytes 417800 | tf_op jit(solution)/shard_map/ppermute | solution.py:38
  30.0 3.2 %collective-permute-start.3 = (bf16[136,512]{1,0:T(8,128)(2,1)S(1)}, bf16[136,512]{1,0:T(8,128)(2,1)S(1)}, u32[]{:S(2)}, u32[]{:S(2)}) collective-permute-start(bf16[136,512]{1,0:T(8,128)(2,1)S(1)} %shard_map.76), channel_id=1, source_target_pairs={{64,0},{96,32},{128,64},{160,96},{192,128},{224,160},{256,192},{28... | collective-permute-start | bytes 417800 | tf_op jit(solution)/shard_map/ppermute | solution.py:38
  33.2 0.7 collective-permute-done.4.refs_1_.a_5_
  33.9 6.9 %collective-permute-start.6 = (bf16[264,512]{1,0:T(8,128)(2,1)S(1)}, bf16[264,512]{1,0:T(8,128)(2,1)S(1)}, u32[]{:S(2)}, u32[]{:S(2)}) collective-permute-start(bf16[264,512]{1,0:T(8,128)(2,1)S(1)} %shard_map.79), channel_id=1, source_target_pairs={{480,0},{0,32},{32,64},{64,96},{96,128},{128,160},{160,192},{192,2... | collective-permute-start | bytes 811016 | tf_op jit(solution)/shard_map/ppermute | solution.py:38
  40.9 7.5 %collective-permute-start.5 = (bf16[328,512]{1,0:T(8,128)(2,1)S(1)}, bf16[328,512]{1,0:T(8,128)(2,1)S(1)}, u32[]{:S(2)}, u32[]{:S(2)}) collective-permute-start(bf16[328,512]{1,0:T(8,128)(2,1)S(1)} %shard_map.78), channel_id=1, source_target_pairs={{32,0},{64,32},{96,64},{128,96},{160,128},{192,160},{224,192},{256... | collective-permute-start | bytes 1007624 | tf_op jit(solution)/shard_map/ppermute | solution.py:38
  48.5 1.4 %broadcast_select_fusion.1 = (bf16[1024,512]{1,0:T(8,128)(2,1)S(1)}, bf16[1024,512]{1,0:T(8,128)(2,1)S(1)}) fusion(bf16[1024,512]{1,0:T(8,128)(2,1)} %sources.1, pred[]{:T(512)S(6)} %eq.4, bf16[1032,512]{1,0:T(8,128)(2,1)S(1)} %collective-permute-done.a_6_), kind=kLoop, calls=%fused_computation.2 | loop fusion | flops 1048576 | bytes 4194305 | tf_op jit(solution)/shard_map/jit(_where)/select_n | solution.py:437
  50.5 1.3 %scores_first.1 = (f32[384,2048]{1,0:T(8,128)S(1)}, f32[1,2048]{1,0:T(1,128)S(1)}, f32[16,128]{1,0:T(8,128)S(1)}) custom-call(bf16[2048,512]{1,0:T(8,128)(2,1)S(1)} %pad_maximum_fusion.a_0_, bf16[72,512]{1,0:T(8,128)(2,1)S(1)} %own.1.refs_0_.a_1_, bf16[72,512]{1,0:T(8,128)(2,1)S(1)} %collective-permute-done.1.refs_1_.refs_2_.a_2_, ...), custom_call_target="tpu_custom_call" | custom-call | flops 805306368 | bytes 3145728 | tf_op jit(solution)/shard_map/scores_first/pallas_call | solution.py:227
  51.9 3.0 %collective-permute-done.5.a_6_ = bf16[328,512]{1,0:T(8,128)(2,1)S(1)} collective-permute-done((bf16[328,512]{1,0:T(8,128)(2,1)S(1)}, bf16[328,512]{1,0:T(8,128)(2,1)S(1)}, u32[]{:S(2)}, u32[]{:S(2)}) %collective-permute-start.5) | collective-permute-done | bytes 335904 | tf_op jit(solution)/shard_map/ppermute | solution.py:38
  54.9 2.4 %scores_last.1 = (f32[640,2048]{1,0:T(8,128)S(1)}, f32[32,16,128]{2,1,0:T(8,128)S(1)}, bf16[512,1024]{1,0:T(8,128)(2,1)S(1)}, f32[16,128]{1,0:T(8,128)S(1)}) custom-call(bf16[2048,512]{1,0:T(8,128)(2,1)S(1)} %pad_maximum_fusion.a_0_, bf16[72,512]{1,0:T(8,128)(2,1)S(1)} %own.1.refs_0_.a_1_, bf16[72,512]{1,0:T(8,128)(2,1)S(1)} %collective-permute-done.1.refs_1_.refs_2_.a_2_, ...), custom_call_target="tpu_custom_call" | custom-call | flops 1342177280 | bytes 5242880 | tf_op jit(solution)/shard_map/scores_last/pallas_call | solution.py:227
  57.3 15.2 %all_to_all.15.parts = f32[32,16,128]{2,1,0:T(8,128)S(1)} all-to-all(f32[32,16,128]{2,1,0:T(8,128)S(1)} %get-tuple-element.21), channel_id=1, replica_groups=mesh['z'=16,'yh'=2,'yl'=2,'x'=4,'c'=2] {'yh','yl','x','c'}, dimensions={0} | all-to-all | bytes 524288 | tf_op jit(solution)/shard_map/all_to_all | solution.py:441
  72.6 3.4 %cols.1 = (f32[1,2048]{1,0:T(1,128)S(1)}, f32[16,8,128]{2,1,0:T(8,128)S(1)}) custom-call(f32[32,16,128]{2,1,0:T(8,128)S(1)} %all_to_all.15.parts, f32[16,128]{1,0:T(8,128)S(1)} %get-tuple-element.22.log_src, f32[384,2048]{1,0:T(8,128)S(1)} %get-tuple-element.23.s1, f32[640,2048]{1,0:T(8,128)S(1)} %get-tuple-element.24.s2), custom_call_target="tpu_custom_call" | custom-call | tf_op jit(solution)/shard_map/cols/pallas_call | solution.py:277
  76.0 20.2 %all_to_all.16.parts = f32[16,8,128]{2,1,0:T(8,128)S(1)} all-to-all(f32[16,8,128]{2,1,0:T(8,128)S(1)} %get-tuple-element.25), channel_id=1, replica_groups=mesh['z'=16,'yh'=2,'yl'=2,'x'=4,'c'=2] {'z'}, dimensions={0} | all-to-all | bytes 131072 | tf_op jit(solution)/shard_map/all_to_all | solution.py:443
  96.2 2.2 %moved.1 = (f32[1,128]{1,0:T(1,128)S(1)}, bf16[264,2048]{1,0:T(8,128)(2,1)S(1)}, f32[1,2048]{1,0:T(1,128)S(1)}, bf16[1024,2048]{1,0:T(8,128)(2,1)S(1)}) custom-call(f32[16,8,128]{2,1,0:T(8,128)S(1)} %all_to_all.16.parts, f32[16,128]{1,0:T(8,128)S(1)} %get-tuple-element.26.lt, f32[1,2048]{1,0:T(1,128)S(1)} %get-tuple-element.27.sp, ...), custom_call_target="tpu_custom_call" | custom-call | tf_op jit(solution)/shard_map/moved/pallas_call | solution.py:322
  98.5 4.0 %collective-permute-start.7 = (bf16[264,2048]{1,0:T(8,128)(2,1)S(1)}, bf16[264,2048]{1,0:T(8,128)(2,1)S(1)}, u32[]{:S(2)}, u32[]{:S(2)}) collective-permute-start(bf16[264,2048]{1,0:T(8,128)(2,1)S(1)} %get-tuple-element.29), channel_id=1, source_target_pairs={{0,1},{1,0},{2,3},{3,2},{4,5},{5,4},{6,7},{7,6},{8,9},{9,8},{10,11... | collective-permute-start | bytes 3244040 | tf_op jit(solution)/shard_map/ppermute | solution.py:445
  102.4 1.3 %mine.1 = bf16[256,2048]{1,0:T(8,128)(2,1)S(1)} custom-call(bf16[512,1024]{1,0:T(8,128)(2,1)S(1)} %get-tuple-element.20.tgt, bf16[1024,2048]{1,0:T(8,128)(2,1)S(1)} %get-tuple-element.28.wide), custom_call_target="tpu_custom_call" | custom-call | flops 1073741824 | bytes 4194304 | tf_op jit(solution)/shard_map/mine/pallas_call | solution.py:348
  103.7 1.0 collective-permute-done.7.theirs
  105.0 20.0 %all_to_all.17.parts = bf16[16,272,128]{2,1,0:T(8,128)(2,1)S(1)} all-to-all(bf16[16,272,128]{2,1,0:T(8,128)(2,1)S(1)} %pack.1), channel_id=1, replica_groups=mesh['z'=16,'yh'=2,'yl'=2,'x'=4,'c'=2] {'yh','yl','x'}, dimensions={0} | all-to-all | bytes 2228224 | tf_op jit(solution)/shard_map/all_to_all | solution.py:447
  125.0 0.8 finish.1
  (12 shorter events, 1.3 us)
Async XLA Ops:
  1.9 46.6 %collective-permute-start = (bf16[1032,512]{1,0:T(8,128)(2,1)S(1)}, bf16[1032,512]{1,0:T(8,128)(2,1)S(1)}, u32[]{:S(2)}, u32[]{:S(2)}) collective-permute-start(bf16[1032,512]{1,0:T(8,128)(2,1)S(1)} %near_message.1), channel_id=1, source_target_pairs={{0,24},{24,0},{8,16},{16,8},{1,25},{25,1},{9,17},{17,9},{2,26},{26... | collective-permute-start | bytes 3170312 | tf_op jit(solution)/shard_map/ppermute | solution.py:431
  8.3 16.1 %collective-permute-start.2 = (bf16[72,512]{1,0:T(8,128)(2,1)S(1)}, bf16[72,512]{1,0:T(8,128)(2,1)S(1)}, u32[]{:S(2)}, u32[]{:S(2)}) collective-permute-start(bf16[72,512]{1,0:T(8,128)(2,1)S(1)} %own.1.refs_0_.a_1_), channel_id=1, source_target_pairs={{352,0},{384,32},{416,64},{448,96},{480,128},{0,160},{32,192},{64,... | collective-permute-start | bytes 221192 | tf_op jit(solution)/shard_map/ppermute | solution.py:38
  18.4 11.4 %collective-permute-start.1 = (bf16[72,512]{1,0:T(8,128)(2,1)S(1)}, bf16[72,512]{1,0:T(8,128)(2,1)S(1)}, u32[]{:S(2)}, u32[]{:S(2)}) collective-permute-start(bf16[72,512]{1,0:T(8,128)(2,1)S(1)} %own.1.refs_0_.a_1_), channel_id=1, source_target_pairs={{128,0},{160,32},{192,64},{224,96},{256,128},{288,160},{320,192},{... | collective-permute-start | bytes 221192 | tf_op jit(solution)/shard_map/ppermute | solution.py:38
  24.4 9.4 %collective-permute-start.4 = (bf16[136,512]{1,0:T(8,128)(2,1)S(1)}, bf16[136,512]{1,0:T(8,128)(2,1)S(1)}, u32[]{:S(2)}, u32[]{:S(2)}) collective-permute-start(bf16[136,512]{1,0:T(8,128)(2,1)S(1)} %shard_map.77), channel_id=1, source_target_pairs={{448,0},{480,32},{0,64},{32,96},{64,128},{96,160},{128,192},{160,2... | collective-permute-start | bytes 417800 | tf_op jit(solution)/shard_map/ppermute | solution.py:38
  30.0 10.9 %collective-permute-start.3 = (bf16[136,512]{1,0:T(8,128)(2,1)S(1)}, bf16[136,512]{1,0:T(8,128)(2,1)S(1)}, u32[]{:S(2)}, u32[]{:S(2)}) collective-permute-start(bf16[136,512]{1,0:T(8,128)(2,1)S(1)} %shard_map.76), channel_id=1, source_target_pairs={{64,0},{96,32},{128,64},{160,96},{192,128},{224,160},{256,192},{28... | collective-permute-start | bytes 417800 | tf_op jit(solution)/shard_map/ppermute | solution.py:38
  33.9 18.0 %collective-permute-start.6 = (bf16[264,512]{1,0:T(8,128)(2,1)S(1)}, bf16[264,512]{1,0:T(8,128)(2,1)S(1)}, u32[]{:S(2)}, u32[]{:S(2)}) collective-permute-start(bf16[264,512]{1,0:T(8,128)(2,1)S(1)} %shard_map.79), channel_id=1, source_target_pairs={{480,0},{0,32},{32,64},{64,96},{96,128},{128,160},{160,192},{192,2... | collective-permute-start | bytes 811016 | tf_op jit(solution)/shard_map/ppermute | solution.py:38
  40.9 13.9 %collective-permute-start.5 = (bf16[328,512]{1,0:T(8,128)(2,1)S(1)}, bf16[328,512]{1,0:T(8,128)(2,1)S(1)}, u32[]{:S(2)}, u32[]{:S(2)}) collective-permute-start(bf16[328,512]{1,0:T(8,128)(2,1)S(1)} %shard_map.78), channel_id=1, source_target_pairs={{32,0},{64,32},{96,64},{128,96},{160,128},{192,160},{224,192},{256... | collective-permute-start | bytes 1007624 | tf_op jit(solution)/shard_map/ppermute | solution.py:38
  49.9 0.7 copy-start
  98.5 6.3 %collective-permute-start.7 = (bf16[264,2048]{1,0:T(8,128)(2,1)S(1)}, bf16[264,2048]{1,0:T(8,128)(2,1)S(1)}, u32[]{:S(2)}, u32[]{:S(2)}) collective-permute-start(bf16[264,2048]{1,0:T(8,128)(2,1)S(1)} %get-tuple-element.29), channel_id=1, source_target_pairs={{0,1},{1,0},{2,3},{3,2},{4,5},{5,4},{6,7},{7,6},{8,9},{9,8},{10,11... | collective-permute-start | bytes 3244040 | tf_op jit(solution)/shard_map/ppermute | solution.py:445

commit v5 on v4

--- a/solution.py
+++ b/solution.py
@@ -12,8 +12,8 @@
 WHOLE = pl.BlockSpec(memory_space=pltpu.VMEM)
 FAR = pl.BlockSpec(memory_space=pltpu.HBM)
 AXES = ("z", "yh", "yl", "x", "c")
-PLANE = ("yh", "yl", "x", "c")
-CHIPS = ("yh", "yl", "x")
+PLANE = ("c", "x", "yh", "yl")
+CHIPS = ("x", "yh", "yl")
 LOG2E = math.log2(math.e)
 LN2 = math.log(2.0)
 B = 64
@@ -147,93 +147,122 @@
     return msgs[m].at[k * B : (k + 1) * B], extra.astype(jnp.float32)
 
 
-def scores_kernel(picks, last, n_msg, scale2, src, *refs):
-    msgs = refs[:n_msg]
-    rest = refs[n_msg:]
-    if last:
-        lse_in, s_out, lse_out, tgt_out, lt_out, tg, pot = rest
-    else:
-        near, log_src, s_out, lse_out, log_out, tg, pot = rest
-        yh = lax.axis_index("yh")
-        logs = near[near.shape[0] - A8 :, :].astype(jnp.float32)
-        logs = logs[0:2] + logs[2:4] + logs[4:6]
-        for q in range(8):
-            mine = log_src[:, q * 128 : (q + 1) * 128]
-            other = logs[q // 4 : q // 4 + 1, q % 4 * 128 : (q % 4 + 1) * 128]
-            log_out[q : q + 1, :] = jnp.where(yh == 0, mine, other) * LOG2E
-            log_out[q + 8 : q + 9, :] = jnp.where(yh == 0, other, mine) * LOG2E
-    t = tg.shape[0]
+def row_lse(s_out, at, pot):
+    t = pot.shape[0]
+
+    def shifted(r):
+        return s_out[r : r + 32, at] + jnp.concatenate([pot[r : r + 32, :]] * (CH // 128), axis=1)
+
+    top = jnp.full((8, CH), -jnp.inf, jnp.float32)
+    for r in range(0, t, 32):
+        top = jnp.maximum(top, jnp.max(shifted(r).reshape(4, 8, CH), axis=0))
+    top = jnp.max(top, axis=0, keepdims=True)
+    tot = jnp.zeros((8, CH), jnp.float32)
+    for r in range(0, t, 32):
+        tot = tot + jnp.sum(jnp.exp2(shifted(r) - top).reshape(4, 8, CH), axis=0)
+    return top + jnp.log2(jnp.sum(tot, axis=0, keepdims=True))
+
+
+def scores(tg, src, scale2):
+    return lax.dot_general(tg, src, (((1,), (1,)), ((), ())), preferred_element_type=jnp.float32) * scale2
+
+
+def laid_out(msgs, picks, tg, pot):
     for p, (m, k) in enumerate(picks):
         rows, ex = block_of(msgs, m, k)
         tg[p * B : (p + 1) * B, :] = rows[...]
         po = (ex[0:1] + ex[1:2] + ex[2:3]) * LOG2E
         pot[p * B : (p + 1) * B, :] = jnp.broadcast_to(to_col(po), (B, 128))
 
+
+def own_first_kernel(scale2, src, *refs):
+    msgs, (s_out, lse_out, tg, pot) = refs[:-4], refs[-4:]
+    laid_out(msgs, PICKS1, tg, pot)
     for n in range(src.shape[0] // CH):
         at = slice(n * CH, (n + 1) * CH)
-        s_out[:, at] = (
-            lax.dot_general(tg[...], src[at, :], (((1,), (1,)), ((), ())), preferred_element_type=jnp.float32) * scale2
-        )
-
-        def shifted(r):
-            return s_out[r : r + 32, at] + jnp.concatenate([pot[r : r + 32, :]] * (CH // 128), axis=1)
-
-        top = jnp.full((8, CH), -jnp.inf, jnp.float32)
-        for r in range(0, t, 32):
-            top = jnp.maximum(top, jnp.max(shifted(r).reshape(4, 8, CH), axis=0))
-        top = jnp.max(top, axis=0, keepdims=True)
-        tot = jnp.zeros((8, CH), jnp.float32)
-        for r in range(0, t, 32):
-            tot = tot + jnp.sum(jnp.exp2(shifted(r) - top).reshape(4, 8, CH), axis=0)
-        lse = top + jnp.log2(jnp.sum(tot, axis=0, keepdims=True))
-        if last:
-            a = lse_in[:, at]
-            hi = jnp.maximum(a, lse)
-            lse = hi + jnp.log2(jnp.exp2(a - hi) + jnp.exp2(lse - hi))
+        s_out[:, at] = scores(tg[...], src[at, :], scale2)
+        lse_out[:, at] = row_lse(s_out, at, pot)
+
+
+def own_last_kernel(scale2, src, lse_in, tg1, pot1, *refs):
+    msgs, (s_out, lse_out, tgs, pots, tgt_out, lt_out, tg, pot) = refs[:-8], refs[-8:]
+    laid_out(msgs, PICKS2, tg, pot)
+    for n in range(src.shape[0] // CH):
+        at = slice(n * CH, (n + 1) * CH)
+        s_out[:, at] = scores(tg[...], src[at, :], scale2)
+        lse_out[:, at] = added_lse(lse_in[:, at], row_lse(s_out, at, pot))
+    t1 = tg1.shape[0]
+    tgs[:t1, :] = tg1[...]
+    tgs[t1:, :] = tg[...]
+    pots[:t1, :] = pot1[...]
+    pots[t1:, :] = pot[...]
+    core = lax.axis_index("c")
+    for p, (m, k) in enumerate(PICKS):
+        _, ex = block_of(msgs, m, k)
+        lt_out[p : p + 1, 0:B] = (ex[3:4] + ex[4:5] + ex[5:6]) * LOG2E
+    for q in range(tgs.shape[0] // 128):
+        at = slice(q * 128, (q + 1) * 128)
+        flipped = (tg1[at, :] if q * 128 < t1 else tg[q * 128 - t1 : (q + 1) * 128 - t1, :]).T
+        for f in range(16):
+            to = pl.multiple_of((((f % 2) ^ core) * 8 + f // 2) * 32, 32)
+            tgt_out[pl.ds(to, 32), at] = flipped[f * 32 : (f + 1) * 32, :]
+
+
+def near_scores_kernel(scale2, near, log_src, lse_in, tgs, pots, s_out, rows_out, log_out):
+    yh = lax.axis_index("yh")
+    ns = near.shape[0] - A8
+    logs = near[ns:, :].astype(jnp.float32)
+    logs = logs[0:2] + logs[2:4] + logs[4:6]
+    for q in range(8):
+        log_out[0, q : q + 1, :] = log_src[:, q * 128 : (q + 1) * 128] * LOG2E
+        log_out[1, q : q + 1, :] = logs[q // 4 : q // 4 + 1, q % 4 * 128 : (q % 4 + 1) * 128] * LOG2E
+    for n in range(ns // CH):
+        at = slice(n * CH, (n + 1) * CH)
+        s_out[:, at] = scores(tgs[...], near[at, :], scale2)
+        for block, lse in ((yh, lse_in[:, at]), (1 - yh, row_lse(s_out, at, pots))):
             for i in range(CH // 128):
-                piece = lse[:, i * 128 : (i + 1) * 128]
+                piece = jnp.broadcast_to(lse[:, i * 128 : (i + 1) * 128][None], (rows_out.shape[0], 1, 128))
                 q = n * (CH // 128) + i
-                lse_out[:, q : q + 1, :] = jnp.broadcast_to(piece[None], (lse_out.shape[0], 1, 128))
-        else:
-            lse_out[:, at] = lse
-
-    if last:
-        core = lax.axis_index("c")
-        pieces = []
-        for p, (m, k) in enumerate(PICKS):
-            rows, ex = block_of(msgs, m, k)
-            lt_out[p : p + 1, 0:B] = (ex[3:4] + ex[4:5] + ex[5:6]) * LOG2E
-            pieces.append(rows[...])
-        for q in range(len(pieces) // 2):
-            flipped = jnp.concatenate(pieces[2 * q : 2 * q + 2], axis=0).T
-            for f in range(16):
-                to = pl.multiple_of((((f % 2) ^ core) * 8 + f // 2) * 32, 32)
-                tgt_out[pl.ds(to, 32), q * 128 : (q + 1) * 128] = flipped[f * 32 : (f + 1) * 32, :]
-
-
-def scores_call(src, msgs, picks, scale2, *more, last):
-    t = len(picks) * B
-    ns, f = src.shape
-    shapes = [jax.ShapeDtypeStruct((t, ns), jnp.float32)]
-    if last:
-        shapes += [
-            jax.ShapeDtypeStruct((32, ns // 128, 128), jnp.float32),
-            jax.ShapeDtypeStruct((f, len(OFF) * B), jnp.bfloat16),
-            jax.ShapeDtypeStruct((len(OFF), 128), jnp.float32),
-        ]
-    else:
-        shapes += [jax.ShapeDtypeStruct((1, ns), jnp.float32), jax.ShapeDtypeStruct((ns // 128, 128), jnp.float32)]
-    args = [src, *msgs, *more]
-    return pl.pallas_call(
-        lambda *a: scores_kernel(picks, last, len(msgs), scale2, *a),
-        name="scores_last" if last else "scores_first",
+                rows_out[:, block, q : q + 1, :] = piece
+
+
+def added_lse(a, b):
+    top = jnp.maximum(a, b)
+    return top + jnp.log2(jnp.exp2(a - top) + jnp.exp2(b - top))
+
+
+def scores_call(kernel, scale2, args, shapes, scratch, flops):
+    return pl.pallas_call(
+        lambda *a: kernel(scale2, *a),
         in_specs=[WHOLE] * len(args),
         out_specs=[WHOLE] * len(shapes),
-        scratch_shapes=[pltpu.VMEM((t, f), jnp.bfloat16), pltpu.VMEM((t, 128), jnp.float32)],
-        out_shape=shapes,
+        scratch_shapes=[pltpu.VMEM(s, d) for s, d in scratch],
+        out_shape=[jax.ShapeDtypeStruct(s, d) for s, d in shapes],
         compiler_params=params(20),
-        cost_estimate=pl.CostEstimate(flops=2 * t * ns * f, bytes_accessed=4 * t * ns, transcendentals=t * ns),
+        cost_estimate=pl.CostEstimate(flops=flops, bytes_accessed=1 << 22, transcendentals=1 << 20),
     )(*args)
+
+
+def all_scores(sources, log_src, near, msgs, scale2):
+    ns, f = sources.shape
+    f32, bf = jnp.float32, jnp.bfloat16
+    t1, t2 = len(PICKS1) * B, len(PICKS2) * B
+    t = t1 + t2
+    flops = lambda rows: 2 * rows * ns * f
+    s1, lse1, tg1, pot1 = scores_call(
+        own_first_kernel, scale2, [sources, *msgs[:5]],
+        [((t1, ns), f32), ((1, ns), f32), ((t1, f), bf), ((t1, 128), f32)], [], flops(t1),
+    )
+    s2, lse2, tgs, pots, tgt, lt = scores_call(
+        own_last_kernel, scale2, [sources, lse1, tg1, pot1, *msgs],
+        [((t2, ns), f32), ((1, ns), f32), ((t, f), bf), ((t, 128), f32), ((f, t), bf), ((len(OFF), 128), f32)],
+        [((t2, f), bf), ((t2, 128), f32)], flops(t2),
+    )
+    s3, rows, logs = scores_call(
+        near_scores_kernel, scale2, [near, log_src.reshape(1, ns), lse2, tgs, pots],
+        [((t, ns), f32), ((32, 2, ns // 128, 128), f32), ((2, ns // 128, 128), f32)], [], flops(t),
+    )
+    return (s1, s2, s3), rows, logs, tgt, lt
 
 
 def merged_lse(parts):
@@ -245,47 +274,49 @@
     return (lax.axis_index("z") + OFF[p]) % 16
 
 
-def cols_kernel(parts, log_src, s1, s2, sp_out, msg_out, held):
-    sp = log_src[...] - merged_lse(parts[...])
-    for r in range(sp.shape[0]):
-        sp_out[:, r * 128 : (r + 1) * 128] = sp[r : r + 1, :]
+def cols_kernel(parts, logs, s1, s2, s3, sp_out, msg_out, held, lse):
+    yh = lax.axis_index("yh")
+    for h in range(2):
+        lse[h] = merged_lse(parts[:, h])
+    for h, block in enumerate((yh, 1 - yh)):
+        sp = logs[h] - lse[block]
+        for r in range(8):
+            sp_out[:, (h * 8 + r) * 128 : (h * 8 + r + 1) * 128] = sp[r : r + 1, :]
     held[...] = jnp.zeros_like(held)
-
-    def step(s_ref, p, i):
+    ns = s1.shape[1]
+    n1 = len(OFF1)
+    for p in range(len(OFF)):
+        s_ref, base = (s1, p * B) if p < n1 else (s2, (p - n1) * B)
         pieces = []
-        for r in range(B // 8):
-            lifted = s_ref[p * B + r * 8 : p * B + r * 8 + 8, :] + sp_out[...]
-            top = jnp.max(lifted, axis=1, keepdims=True)
-            pieces.append(top + jnp.log2(jnp.sum(jnp.exp2(lifted - top), axis=1, keepdims=True)))
+        for r in range(0, B, 8):
+            mine = s_ref[base + r : base + r + 8, :] + sp_out[:, :ns]
+            other = s3[p * B + r : p * B + r + 8, :] + sp_out[:, ns:]
+            top = jnp.max(jnp.maximum(mine, other), axis=1, keepdims=True)
+            total = jnp.sum(jnp.exp2(mine - top) + jnp.exp2(other - top), axis=1, keepdims=True)
+            pieces.append(top + jnp.log2(total))
         row = to_row(jnp.concatenate(pieces, axis=0))
         row = jnp.concatenate([row, row], axis=1)
-        slot = slot_of(i)
+        slot = slot_of(p)
         at = slot // 2
         half = lax.broadcasted_iota(jnp.int32, (1, 128), 1) // B
         held[pl.ds(at, 1), :] = jnp.where(half == slot % 2, row, held[pl.ds(at, 1), :])
-
-    for p in range(len(OFF1)):
-        step(s1, p, p)
-    for p in range(len(OFF2)):
-        step(s2, p, p + len(OFF1))
-
     msg_out[...] = jnp.broadcast_to(held[...][None], msg_out.shape)
 
 
-def cols_call(parts, log_src, s1, s2):
-    ns = s1.shape[1]
+def cols_call(parts, logs, s):
+    ns = s[0].shape[1]
     return pl.pallas_call(
         cols_kernel,
         name="cols",
-        in_specs=[WHOLE] * 4,
+        in_specs=[WHOLE] * 5,
         out_specs=[WHOLE] * 2,
-        scratch_shapes=[pltpu.VMEM((8, 128), jnp.float32)],
-        out_shape=[jax.ShapeDtypeStruct((1, ns), jnp.float32), jax.ShapeDtypeStruct((16, 8, 128), jnp.float32)],
+        scratch_shapes=[pltpu.VMEM((8, 128), jnp.float32), pltpu.VMEM((2, 8, 128), jnp.float32)],
+        out_shape=[jax.ShapeDtypeStruct((1, 2 * ns), jnp.float32), jax.ShapeDtypeStruct((16, 8, 128), jnp.float32)],
         compiler_params=params(16),
-    )(parts, log_src, s1, s2)
-
-
-def moved_kernel(parts, lt, sp, s1, s2, tgt, pot_out, theirs_out, mass_out, wide, tp, lse):
+    )(parts, logs, *s)
+
+
+def moved_kernel(parts, lt, sp, s1, s2, s3, tgt, pot_out, theirs_out, mass_out, wide, tp, lse):
     lse[...] = merged_lse(parts[...])
     for p in range(len(OFF)):
         slot = slot_of(p)
@@ -297,14 +328,18 @@
         tp[p * B : (p + 1) * B, :] = jnp.broadcast_to(to_col(tpot), (B, 128))
 
     t1 = s1.shape[0]
+    ns = s1.shape[1]
     half = tgt.shape[0] // 2
     for n in range(sp.shape[1] // CH):
         at = slice(n * CH, (n + 1) * CH)
         spn = sp[:, at]
         mass = jnp.zeros((8, CH), jnp.float32)
         for r in range(0, tp.shape[0], 32):
-            s_ref, q = (s1, r) if r < t1 else (s2, r - t1)
-            e = jnp.exp2(s_ref[q : q + 32, at] + spn + jnp.concatenate([tp[r : r + 32, :]] * (CH // 128), axis=1))
+            if n * CH < ns:
+                s = s1[r : r + 32, at] if r < t1 else s2[r - t1 : r - t1 + 32, at]
+            else:
+                s = s3[r : r + 32, n * CH - ns : (n + 1) * CH - ns]
+            e = jnp.exp2(s + spn + jnp.concatenate([tp[r : r + 32, :]] * (CH // 128), axis=1))
             mass = mass + jnp.sum(e.reshape(4, 8, CH), axis=0)
             wide[r : r + 32, at] = e.astype(jnp.bfloat16)
         mass = jnp.sum(mass, axis=0, keepdims=True)
@@ -316,13 +351,13 @@
         theirs_out[half : half + 8, at] = jnp.concatenate([hi, mass - hi, pad], axis=0).astype(jnp.bfloat16)
 
 
-def moved_call(parts, lt, sp, s1, s2, tgt):
-    ns = s1.shape[1]
+def moved_call(parts, lt, sp, s, tgt):
+    ns = sp.shape[1]
     f, t = tgt.shape
     return pl.pallas_call(
         moved_kernel,
         name="moved",
-        in_specs=[WHOLE] * 6,
+        in_specs=[WHOLE] * 7,
         out_specs=[WHOLE] * 4,
         scratch_shapes=[pltpu.VMEM((t, 128), jnp.float32), pltpu.VMEM((8, 128), jnp.float32)],
         out_shape=[
@@ -332,7 +367,7 @@
             jax.ShapeDtypeStruct((t, ns), jnp.bfloat16),
         ],
         compiler_params=params(20),
-    )(parts, lt, sp, s1, s2, tgt)
+    )(parts, lt, sp, *s, tgt)
 
 
 def mine_kernel(tgt, wide, out):
@@ -362,15 +397,18 @@
     total = mass[...] + extra[0:1] + extra[1:2]
     hi = total.astype(jnp.bfloat16).astype(f32)
     lo = total - hi
+    yh = lax.axis_index("yh")
     for h in range(2):
+        to = (h ^ yh) * 2
         rows = [v[:, (h * 8 + q) * 128 : (h * 8 + q + 1) * 128] for v in (hi, lo) for q in range(8)]
         rows = jnp.concatenate(rows, axis=0).astype(jnp.bfloat16)
         for g in range(8):
+            at_chip = g % 4 * 4 + g // 4
             for q in range(8):
                 at = (slice(g * 32, (g + 1) * 32), slice((h * 8 + q) * 128, (h * 8 + q + 1) * 128))
                 both = mine[at].astype(f32) + theirs[at].astype(f32)
-                out[h * 8 + g, q * 32 : (q + 1) * 32, :] = both.astype(jnp.bfloat16)
-            out[h * 8 + g, 256:272, :] = rows
+                out[to + at_chip, q * 32 : (q + 1) * 32, :] = both.astype(jnp.bfloat16)
+            out[to + at_chip, 256:272, :] = rows
 
 
 def pack_call(mine, theirs, mass):
@@ -393,10 +431,8 @@
             total = total + parts[k, at, :].astype(f32)
         return total
 
-    first = lax.axis_index("yh") == 0
     for q in range(8):
-        rows = [sp[:, (h * 8 + q) * 128 : (h * 8 + q + 1) * 128] for h in range(2)]
-        src_pot[q : q + 1, :] = jnp.where(first, rows[0], rows[1]) * LN2
+        src_pot[q : q + 1, :] = sp[:, q * 128 : (q + 1) * 128] * LN2
     tgt_pot[...] = tpot[:, 0:B]
     mass = added(slice(256, 272))
     mass = mass[:8] + mass[8:]
@@ -423,7 +459,6 @@
 def body(sources, log_src, targets, potential, log_tgt):
     f = sources.shape[1]
     scale2 = LOG2E / math.sqrt(f)
-    yh = lax.axis_index("yh")
 
     own = own_call(targets, potential, log_tgt)
     ra = from_z(own, 4)
@@ -433,15 +468,11 @@
     lb = from_z(joined([(1, 0), (0, 0)], [own, la]), -2)
     rc = from_z(joined([(0, 0), (1, 0), (1, 1), (2, 0), (3, 0)], [own, rb, ra, la]), 1)
     lc = from_z(joined([(0, 0), (1, 0), (1, 1), (2, 0)], [own, lb, la]), -1)
-    other = near[: sources.shape[0]]
-    src = jnp.concatenate([jnp.where(yh == 0, sources, other), jnp.where(yh == 0, other, sources)], axis=0)
-    msgs = [own, ra, la, rb, lb, rc, lc]
-    s1, lse1, log_all = scores_call(src, msgs[:5], PICKS1, scale2, near, log_src.reshape(1, -1), last=False)
-    s2, rows, tgt, lt = scores_call(src, msgs, PICKS2, scale2, lse1, last=True)
+    s, rows, logs, tgt, lt = all_scores(sources, log_src, near, [own, ra, la, rb, lb, rc, lc], scale2)
     row_parts = lax.all_to_all(rows, PLANE, split_axis=0, concat_axis=0, tiled=True)
-    sp, cols = cols_call(row_parts, log_all, s1, s2)
+    sp, cols = cols_call(row_parts, logs, s)
     col_parts = lax.all_to_all(cols, "z", split_axis=0, concat_axis=0, tiled=True)
-    tpot, theirs, mass, wide = moved_call(col_parts, lt, sp, s1, s2, tgt)
+    tpot, theirs, mass, wide = moved_call(col_parts, lt, sp, s, tgt)
     theirs = lax.ppermute(theirs, "c", [(0, 1), (1, 0)])
     packed = pack_call(mine_call(tgt, wide), theirs, mass)
     parts = lax.all_to_all(packed, CHIPS, split_axis=0, concat_axis=0, tiled=True)

time: 126 us -> 128 us (1.016)
  waiting for transfers between devices: 6.41 us -> 18.5 us
  starting transfers between devices: 46.9 us -> 38 us
  other arithmetic: 1.51 us -> 0 us
    ppermute x6, waiting for transfers between devices: 5.38 us -> 17.5 us  [from_z(): return lax.ppermute(array, 'z', [((i + d) % n, i) for i in range(n)])]
    ppermute x6, starting transfers between devices: 37.5 us -> 28.5 us  [from_z(): return lax.ppermute(array, 'z', [((i + d) % n, i) for i in range(n)])]
    select_n x1 -> x0, other arithmetic: 1.37 us -> none  [body(): jnp.where(yh == 0, sources, other)]
    pallas_call x4 -> x5, Pallas kernels: 9.38 us -> 10 us  [the longest x3 4.27 us: scores_call(): pl.pallas_call(lambda *a: kernel(scale2, *a), in_specs=[WHOLE] * len(args...]
  transfers between devices with their start and end apart: 8 -> 8, of which waited for: 4 -> 6; matrix products, arithmetic and copies ran while one was open for 1% -> 0% of each run, Pallas kernels for 3% -> 4%
where the time goes in v5:
time: 128 us; the launch traced here: 127 us
  blocking collectives  55.3 us (43%)
  starting transfers between devices  38 us (30%)
  waiting for transfers between devices  18.5 us (14%)
  Pallas kernels  14.8 us (12%)
    ppermute x6, starting transfers between devices, from_z(): return lax.ppermute(array, 'z', [((i + d) % n, i) for i in range(n)])  28.5 us
    all_to_all x1, blocking collectives, body(): lax.all_to_all(packed, CHIPS, split_axis=0, concat_axis=0, tiled=True)  20.2 us
    all_to_all x1, blocking collectives, body(): lax.all_to_all(cols, 'z', split_axis=0, concat_axis=0, tiled=True)  20.1 us
    ppermute x6, waiting for transfers between devices, from_z(): return lax.ppermute(array, 'z', [((i + d) % n, i) for i in range(n)])  17.5 us
    all_to_all x1, blocking collectives, body(): lax.all_to_all(rows, PLANE, split_axis=0, concat_axis=0, tiled=True)  14.9 us
    ppermute x1, starting transfers between devices, body(): lax.ppermute(near_call(sources, log_src), ('yh', 'yl'), [(0, 3), (3, 0),...  5.59 us
    pallas_call x3, Pallas kernels, scores_call(): pl.pallas_call(lambda *a: kernel(scale2, *a), in_specs=[WHOLE] * len(args...  4.27 us
    ppermute x1, starting transfers between devices, body(): theirs = lax.ppermute(theirs, 'c', [(0, 1), (1, 0)])  3.95 us
  transfers between devices with their start and end apart: 8, of which 6 were waited for; matrix products, arithmetic and copies ran while one was open for 0% of the time, Pallas kernels for 4%

profile of v5, /device:TPU:1, one launch (start us, length us, event | category | flops | bytes accessed | tf_op | source)
XLA Modules:
  0.0 127.5 jit_solution(16067075297308331119)
XLA Ops:
  0.6 1.3 near_message.1
  1.9 5.6 %collective-permute-start.6 = (bf16[1032,512]{1,0:T(8,128)(2,1)S(1)}, bf16[1032,512]{1,0:T(8,128)(2,1)S(1)}, u32[]{:S(2)}, u32[]{:S(2)}) collective-permute-start(bf16[1032,512]{1,0:T(8,128)(2,1)S(1)} %near_message.1), channel_id=1, source_target_pairs={{0,24},{24,0},{8,16},{16,8},{1,25},{25,1},{9,17},{17,9},{2,26},{26... | collective-permute-start | bytes 3170312 | tf_op jit(solution)/shard_map/ppermute | solution.py:466
  7.5 0.9 own.1.refs_0_.a_1_.a_4_
  8.4 12.5 %collective-permute-start = (bf16[72,512]{1,0:T(8,128)(2,1)S(1)}, bf16[72,512]{1,0:T(8,128)(2,1)S(1)}, u32[]{:S(2)}, u32[]{:S(2)}) collective-permute-start(bf16[72,512]{1,0:T(8,128)(2,1)S(1)} %own.1.refs_0_.a_1_.a_4_), channel_id=1, source_target_pairs={{128,0},{160,32},{192,64},{224,96},{256,128},{288,160},{320,192},{... | collective-permute-start | bytes 221192 | tf_op jit(solution)/shard_map/ppermute | solution.py:38
  20.9 1.9 %collective-permute-start.1 = (bf16[72,512]{1,0:T(8,128)(2,1)S(1)}, bf16[72,512]{1,0:T(8,128)(2,1)S(1)}, u32[]{:S(2)}, u32[]{:S(2)}) collective-permute-start(bf16[72,512]{1,0:T(8,128)(2,1)S(1)} %own.1.refs_0_.a_1_.a_4_), channel_id=1, source_target_pairs={{352,0},{384,32},{416,64},{448,96},{480,128},{0,160},{32,192},{64,... | collective-permute-start | bytes 221192 | tf_op jit(solution)/shard_map/ppermute | solution.py:38
  22.8 1.6 %collective-permute-done.refs_1_.a_2_.refs_2_.a_5_ = bf16[72,512]{1,0:T(8,128)(2,1)S(1)} collective-permute-done((bf16[72,512]{1,0:T(8,128)(2,1)S(1)}, bf16[72,512]{1,0:T(8,128)(2,1)S(1)}, u32[]{:S(2)}, u32[]{:S(2)}) %collective-permute-start) | collective-permute-done | bytes 73760 | tf_op jit(solution)/shard_map/ppermute | solution.py:38
  24.5 7.4 %collective-permute-start.2 = (bf16[136,512]{1,0:T(8,128)(2,1)S(1)}, bf16[136,512]{1,0:T(8,128)(2,1)S(1)}, u32[]{:S(2)}, u32[]{:S(2)}) collective-permute-start(bf16[136,512]{1,0:T(8,128)(2,1)S(1)} %shard_map.76), channel_id=1, source_target_pairs={{64,0},{96,32},{128,64},{160,96},{192,128},{224,160},{256,192},{28... | collective-permute-start | bytes 417800 | tf_op jit(solution)/shard_map/ppermute | solution.py:38
  31.9 2.6 %collective-permute-done.1.refs_1_.a_3_.refs_3_.refs_2_.a_6_ = bf16[72,512]{1,0:T(8,128)(2,1)S(1)} collective-permute-done((bf16[72,512]{1,0:T(8,128)(2,1)S(1)}, bf16[72,512]{1,0:T(8,128)(2,1)S(1)}, u32[]{:S(2)}, u32[]{:S(2)}) %collective-permute-start.1) | collective-permute-done | bytes 73760 | tf_op jit(solution)/shard_map/ppermute | solution.py:38
  34.6 1.9 %collective-permute-start.3 = (bf16[136,512]{1,0:T(8,128)(2,1)S(1)}, bf16[136,512]{1,0:T(8,128)(2,1)S(1)}, u32[]{:S(2)}, u32[]{:S(2)}) collective-permute-start(bf16[136,512]{1,0:T(8,128)(2,1)S(1)} %shard_map.77), channel_id=1, source_target_pairs={{448,0},{480,32},{0,64},{32,96},{64,128},{96,160},{128,192},{160,2... | collective-permute-start | bytes 417800 | tf_op jit(solution)/shard_map/ppermute | solution.py:38
  37.3 1.9 %collective-permute-start.4 = (bf16[328,512]{1,0:T(8,128)(2,1)S(1)}, bf16[328,512]{1,0:T(8,128)(2,1)S(1)}, u32[]{:S(2)}, u32[]{:S(2)}) collective-permute-start(bf16[328,512]{1,0:T(8,128)(2,1)S(1)} %shard_map.79), channel_id=1, source_target_pairs={{32,0},{64,32},{96,64},{128,96},{160,128},{192,160},{224,192},{256... | collective-permute-start | bytes 1007624 | tf_op jit(solution)/shard_map/ppermute | solution.py:38
  39.2 4.1 %collective-permute-done.3.a_5_.refs_1_.a_8_ = bf16[136,512]{1,0:T(8,128)(2,1)S(1)} collective-permute-done((bf16[136,512]{1,0:T(8,128)(2,1)S(1)}, bf16[136,512]{1,0:T(8,128)(2,1)S(1)}, u32[]{:S(2)}, u32[]{:S(2)}) %collective-permute-start.3) | collective-permute-done | bytes 139296 | tf_op jit(solution)/shard_map/ppermute | solution.py:38
  43.4 2.8 %collective-permute-start.5 = (bf16[264,512]{1,0:T(8,128)(2,1)S(1)}, bf16[264,512]{1,0:T(8,128)(2,1)S(1)}, u32[]{:S(2)}, u32[]{:S(2)}) collective-permute-start(bf16[264,512]{1,0:T(8,128)(2,1)S(1)} %shard_map.80), channel_id=1, source_target_pairs={{480,0},{0,32},{32,64},{64,96},{96,128},{128,160},{160,192},{192,2... | collective-permute-start | bytes 811016 | tf_op jit(solution)/shard_map/ppermute | solution.py:38
  46.2 0.8 shard_map.78
  47.0 8.5 %collective-permute-done.5.a_10_ = bf16[264,512]{1,0:T(8,128)(2,1)S(1)} collective-permute-done((bf16[264,512]{1,0:T(8,128)(2,1)S(1)}, bf16[264,512]{1,0:T(8,128)(2,1)S(1)}, u32[]{:S(2)}, u32[]{:S(2)}) %collective-permute-start.5) | collective-permute-done | bytes 270368 | tf_op jit(solution)/shard_map/ppermute | solution.py:38
  55.6 1.4 %shard_map.81 = (f32[640,1024]{1,0:T(8,128)S(1)}, f32[1,1024]{1,0:T(1,128)S(1)}, bf16[1024,512]{1,0:T(8,128)(2,1)S(1)}, f32[1024,128]{1,0:T(8,128)S(1)}, bf16[51...) custom-call(bf16[1024,512]{1,0:T(8,128)(2,1)S(1)} %copy-done, f32[1,1024]{1,0:T(1,128)S(1)} %get-tuple-element.25.a_1_, ...), custom_call_target="tpu_custom_call" | custom-call | flops 671088640 | bytes 4194304 | tf_op jit(solution)/shard_map/pallas_call | solution.py:235
  57.0 2.0 %shard_map.82 = (f32[1024,1024]{1,0:T(8,128)S(1)}, f32[32,2,8,128]{3,2,1,0:T(8,128)S(1)}, f32[2,8,128]{2,1,0:T(8,128)S(1)}) custom-call(bf16[1032,512]{1,0:T(8,128)(2,1)S(1)} %collective-permute-done.6.a_0_, f32[1,1024]{1,0:T(1,128)S(1)} %bitcast.7, f32[1,1024]{1,0:T(1,128)S(1)} %get-tuple-element.29.a_2_, bf16[1024,512]{1,0:T(8,128)(2,1)S(1)} %get-tuple-element.30.a_3_, ...), custom_call_target="tpu_custom_call" | custom-call | flops 1073741824 | bytes 4194304 | tf_op jit(solution)/shard_map/pallas_call | solution.py:235
  59.1 14.9 %all_to_all.15.parts = f32[32,2,8,128]{3,2,1,0:T(8,128)S(1)} all-to-all(f32[32,2,8,128]{3,2,1,0:T(8,128)S(1)} %get-tuple-element.32), channel_id=1, replica_groups=mesh['z'=16,'yh'=2,'yl'=2,'x'=4,'c'=2] {'c','x','yh','yl'}, dimensions={0} | all-to-all | bytes 524288 | tf_op jit(solution)/shard_map/all_to_all | solution.py:472
  74.0 3.5 %cols.1 = (f32[1,2048]{1,0:T(1,128)S(1)}, f32[16,8,128]{2,1,0:T(8,128)S(1)}) custom-call(f32[32,2,8,128]{3,2,1,0:T(8,128)S(1)} %all_to_all.15.parts, f32[2,8,128]{2,1,0:T(8,128)S(1)} %get-tuple-element.33.logs, f32[384,1024]{1,0:T(8,128)S(1)} %get-tuple-element.34.s1, f32[640,1024]{1,0:T(8,128)S(1)} %get-tuple-element.35.s2, ...), custom_call_target="tpu_custom_call" | custom-call | tf_op jit(solution)/shard_map/cols/pallas_call | solution.py:308
  77.5 20.1 %all_to_all.16.parts = f32[16,8,128]{2,1,0:T(8,128)S(1)} all-to-all(f32[16,8,128]{2,1,0:T(8,128)S(1)} %get-tuple-element.37), channel_id=1, replica_groups=mesh['z'=16,'yh'=2,'yl'=2,'x'=4,'c'=2] {'z'}, dimensions={0} | all-to-all | bytes 131072 | tf_op jit(solution)/shard_map/all_to_all | solution.py:474
  97.6 2.3 %moved.1 = (f32[1,128]{1,0:T(1,128)S(1)}, bf16[264,2048]{1,0:T(8,128)(2,1)S(1)}, f32[1,2048]{1,0:T(1,128)S(1)}, bf16[1024,2048]{1,0:T(8,128)(2,1)S(1)}) custom-call(f32[16,8,128]{2,1,0:T(8,128)S(1)} %all_to_all.16.parts, f32[16,128]{1,0:T(8,128)S(1)} %get-tuple-element.38.lt, f32[1,2048]{1,0:T(1,128)S(1)} %get-tuple-element.39.sp, ...), custom_call_target="tpu_custom_call" | custom-call | tf_op jit(solution)/shard_map/moved/pallas_call | solution.py:357
  99.9 3.9 %collective-permute-start.7 = (bf16[264,2048]{1,0:T(8,128)(2,1)S(1)}, bf16[264,2048]{1,0:T(8,128)(2,1)S(1)}, u32[]{:S(2)}, u32[]{:S(2)}) collective-permute-start(bf16[264,2048]{1,0:T(8,128)(2,1)S(1)} %get-tuple-element.41), channel_id=1, source_target_pairs={{0,1},{1,0},{2,3},{3,2},{4,5},{5,4},{6,7},{7,6},{8,9},{9,8},{10,11... | collective-permute-start | bytes 3244040 | tf_op jit(solution)/shard_map/ppermute | solution.py:476
  103.9 1.3 mine.1
  105.1 1.0 collective-permute-done.7.theirs
  106.4 20.2 %all_to_all.17.parts = bf16[16,272,128]{2,1,0:T(8,128)(2,1)S(1)} all-to-all(bf16[16,272,128]{2,1,0:T(8,128)(2,1)S(1)} %pack.1), channel_id=1, replica_groups=mesh['z'=16,'yh'=2,'yl'=2,'x'=4,'c'=2] {'x','yh','yl'}, dimensions={0} | all-to-all | bytes 2228224 | tf_op jit(solution)/shard_map/all_to_all | solution.py:478
  (13 shorter events, 2.1 us)
Async XLA Ops:
  1.9 44.3 %copy-start = (bf16[1024,512]{1,0:T(8,128)(2,1)S(1)}, bf16[1024,512]{1,0:T(8,128)(2,1)}, u32[]{:S(2)}) copy-start(bf16[1024,512]{1,0:T(8,128)(2,1)} %sources.1) | copy-start | bytes 3145732
  1.9 55.1 %collective-permute-start.6 = (bf16[1032,512]{1,0:T(8,128)(2,1)S(1)}, bf16[1032,512]{1,0:T(8,128)(2,1)S(1)}, u32[]{:S(2)}, u32[]{:S(2)}) collective-permute-start(bf16[1032,512]{1,0:T(8,128)(2,1)S(1)} %near_message.1), channel_id=1, source_target_pairs={{0,24},{24,0},{8,16},{16,8},{1,25},{25,1},{9,17},{17,9},{2,26},{26... | collective-permute-start | bytes 3170312 | tf_op jit(solution)/shard_map/ppermute | solution.py:466
  8.4 16.0 %collective-permute-start = (bf16[72,512]{1,0:T(8,128)(2,1)S(1)}, bf16[72,512]{1,0:T(8,128)(2,1)S(1)}, u32[]{:S(2)}, u32[]{:S(2)}) collective-permute-start(bf16[72,512]{1,0:T(8,128)(2,1)S(1)} %own.1.refs_0_.a_1_.a_4_), channel_id=1, source_target_pairs={{128,0},{160,32},{192,64},{224,96},{256,128},{288,160},{320,192},{... | collective-permute-start | bytes 221192 | tf_op jit(solution)/shard_map/ppermute | solution.py:38
  20.9 13.6 %collective-permute-start.1 = (bf16[72,512]{1,0:T(8,128)(2,1)S(1)}, bf16[72,512]{1,0:T(8,128)(2,1)S(1)}, u32[]{:S(2)}, u32[]{:S(2)}) collective-permute-start(bf16[72,512]{1,0:T(8,128)(2,1)S(1)} %own.1.refs_0_.a_1_.a_4_), channel_id=1, source_target_pairs={{352,0},{384,32},{416,64},{448,96},{480,128},{0,160},{32,192},{64,... | collective-permute-start | bytes 221192 | tf_op jit(solution)/shard_map/ppermute | solution.py:38
  24.5 12.7 %collective-permute-start.2 = (bf16[136,512]{1,0:T(8,128)(2,1)S(1)}, bf16[136,512]{1,0:T(8,128)(2,1)S(1)}, u32[]{:S(2)}, u32[]{:S(2)}) collective-permute-start(bf16[136,512]{1,0:T(8,128)(2,1)S(1)} %shard_map.76), channel_id=1, source_target_pairs={{64,0},{96,32},{128,64},{160,96},{192,128},{224,160},{256,192},{28... | collective-permute-start | bytes 417800 | tf_op jit(solution)/shard_map/ppermute | solution.py:38
  34.6 8.7 %collective-permute-start.3 = (bf16[136,512]{1,0:T(8,128)(2,1)S(1)}, bf16[136,512]{1,0:T(8,128)(2,1)S(1)}, u32[]{:S(2)}, u32[]{:S(2)}) collective-permute-start(bf16[136,512]{1,0:T(8,128)(2,1)S(1)} %shard_map.77), channel_id=1, source_target_pairs={{448,0},{480,32},{0,64},{32,96},{64,128},{96,160},{128,192},{160,2... | collective-permute-start | bytes 417800 | tf_op jit(solution)/shard_map/ppermute | solution.py:38
  37.3 18.3 %collective-permute-start.4 = (bf16[328,512]{1,0:T(8,128)(2,1)S(1)}, bf16[328,512]{1,0:T(8,128)(2,1)S(1)}, u32[]{:S(2)}, u32[]{:S(2)}) collective-permute-start(bf16[328,512]{1,0:T(8,128)(2,1)S(1)} %shard_map.79), channel_id=1, source_target_pairs={{32,0},{64,32},{96,64},{128,96},{160,128},{192,160},{224,192},{256... | collective-permute-start | bytes 1007624 | tf_op jit(solution)/shard_map/ppermute | solution.py:38
  43.4 12.2 %collective-permute-start.5 = (bf16[264,512]{1,0:T(8,128)(2,1)S(1)}, bf16[264,512]{1,0:T(8,128)(2,1)S(1)}, u32[]{:S(2)}, u32[]{:S(2)}) collective-permute-start(bf16[264,512]{1,0:T(8,128)(2,1)S(1)} %shard_map.80), channel_id=1, source_target_pairs={{480,0},{0,32},{32,64},{64,96},{96,128},{128,160},{160,192},{192,2... | collective-permute-start | bytes 811016 | tf_op jit(solution)/shard_map/ppermute | solution.py:38
  55.6 1.5 %copy-start.1 = (f32[1024]{0:T(1024)S(1)}, f32[1024]{0:T(1024)}, u32[]{:S(2)}) copy-start(f32[1024]{0:T(1024)} %param.6) | copy-start | bytes 12292
  99.9 6.3 %collective-permute-start.7 = (bf16[264,2048]{1,0:T(8,128)(2,1)S(1)}, bf16[264,2048]{1,0:T(8,128)(2,1)S(1)}, u32[]{:S(2)}, u32[]{:S(2)}) collective-permute-start(bf16[264,2048]{1,0:T(8,128)(2,1)S(1)} %get-tuple-element.41), channel_id=1, source_target_pairs={{0,1},{1,0},{2,3},{3,2},{4,5},{5,4},{6,7},{7,6},{8,9},{9,8},{10,11... | collective-permute-start | bytes 3244040 | tf_op jit(solution)/shard_map/ppermute | solution.py:476

commit v6 on v5

--- a/solution.py
+++ b/solution.py
@@ -18,12 +18,12 @@
 LN2 = math.log(2.0)
 B = 64
 A8 = 8
-OFF1 = (0, 4, 11, 2, 6, 9)
-OFF2 = (14, 1, 3, 7, 5, 12, 15, 8, 13, 10)
+OFF1 = (0, 4, 11, 2, 6, 9, 14, 1, 5, 12, 15, 10)
+OFF2 = (3, 7, 8, 13)
 OFF = OFF1 + OFF2
-PICKS = ((0, 0), (1, 0), (2, 0), (3, 0), (3, 1), (4, 0), (4, 1)) + tuple((5, k) for k in range(5)) + tuple((6, k) for k in range(4))
-PICKS1 = PICKS[:6]
-PICKS2 = PICKS[6:]
+PICKS = tuple((m, k) for m, count in enumerate((1, 1, 1, 2, 2, 3, 2, 2, 2)) for k in range(count))
+PICKS1 = PICKS[: len(OFF1)]
+PICKS2 = PICKS[len(OFF1) :]
 
 
 MIB = 1 << 20
@@ -78,33 +78,6 @@
     )(*[far(a) for a in (targets, potential.reshape(1, B), log_tgt.reshape(1, B))])
 
 
-def near_kernel(sources, log_src, out, log, sems):
-    copies = [
-        pltpu.make_async_copy(sources, out.at[0 : sources.shape[0]], sems.at[0]),
-        pltpu.make_async_copy(log_src, log, sems.at[1]),
-    ]
-    for copy in copies:
-        copy.start()
-    for copy in copies:
-        copy.wait()
-    f = out.shape[1]
-    rows = [part[:, h * f : (h + 1) * f] for part in split(log[...]) for h in range(2)]
-    out[sources.shape[0] :, :] = jnp.concatenate(rows + [jnp.zeros((2, f), jnp.float32)], axis=0).astype(out.dtype)
-
-
-def near_call(sources, log_src):
-    n, f = sources.shape
-    return pl.pallas_call(
-        near_kernel,
-        name="near_message",
-        in_specs=[FAR] * 2,
-        out_specs=WHOLE,
-        out_shape=jax.ShapeDtypeStruct((n + A8, f), sources.dtype),
-        scratch_shapes=[pltpu.VMEM((1, n), jnp.float32), pltpu.SemaphoreType.DMA((2,))],
-        compiler_params=params(4),
-    )(far(sources), far(log_src.reshape(1, n)))
-
-
 def joined(picks, msgs):
     def kernel(*refs):
         out = refs[-1]
@@ -175,55 +148,47 @@
         pot[p * B : (p + 1) * B, :] = jnp.broadcast_to(to_col(po), (B, 128))
 
 
-def own_first_kernel(scale2, src, *refs):
-    msgs, (s_out, lse_out, tg, pot) = refs[:-4], refs[-4:]
+def turned(tg, out, base):
+    core = lax.axis_index("c")
+    for q in range(tg.shape[0] // 128):
+        flipped = tg[q * 128 : (q + 1) * 128, :].T
+        for f in range(16):
+            to = pl.multiple_of((((f % 2) ^ core) * 8 + f // 2) * 32, 32)
+            out[pl.ds(to, 32), base + q * 128 : base + (q + 1) * 128] = flipped[f * 32 : (f + 1) * 32, :]
+
+
+def first_kernel(scale2, sources, near, *refs):
+    msgs, (s_out, lse_out, tgt_out, tg, pot) = refs[:-5], refs[-5:]
     laid_out(msgs, PICKS1, tg, pot)
-    for n in range(src.shape[0] // CH):
+    ns = sources.shape[0]
+    for n in range(2 * ns // CH):
         at = slice(n * CH, (n + 1) * CH)
-        s_out[:, at] = scores(tg[...], src[at, :], scale2)
+        ref, row = (sources, n * CH) if n * CH < ns else (near, n * CH - ns)
+        s_out[:, at] = scores(tg[...], ref[row : row + CH, :], scale2)
         lse_out[:, at] = row_lse(s_out, at, pot)
-
-
-def own_last_kernel(scale2, src, lse_in, tg1, pot1, *refs):
-    msgs, (s_out, lse_out, tgs, pots, tgt_out, lt_out, tg, pot) = refs[:-8], refs[-8:]
+    turned(tg, tgt_out, 0)
+
+
+def last_kernel(scale2, sources, near, lse_in, tgt_in, *refs):
+    msgs, (s_out, rows_out, tgt_out, lt_out, tg, pot) = refs[:-6], refs[-6:]
     laid_out(msgs, PICKS2, tg, pot)
-    for n in range(src.shape[0] // CH):
+    yh = lax.axis_index("yh")
+    ns = sources.shape[0]
+    for n in range(2 * ns // CH):
         at = slice(n * CH, (n + 1) * CH)
-        s_out[:, at] = scores(tg[...], src[at, :], scale2)
-        lse_out[:, at] = added_lse(lse_in[:, at], row_lse(s_out, at, pot))
-    t1 = tg1.shape[0]
-    tgs[:t1, :] = tg1[...]
-    tgs[t1:, :] = tg[...]
-    pots[:t1, :] = pot1[...]
-    pots[t1:, :] = pot[...]
-    core = lax.axis_index("c")
+        ref, row, block = (sources, n * CH, yh) if n * CH < ns else (near, n * CH - ns, 1 - yh)
+        s_out[:, at] = scores(tg[...], ref[row : row + CH, :], scale2)
+        lse = added_lse(lse_in[:, at], row_lse(s_out, at, pot))
+        for i in range(CH // 128):
+            piece = jnp.broadcast_to(lse[:, i * 128 : (i + 1) * 128][None], (rows_out.shape[0], 1, 128))
+            q = row // 128 + i
+            rows_out[:, block, q : q + 1, :] = piece
     for p, (m, k) in enumerate(PICKS):
         _, ex = block_of(msgs, m, k)
         lt_out[p : p + 1, 0:B] = (ex[3:4] + ex[4:5] + ex[5:6]) * LOG2E
-    for q in range(tgs.shape[0] // 128):
-        at = slice(q * 128, (q + 1) * 128)
-        flipped = (tg1[at, :] if q * 128 < t1 else tg[q * 128 - t1 : (q + 1) * 128 - t1, :]).T
-        for f in range(16):
-            to = pl.multiple_of((((f % 2) ^ core) * 8 + f // 2) * 32, 32)
-            tgt_out[pl.ds(to, 32), at] = flipped[f * 32 : (f + 1) * 32, :]
-
-
-def near_scores_kernel(scale2, near, log_src, lse_in, tgs, pots, s_out, rows_out, log_out):
-    yh = lax.axis_index("yh")
-    ns = near.shape[0] - A8
-    logs = near[ns:, :].astype(jnp.float32)
-    logs = logs[0:2] + logs[2:4] + logs[4:6]
-    for q in range(8):
-        log_out[0, q : q + 1, :] = log_src[:, q * 128 : (q + 1) * 128] * LOG2E
-        log_out[1, q : q + 1, :] = logs[q // 4 : q // 4 + 1, q % 4 * 128 : (q % 4 + 1) * 128] * LOG2E
-    for n in range(ns // CH):
-        at = slice(n * CH, (n + 1) * CH)
-        s_out[:, at] = scores(tgs[...], near[at, :], scale2)
-        for block, lse in ((yh, lse_in[:, at]), (1 - yh, row_lse(s_out, at, pots))):
-            for i in range(CH // 128):
-                piece = jnp.broadcast_to(lse[:, i * 128 : (i + 1) * 128][None], (rows_out.shape[0], 1, 128))
-                q = n * (CH // 128) + i
-                rows_out[:, block, q : q + 1, :] = piece
+    t1 = tgt_in.shape[1]
+    tgt_out[:, :t1] = tgt_in[...]
+    turned(tg, tgt_out, t1)
 
 
 def added_lse(a, b):
@@ -243,26 +208,21 @@
     )(*args)
 
 
-def all_scores(sources, log_src, near, msgs, scale2):
+def all_scores(sources, near, msgs, scale2):
     ns, f = sources.shape
     f32, bf = jnp.float32, jnp.bfloat16
     t1, t2 = len(PICKS1) * B, len(PICKS2) * B
-    t = t1 + t2
-    flops = lambda rows: 2 * rows * ns * f
-    s1, lse1, tg1, pot1 = scores_call(
-        own_first_kernel, scale2, [sources, *msgs[:5]],
-        [((t1, ns), f32), ((1, ns), f32), ((t1, f), bf), ((t1, 128), f32)], [], flops(t1),
+    s1, lse1, tgt1 = scores_call(
+        first_kernel, scale2, [sources, near, *msgs[:7]],
+        [((t1, 2 * ns), f32), ((1, 2 * ns), f32), ((f, t1), bf)],
+        [((t1, f), bf), ((t1, 128), f32)], 4 * t1 * ns * f,
     )
-    s2, lse2, tgs, pots, tgt, lt = scores_call(
-        own_last_kernel, scale2, [sources, lse1, tg1, pot1, *msgs],
-        [((t2, ns), f32), ((1, ns), f32), ((t, f), bf), ((t, 128), f32), ((f, t), bf), ((len(OFF), 128), f32)],
-        [((t2, f), bf), ((t2, 128), f32)], flops(t2),
+    s2, rows, tgt, lt = scores_call(
+        last_kernel, scale2, [sources, near, lse1, tgt1, *msgs],
+        [((t2, 2 * ns), f32), ((32, 2, ns // 128, 128), f32), ((f, t1 + t2), bf), ((len(OFF), 128), f32)],
+        [((t2, f), bf), ((t2, 128), f32)], 4 * t2 * ns * f,
     )
-    s3, rows, logs = scores_call(
-        near_scores_kernel, scale2, [near, log_src.reshape(1, ns), lse2, tgs, pots],
-        [((t, ns), f32), ((32, 2, ns // 128, 128), f32), ((2, ns // 128, 128), f32)], [], flops(t),
-    )
-    return (s1, s2, s3), rows, logs, tgt, lt
+    return (s1, s2), rows, tgt, lt
 
 
 def merged_lse(parts):
@@ -274,26 +234,23 @@
     return (lax.axis_index("z") + OFF[p]) % 16
 
 
-def cols_kernel(parts, logs, s1, s2, s3, sp_out, msg_out, held, lse):
+def cols_kernel(parts, log_own, log_near, s1, s2, sp_out, msg_out, held, lse):
     yh = lax.axis_index("yh")
     for h in range(2):
         lse[h] = merged_lse(parts[:, h])
     for h, block in enumerate((yh, 1 - yh)):
-        sp = logs[h] - lse[block]
+        sp = (log_near if h else log_own)[...] * LOG2E - lse[block]
         for r in range(8):
             sp_out[:, (h * 8 + r) * 128 : (h * 8 + r + 1) * 128] = sp[r : r + 1, :]
     held[...] = jnp.zeros_like(held)
-    ns = s1.shape[1]
     n1 = len(OFF1)
     for p in range(len(OFF)):
         s_ref, base = (s1, p * B) if p < n1 else (s2, (p - n1) * B)
         pieces = []
         for r in range(0, B, 8):
-            mine = s_ref[base + r : base + r + 8, :] + sp_out[:, :ns]
-            other = s3[p * B + r : p * B + r + 8, :] + sp_out[:, ns:]
-            top = jnp.max(jnp.maximum(mine, other), axis=1, keepdims=True)
-            total = jnp.sum(jnp.exp2(mine - top) + jnp.exp2(other - top), axis=1, keepdims=True)
-            pieces.append(top + jnp.log2(total))
+            lifted = s_ref[base + r : base + r + 8, :] + sp_out[...]
+            top = jnp.max(lifted, axis=1, keepdims=True)
+            pieces.append(top + jnp.log2(jnp.sum(jnp.exp2(lifted - top), axis=1, keepdims=True)))
         row = to_row(jnp.concatenate(pieces, axis=0))
         row = jnp.concatenate([row, row], axis=1)
         slot = slot_of(p)
@@ -303,7 +260,7 @@
     msg_out[...] = jnp.broadcast_to(held[...][None], msg_out.shape)
 
 
-def cols_call(parts, logs, s):
+def cols_call(parts, log_own, log_near, s):
     ns = s[0].shape[1]
     return pl.pallas_call(
         cols_kernel,
@@ -311,12 +268,12 @@
         in_specs=[WHOLE] * 5,
         out_specs=[WHOLE] * 2,
         scratch_shapes=[pltpu.VMEM((8, 128), jnp.float32), pltpu.VMEM((2, 8, 128), jnp.float32)],
-        out_shape=[jax.ShapeDtypeStruct((1, 2 * ns), jnp.float32), jax.ShapeDtypeStruct((16, 8, 128), jnp.float32)],
+        out_shape=[jax.ShapeDtypeStruct((1, ns), jnp.float32), jax.ShapeDtypeStruct((16, 8, 128), jnp.float32)],
         compiler_params=params(16),
-    )(parts, logs, *s)
-
-
-def moved_kernel(parts, lt, sp, s1, s2, s3, tgt, pot_out, theirs_out, mass_out, wide, tp, lse):
+    )(parts, log_own, log_near, *s)
+
+
+def moved_kernel(parts, lt, sp, s1, s2, tgt, pot_out, theirs_out, mass_out, wide, tp, lse):
     lse[...] = merged_lse(parts[...])
     for p in range(len(OFF)):
         slot = slot_of(p)
@@ -328,17 +285,13 @@
         tp[p * B : (p + 1) * B, :] = jnp.broadcast_to(to_col(tpot), (B, 128))
 
     t1 = s1.shape[0]
-    ns = s1.shape[1]
     half = tgt.shape[0] // 2
     for n in range(sp.shape[1] // CH):
         at = slice(n * CH, (n + 1) * CH)
         spn = sp[:, at]
         mass = jnp.zeros((8, CH), jnp.float32)
         for r in range(0, tp.shape[0], 32):
-            if n * CH < ns:
-                s = s1[r : r + 32, at] if r < t1 else s2[r - t1 : r - t1 + 32, at]
-            else:
-                s = s3[r : r + 32, n * CH - ns : (n + 1) * CH - ns]
+            s = s1[r : r + 32, at] if r < t1 else s2[r - t1 : r - t1 + 32, at]
             e = jnp.exp2(s + spn + jnp.concatenate([tp[r : r + 32, :]] * (CH // 128), axis=1))
             mass = mass + jnp.sum(e.reshape(4, 8, CH), axis=0)
             wide[r : r + 32, at] = e.astype(jnp.bfloat16)
@@ -357,7 +310,7 @@
     return pl.pallas_call(
         moved_kernel,
         name="moved",
-        in_specs=[WHOLE] * 7,
+        in_specs=[WHOLE] * 6,
         out_specs=[WHOLE] * 4,
         scratch_shapes=[pltpu.VMEM((t, 128), jnp.float32), pltpu.VMEM((8, 128), jnp.float32)],
         out_shape=[
@@ -460,17 +413,23 @@
     f = sources.shape[1]
     scale2 = LOG2E / math.sqrt(f)
 
+    other = [(0, 3), (3, 0), (1, 2), (2, 1)]
+    near = lax.ppermute(sources, ("yh", "yl"), other)
     own = own_call(targets, potential, log_tgt)
     ra = from_z(own, 4)
     la = from_z(own, -5)
-    near = lax.ppermute(near_call(sources, log_src), ("yh", "yl"), [(0, 3), (3, 0), (1, 2), (2, 1)])
     rb = from_z(joined([(0, 0), (1, 0)], [own, ra]), 2)
     lb = from_z(joined([(1, 0), (0, 0)], [own, la]), -2)
-    rc = from_z(joined([(0, 0), (1, 0), (1, 1), (2, 0), (3, 0)], [own, rb, ra, la]), 1)
-    lc = from_z(joined([(0, 0), (1, 0), (1, 1), (2, 0)], [own, lb, la]), -1)
-    s, rows, logs, tgt, lt = all_scores(sources, log_src, near, [own, ra, la, rb, lb, rc, lc], scale2)
+    rc1 = from_z(joined([(0, 0), (1, 0), (2, 0)], [own, ra, la]), 1)
+    lc1 = from_z(joined([(0, 0), (1, 0)], [own, la]), -1)
+    rc2 = from_z(rb, 1)
+    lc2 = from_z(lb, -1)
+    log_own = log_src.reshape(8, 128)
+    log_near = lax.ppermute(log_own, ("yh", "yl"), other)
+    s, rows, tgt, lt = all_scores(sources, near, [own, ra, la, rb, lb, rc1, lc1, rc2, lc2], scale2)
+    rows, log_near = lax.optimization_barrier((rows, log_near))
     row_parts = lax.all_to_all(rows, PLANE, split_axis=0, concat_axis=0, tiled=True)
-    sp, cols = cols_call(row_parts, logs, s)
+    sp, cols = cols_call(row_parts, log_own, log_near, s)
     col_parts = lax.all_to_all(cols, "z", split_axis=0, concat_axis=0, tiled=True)
     tpot, theirs, mass, wide = moved_call(col_parts, lt, sp, s, tgt)
     theirs = lax.ppermute(theirs, "c", [(0, 1), (1, 0)])

time: 128 us -> 131 us (1.023)
  starting transfers between devices: 38 us -> 53 us
  waiting for transfers between devices: 18.5 us -> 8.1 us
  Pallas kernels: 14.8 us -> 13.2 us
    ppermute x6 -> x8, starting transfers between devices: 28.5 us -> 41.5 us  [from_z(): return lax.ppermute(array, 'z', [((i + d) % n, i) for i in range(n)])]
    ppermute x6 -> x8, waiting for transfers between devices: 17.5 us -> 7.06 us  [from_z(): return lax.ppermute(array, 'z', [((i + d) % n, i) for i in range(n)])]
    ppermute x1 -> x2, starting transfers between devices: 5.59 us -> 7.51 us  [the longest x1 5.59 us: body(): near = lax.ppermute(sources, ('yh', 'yl'), other)]
    pallas_call x2 -> x1, Pallas kernels: 3.52 us -> 2.26 us  [moved_call(): pl.pallas_call(moved_kernel, name='moved', in_specs=[WHOLE] * 6, out_spec...]
    pallas_call x3 -> x2, Pallas kernels: 4.27 us -> 4.01 us  [scores_call(): pl.pallas_call(lambda *a: kernel(scale2, *a), in_specs=[WHOLE] * len(args...]
  transfers between devices with their start and end apart: 8 -> 11, of which waited for: 6 -> 4; matrix products, arithmetic and copies ran while one was open for 0% -> 0% of each run, Pallas kernels for 4% -> 5%
where the time goes in v6:
time: 131 us; the launch traced here: 130 us
  blocking collectives  55.3 us (42%)
  starting transfers between devices  53 us (40%)
  Pallas kernels  13.2 us (10%)
  waiting for transfers between devices  8.1 us (6%)
    ppermute x8, starting transfers between devices, from_z(): return lax.ppermute(array, 'z', [((i + d) % n, i) for i in range(n)])  41.5 us
    all_to_all x1, blocking collectives, body(): lax.all_to_all(packed, CHIPS, split_axis=0, concat_axis=0, tiled=True)  20.2 us
    all_to_all x1, blocking collectives, body(): lax.all_to_all(cols, 'z', split_axis=0, concat_axis=0, tiled=True)  19 us
    all_to_all x1, blocking collectives, body(): lax.all_to_all(rows, PLANE, split_axis=0, concat_axis=0, tiled=True)  16 us
    ppermute x8, waiting for transfers between devices, from_z(): return lax.ppermute(array, 'z', [((i + d) % n, i) for i in range(n)])  7.06 us
    ppermute x1, starting transfers between devices, body(): near = lax.ppermute(sources, ('yh', 'yl'), other)  5.59 us
    pallas_call x2, Pallas kernels, scores_call(): pl.pallas_call(lambda *a: kernel(scale2, *a), in_specs=[WHOLE] * len(args...  4.01 us
    ppermute x1, starting transfers between devices, body(): theirs = lax.ppermute(theirs, 'c', [(0, 1), (1, 0)])  3.94 us
  transfers between devices with their start and end apart: 11, of which 4 were waited for; matrix products, arithmetic and copies ran while one was open for 0% of the time, Pallas kernels for 5%

profile of v6, /device:TPU:1, one launch (start us, length us, event | category | flops | bytes accessed | tf_op | source)
XLA Modules:
  0.0 130.3 jit_solution(18260657204439726218)
XLA Ops:
  0.7 5.6 %collective-permute-start = (bf16[1024,512]{1,0:T(8,128)(2,1)}, bf16[1024,512]{1,0:T(8,128)(2,1)S(1)}, u32[]{:S(2)}, u32[]{:S(2)}) collective-permute-start(bf16[1024,512]{1,0:T(8,128)(2,1)} %a_0_.3), channel_id=1, source_target_pairs={{0,24},{24,0},{8,16},{16,8},{1,25},{25,1},{9,17},{17,9},{2,26},{26... | collective-permute-start | bytes 3145736 | tf_op jit(solution)/shard_map/ppermute | solution.py:417
  6.3 0.9 own.1.refs_0_.a_2_.a_4_
  7.1 10.2 %collective-permute-start.2 = (bf16[72,512]{1,0:T(8,128)(2,1)S(1)}, bf16[72,512]{1,0:T(8,128)(2,1)S(1)}, u32[]{:S(2)}, u32[]{:S(2)}) collective-permute-start(bf16[72,512]{1,0:T(8,128)(2,1)S(1)} %own.1.refs_0_.a_2_.a_4_), channel_id=1, source_target_pairs={{352,0},{384,32},{416,64},{448,96},{480,128},{0,160},{32,192},{64,... | collective-permute-start | bytes 221192 | tf_op jit(solution)/shard_map/ppermute | solution.py:38
  17.3 4.2 %collective-permute-start.1 = (bf16[72,512]{1,0:T(8,128)(2,1)S(1)}, bf16[72,512]{1,0:T(8,128)(2,1)S(1)}, u32[]{:S(2)}, u32[]{:S(2)}) collective-permute-start(bf16[72,512]{1,0:T(8,128)(2,1)S(1)} %own.1.refs_0_.a_2_.a_4_), channel_id=1, source_target_pairs={{128,0},{160,32},{192,64},{224,96},{256,128},{288,160},{320,192},{... | collective-permute-start | bytes 221192 | tf_op jit(solution)/shard_map/ppermute | solution.py:38
  21.5 1.7 %collective-permute-done.2.refs_1_.refs_2_.a_4_.a_6_ = bf16[72,512]{1,0:T(8,128)(2,1)S(1)} collective-permute-done((bf16[72,512]{1,0:T(8,128)(2,1)S(1)}, bf16[72,512]{1,0:T(8,128)(2,1)S(1)}, u32[]{:S(2)}, u32[]{:S(2)}) %collective-permute-start.2) | collective-permute-done | bytes 73760 | tf_op jit(solution)/shard_map/ppermute | solution.py:38
  23.2 4.1 %collective-permute-done.1.refs_1_.a_3_.a_5_ = bf16[72,512]{1,0:T(8,128)(2,1)S(1)} collective-permute-done((bf16[72,512]{1,0:T(8,128)(2,1)S(1)}, bf16[72,512]{1,0:T(8,128)(2,1)S(1)}, u32[]{:S(2)}, u32[]{:S(2)}) %collective-permute-start.1) | collective-permute-done | bytes 73760 | tf_op jit(solution)/shard_map/ppermute | solution.py:38
  27.4 8.6 %collective-permute-start.5 = (bf16[200,512]{1,0:T(8,128)(2,1)S(1)}, bf16[200,512]{1,0:T(8,128)(2,1)S(1)}, u32[]{:S(2)}, u32[]{:S(2)}) collective-permute-start(bf16[200,512]{1,0:T(8,128)(2,1)S(1)} %shard_map.78), channel_id=1, source_target_pairs={{32,0},{64,32},{96,64},{128,96},{160,128},{192,160},{224,192},{256... | collective-permute-start | bytes 614408 | tf_op jit(solution)/shard_map/ppermute | solution.py:38
  36.1 1.9 %collective-permute-start.4 = (bf16[136,512]{1,0:T(8,128)(2,1)S(1)}, bf16[136,512]{1,0:T(8,128)(2,1)S(1)}, u32[]{:S(2)}, u32[]{:S(2)}) collective-permute-start(bf16[136,512]{1,0:T(8,128)(2,1)S(1)} %shard_map.77), channel_id=1, source_target_pairs={{448,0},{480,32},{0,64},{32,96},{64,128},{96,160},{128,192},{160,2... | collective-permute-start | bytes 417800 | tf_op jit(solution)/shard_map/ppermute | solution.py:38
  38.1 4.7 %collective-permute-start.6 = (bf16[136,512]{1,0:T(8,128)(2,1)S(1)}, bf16[136,512]{1,0:T(8,128)(2,1)S(1)}, u32[]{:S(2)}, u32[]{:S(2)}) collective-permute-start(bf16[136,512]{1,0:T(8,128)(2,1)S(1)} %shard_map.79), channel_id=1, source_target_pairs={{480,0},{0,32},{32,64},{64,96},{96,128},{128,160},{160,192},{192,2... | collective-permute-start | bytes 417800 | tf_op jit(solution)/shard_map/ppermute | solution.py:38
  42.9 2.6 %collective-permute-start.3 = (bf16[136,512]{1,0:T(8,128)(2,1)S(1)}, bf16[136,512]{1,0:T(8,128)(2,1)S(1)}, u32[]{:S(2)}, u32[]{:S(2)}) collective-permute-start(bf16[136,512]{1,0:T(8,128)(2,1)S(1)} %shard_map.76), channel_id=1, source_target_pairs={{64,0},{96,32},{128,64},{160,96},{192,128},{224,160},{256,192},{28... | collective-permute-start | bytes 417800 | tf_op jit(solution)/shard_map/ppermute | solution.py:38
  45.6 1.9 %collective-permute-start.9 = (f32[8,128]{1,0:T(8,128)S(1)}, f32[8,128]{1,0:T(8,128)S(1)}, u32[]{:S(2)}, u32[]{:S(2)}) collective-permute-start(f32[8,128]{1,0:T(8,128)S(1)} %bitcast.6), channel_id=1, source_target_pairs={{0,24},{24,0},{8,16},{16,8},{1,25},{25,1},{9,17},{17,9},{2,26},{26... | collective-permute-start | bytes 12296 | tf_op jit(solution)/shard_map/ppermute | solution.py:428
  47.5 1.3 collective-permute-done.6.a_8_.a_10_
  48.8 2.6 %collective-permute-start.8 = (bf16[136,512]{1,0:T(8,128)(2,1)S(1)}, bf16[136,512]{1,0:T(8,128)(2,1)S(1)}, u32[]{:S(2)}, u32[]{:S(2)}) collective-permute-start(bf16[136,512]{1,0:T(8,128)(2,1)S(1)} %collective-permute-done.4.a_6_.a_8_), channel_id=1, source_target_pairs={{480,0},{0,32},{32,64},{64,96},{96,128},{128,160},{160,192},{192,2... | collective-permute-start | bytes 417800 | tf_op jit(solution)/shard_map/ppermute | solution.py:38
  51.4 6.6 %collective-permute-start.7 = (bf16[136,512]{1,0:T(8,128)(2,1)S(1)}, bf16[136,512]{1,0:T(8,128)(2,1)S(1)}, u32[]{:S(2)}, u32[]{:S(2)}) collective-permute-start(bf16[136,512]{1,0:T(8,128)(2,1)S(1)} %collective-permute-done.3.a_5_.a_7_), channel_id=1, source_target_pairs={{32,0},{64,32},{96,64},{128,96},{160,128},{192,160},{224,192},{256... | collective-permute-start | bytes 417800 | tf_op jit(solution)/shard_map/ppermute | solution.py:38
  58.1 2.9 %shard_map.80 = (f32[768,2048]{1,0:T(8,128)S(1)}, f32[1,2048]{1,0:T(1,128)S(1)}, bf16[512,768]{1,0:T(8,128)(2,1)S(1)}) custom-call(bf16[1024,512]{1,0:T(8,128)(2,1)S(1)} %copy-done, bf16[1024,512]{1,0:T(8,128)(2,1)S(1)} %collective-permute-done.a_1_, bf16[72,512]{1,0:T(8,128)(2,1)S(1)} %own.1.refs_0_.a_2_.a_4_, ...), custom_call_target="tpu_custom_call" | custom-call | flops 1610612736 | bytes 4194304 | tf_op jit(solution)/shard_map/pallas_call | solution.py:200
  60.9 1.1 shard_map.81
  62.1 16.0 %all_to_all.15.parts = f32[32,2,8,128]{3,2,1,0:T(8,128)S(1)} all-to-all(f32[32,2,8,128]{3,2,1,0:T(8,128)S(1)} %get-tuple-element.25), channel_id=1, replica_groups=mesh['z'=16,'yh'=2,'yl'=2,'x'=4,'c'=2] {'c','x','yh','yl'}, dimensions={0} | all-to-all | bytes 524288 | tf_op jit(solution)/shard_map/all_to_all | solution.py:431
  78.1 3.4 %cols.1 = (f32[1,2048]{1,0:T(1,128)S(1)}, f32[16,8,128]{2,1,0:T(8,128)S(1)}) custom-call(f32[32,2,8,128]{3,2,1,0:T(8,128)S(1)} %all_to_all.15.parts, f32[8,128]{1,0:T(8,128)S(1)} %bitcast.7, f32[8,128]{1,0:T(8,128)S(1)} %collective-permute-done.9.log_near, f32[768,2048]{1,0:T(8,128)S(1)} %get-tuple-element.27.s1, f32[256,2048]{1,0:T(8,128)S(1)} %get-tuple-element.28.s2), custom_call_target="tpu_custom_call" | custom-call | tf_op jit(solution)/shard_map/cols/pallas_call | solution.py:265
  81.5 19.0 %all_to_all.16.parts = f32[16,8,128]{2,1,0:T(8,128)S(1)} all-to-all(f32[16,8,128]{2,1,0:T(8,128)S(1)} %get-tuple-element.29), channel_id=1, replica_groups=mesh['z'=16,'yh'=2,'yl'=2,'x'=4,'c'=2] {'z'}, dimensions={0} | all-to-all | bytes 131072 | tf_op jit(solution)/shard_map/all_to_all | solution.py:433
  100.5 2.3 %moved.1 = (f32[1,128]{1,0:T(1,128)S(1)}, bf16[264,2048]{1,0:T(8,128)(2,1)S(1)}, f32[1,2048]{1,0:T(1,128)S(1)}, bf16[1024,2048]{1,0:T(8,128)(2,1)S(1)}) custom-call(f32[16,8,128]{2,1,0:T(8,128)S(1)} %all_to_all.16.parts, f32[16,128]{1,0:T(8,128)S(1)} %get-tuple-element.30.lt, f32[1,2048]{1,0:T(1,128)S(1)} %get-tuple-element.31.sp, ...), custom_call_target="tpu_custom_call" | custom-call | tf_op jit(solution)/shard_map/moved/pallas_call | solution.py:310
  102.8 3.9 %collective-permute-start.10 = (bf16[264,2048]{1,0:T(8,128)(2,1)S(1)}, bf16[264,2048]{1,0:T(8,128)(2,1)S(1)}, u32[]{:S(2)}, u32[]{:S(2)}) collective-permute-start(bf16[264,2048]{1,0:T(8,128)(2,1)S(1)} %get-tuple-element.33), channel_id=1, source_target_pairs={{0,1},{1,0},{2,3},{3,2},{4,5},{5,4},{6,7},{7,6},{8,9},{9,8},{10,11... | collective-permute-start | bytes 3244040 | tf_op jit(solution)/shard_map/ppermute | solution.py:435
  106.7 1.3 mine.1
  108.0 1.0 collective-permute-done.10.theirs
  109.3 20.2 %all_to_all.17.parts = bf16[16,272,128]{2,1,0:T(8,128)(2,1)S(1)} all-to-all(bf16[16,272,128]{2,1,0:T(8,128)(2,1)S(1)} %pack.1), channel_id=1, replica_groups=mesh['z'=16,'yh'=2,'yl'=2,'x'=4,'c'=2] {'x','yh','yl'}, dimensions={0} | all-to-all | bytes 2228224 | tf_op jit(solution)/shard_map/all_to_all | solution.py:437
  (17 shorter events, 1.4 us)
Async XLA Ops:
  0.6 57.4 %copy-start = (bf16[1024,512]{1,0:T(8,128)(2,1)S(1)}, bf16[1024,512]{1,0:T(8,128)(2,1)}, u32[]{:S(2)}) copy-start(bf16[1024,512]{1,0:T(8,128)(2,1)} %a_0_.3) | copy-start | bytes 3145732
  0.6 44.9 %copy-start.1 = (f32[1024]{0:T(1024)S(1)}, f32[1024]{0:T(1024)}, u32[]{:S(2)}) copy-start(f32[1024]{0:T(1024)} %param.6) | copy-start | bytes 12292
  0.7 57.4 %collective-permute-start = (bf16[1024,512]{1,0:T(8,128)(2,1)}, bf16[1024,512]{1,0:T(8,128)(2,1)S(1)}, u32[]{:S(2)}, u32[]{:S(2)}) collective-permute-start(bf16[1024,512]{1,0:T(8,128)(2,1)} %a_0_.3), channel_id=1, source_target_pairs={{0,24},{24,0},{8,16},{16,8},{1,25},{25,1},{9,17},{17,9},{2,26},{26... | collective-permute-start | bytes 3145736 | tf_op jit(solution)/shard_map/ppermute | solution.py:417
  7.1 16.1 %collective-permute-start.2 = (bf16[72,512]{1,0:T(8,128)(2,1)S(1)}, bf16[72,512]{1,0:T(8,128)(2,1)S(1)}, u32[]{:S(2)}, u32[]{:S(2)}) collective-permute-start(bf16[72,512]{1,0:T(8,128)(2,1)S(1)} %own.1.refs_0_.a_2_.a_4_), channel_id=1, source_target_pairs={{352,0},{384,32},{416,64},{448,96},{480,128},{0,160},{32,192},{64,... | collective-permute-start | bytes 221192 | tf_op jit(solution)/shard_map/ppermute | solution.py:38
  17.3 10.0 %collective-permute-start.1 = (bf16[72,512]{1,0:T(8,128)(2,1)S(1)}, bf16[72,512]{1,0:T(8,128)(2,1)S(1)}, u32[]{:S(2)}, u32[]{:S(2)}) collective-permute-start(bf16[72,512]{1,0:T(8,128)(2,1)S(1)} %own.1.refs_0_.a_2_.a_4_), channel_id=1, source_target_pairs={{128,0},{160,32},{192,64},{224,96},{256,128},{288,160},{320,192},{... | collective-permute-start | bytes 221192 | tf_op jit(solution)/shard_map/ppermute | solution.py:38
  27.4 30.6 %collective-permute-start.5 = (bf16[200,512]{1,0:T(8,128)(2,1)S(1)}, bf16[200,512]{1,0:T(8,128)(2,1)S(1)}, u32[]{:S(2)}, u32[]{:S(2)}) collective-permute-start(bf16[200,512]{1,0:T(8,128)(2,1)S(1)} %shard_map.78), channel_id=1, source_target_pairs={{32,0},{64,32},{96,64},{128,96},{160,128},{192,160},{224,192},{256... | collective-permute-start | bytes 614408 | tf_op jit(solution)/shard_map/ppermute | solution.py:38
  36.1 9.5 %collective-permute-start.4 = (bf16[136,512]{1,0:T(8,128)(2,1)S(1)}, bf16[136,512]{1,0:T(8,128)(2,1)S(1)}, u32[]{:S(2)}, u32[]{:S(2)}) collective-permute-start(bf16[136,512]{1,0:T(8,128)(2,1)S(1)} %shard_map.77), channel_id=1, source_target_pairs={{448,0},{480,32},{0,64},{32,96},{64,128},{96,160},{128,192},{160,2... | collective-permute-start | bytes 417800 | tf_op jit(solution)/shard_map/ppermute | solution.py:38
  38.1 10.7 %collective-permute-start.6 = (bf16[136,512]{1,0:T(8,128)(2,1)S(1)}, bf16[136,512]{1,0:T(8,128)(2,1)S(1)}, u32[]{:S(2)}, u32[]{:S(2)}) collective-permute-start(bf16[136,512]{1,0:T(8,128)(2,1)S(1)} %shard_map.79), channel_id=1, source_target_pairs={{480,0},{0,32},{32,64},{64,96},{96,128},{128,160},{160,192},{192,2... | collective-permute-start | bytes 417800 | tf_op jit(solution)/shard_map/ppermute | solution.py:38
  42.9 8.5 %collective-permute-start.3 = (bf16[136,512]{1,0:T(8,128)(2,1)S(1)}, bf16[136,512]{1,0:T(8,128)(2,1)S(1)}, u32[]{:S(2)}, u32[]{:S(2)}) collective-permute-start(bf16[136,512]{1,0:T(8,128)(2,1)S(1)} %shard_map.76), channel_id=1, source_target_pairs={{64,0},{96,32},{128,64},{160,96},{192,128},{224,160},{256,192},{28... | collective-permute-start | bytes 417800 | tf_op jit(solution)/shard_map/ppermute | solution.py:38
  45.6 16.5 %collective-permute-start.9 = (f32[8,128]{1,0:T(8,128)S(1)}, f32[8,128]{1,0:T(8,128)S(1)}, u32[]{:S(2)}, u32[]{:S(2)}) collective-permute-start(f32[8,128]{1,0:T(8,128)S(1)} %bitcast.6), channel_id=1, source_target_pairs={{0,24},{24,0},{8,16},{16,8},{1,25},{25,1},{9,17},{17,9},{2,26},{26... | collective-permute-start | bytes 12296 | tf_op jit(solution)/shard_map/ppermute | solution.py:428
  48.8 12.2 %collective-permute-start.8 = (bf16[136,512]{1,0:T(8,128)(2,1)S(1)}, bf16[136,512]{1,0:T(8,128)(2,1)S(1)}, u32[]{:S(2)}, u32[]{:S(2)}) collective-permute-start(bf16[136,512]{1,0:T(8,128)(2,1)S(1)} %collective-permute-done.4.a_6_.a_8_), channel_id=1, source_target_pairs={{480,0},{0,32},{32,64},{64,96},{96,128},{128,160},{160,192},{192,2... | collective-permute-start | bytes 417800 | tf_op jit(solution)/shard_map/ppermute | solution.py:38
  51.4 9.6 %collective-permute-start.7 = (bf16[136,512]{1,0:T(8,128)(2,1)S(1)}, bf16[136,512]{1,0:T(8,128)(2,1)S(1)}, u32[]{:S(2)}, u32[]{:S(2)}) collective-permute-start(bf16[136,512]{1,0:T(8,128)(2,1)S(1)} %collective-permute-done.3.a_5_.a_7_), channel_id=1, source_target_pairs={{32,0},{64,32},{96,64},{128,96},{160,128},{192,160},{224,192},{256... | collective-permute-start | bytes 417800 | tf_op jit(solution)/shard_map/ppermute | solution.py:38
  102.8 6.3 %collective-permute-start.10 = (bf16[264,2048]{1,0:T(8,128)(2,1)S(1)}, bf16[264,2048]{1,0:T(8,128)(2,1)S(1)}, u32[]{:S(2)}, u32[]{:S(2)}) collective-permute-start(bf16[264,2048]{1,0:T(8,128)(2,1)S(1)} %get-tuple-element.33), channel_id=1, source_target_pairs={{0,1},{1,0},{2,3},{3,2},{4,5},{5,4},{6,7},{7,6},{8,9},{9,8},{10,11... | collective-permute-start | bytes 3244040 | tf_op jit(solution)/shard_map/ppermute | solution.py:435

commit v7 on v6

--- a/solution.py
+++ b/solution.py
@@ -18,10 +18,10 @@
 LN2 = math.log(2.0)
 B = 64
 A8 = 8
-OFF1 = (0, 4, 11, 2, 6, 9, 14, 1, 5, 12, 15, 10)
-OFF2 = (3, 7, 8, 13)
+OFF1 = (0, 4, 11, 2, 6, 9, 14, 1, 3, 7, 5, 12)
+OFF2 = (15, 8, 13, 10)
 OFF = OFF1 + OFF2
-PICKS = tuple((m, k) for m, count in enumerate((1, 1, 1, 2, 2, 3, 2, 2, 2)) for k in range(count))
+PICKS = tuple((m, k) for m, count in enumerate((1, 1, 1, 2, 2, 5, 4)) for k in range(count))
 PICKS1 = PICKS[: len(OFF1)]
 PICKS2 = PICKS[len(OFF1) :]
 
@@ -78,6 +78,33 @@
     )(*[far(a) for a in (targets, potential.reshape(1, B), log_tgt.reshape(1, B))])
 
 
+def near_kernel(sources, log_src, out, log, sems):
+    copies = [
+        pltpu.make_async_copy(sources, out.at[0 : sources.shape[0]], sems.at[0]),
+        pltpu.make_async_copy(log_src, log, sems.at[1]),
+    ]
+    for copy in copies:
+        copy.start()
+    for copy in copies:
+        copy.wait()
+    f = out.shape[1]
+    rows = [part[:, h * f : (h + 1) * f] for part in split(log[...]) for h in range(2)]
+    out[sources.shape[0] :, :] = jnp.concatenate(rows + [jnp.zeros((2, f), jnp.float32)], axis=0).astype(out.dtype)
+
+
+def near_call(sources, log_src):
+    n, f = sources.shape
+    return pl.pallas_call(
+        near_kernel,
+        name="near_message",
+        in_specs=[FAR] * 2,
+        out_specs=WHOLE,
+        out_shape=jax.ShapeDtypeStruct((n + A8, f), sources.dtype),
+        scratch_shapes=[pltpu.VMEM((1, n), jnp.float32), pltpu.SemaphoreType.DMA((2,))],
+        compiler_params=params(4),
+    )(far(sources), far(log_src.reshape(1, n)))
+
+
 def joined(picks, msgs):
     def kernel(*refs):
         out = refs[-1]
@@ -157,28 +184,40 @@
             out[pl.ds(to, 32), base + q * 128 : base + (q + 1) * 128] = flipped[f * 32 : (f + 1) * 32, :]
 
 
-def first_kernel(scale2, sources, near, *refs):
+def own_kernel_first(scale2, sources, *refs):
     msgs, (s_out, lse_out, tgt_out, tg, pot) = refs[:-5], refs[-5:]
     laid_out(msgs, PICKS1, tg, pot)
-    ns = sources.shape[0]
-    for n in range(2 * ns // CH):
+    for n in range(sources.shape[0] // CH):
         at = slice(n * CH, (n + 1) * CH)
-        ref, row = (sources, n * CH) if n * CH < ns else (near, n * CH - ns)
-        s_out[:, at] = scores(tg[...], ref[row : row + CH, :], scale2)
+        s_out[:, at] = scores(tg[...], sources[at, :], scale2)
         lse_out[:, at] = row_lse(s_out, at, pot)
     turned(tg, tgt_out, 0)
 
 
-def last_kernel(scale2, sources, near, lse_in, tgt_in, *refs):
+def near_kernel_first(scale2, near, log_src, tg, pot, s_out, lse_out, log_out):
+    ns = near.shape[0] - A8
+    logs = near[ns:, :].astype(jnp.float32)
+    logs = logs[0:2] + logs[2:4] + logs[4:6]
+    for q in range(8):
+        log_out[0, q : q + 1, :] = log_src[:, q * 128 : (q + 1) * 128] * LOG2E
+        log_out[1, q : q + 1, :] = logs[q // 4 : q // 4 + 1, q % 4 * 128 : (q % 4 + 1) * 128] * LOG2E
+    for n in range(ns // CH):
+        at = slice(n * CH, (n + 1) * CH)
+        s_out[:, at] = scores(tg[...], near[at, :], scale2)
+        lse_out[:, at] = row_lse(s_out, at, pot)
+
+
+def last_kernel(scale2, sources, near, lse_own, lse_near, tgt_in, *refs):
     msgs, (s_out, rows_out, tgt_out, lt_out, tg, pot) = refs[:-6], refs[-6:]
     laid_out(msgs, PICKS2, tg, pot)
     yh = lax.axis_index("yh")
     ns = sources.shape[0]
     for n in range(2 * ns // CH):
         at = slice(n * CH, (n + 1) * CH)
-        ref, row, block = (sources, n * CH, yh) if n * CH < ns else (near, n * CH - ns, 1 - yh)
+        first = n * CH < ns
+        ref, lse_in, row, block = (sources, lse_own, n * CH, yh) if first else (near, lse_near, n * CH - ns, 1 - yh)
         s_out[:, at] = scores(tg[...], ref[row : row + CH, :], scale2)
-        lse = added_lse(lse_in[:, at], row_lse(s_out, at, pot))
+        lse = added_lse(lse_in[:, row : row + CH], row_lse(s_out, at, pot))
         for i in range(CH // 128):
             piece = jnp.broadcast_to(lse[:, i * 128 : (i + 1) * 128][None], (rows_out.shape[0], 1, 128))
             q = row // 128 + i
@@ -208,21 +247,24 @@
     )(*args)
 
 
-def all_scores(sources, near, msgs, scale2):
+def all_scores(sources, log_src, near, msgs, scale2):
     ns, f = sources.shape
     f32, bf = jnp.float32, jnp.bfloat16
     t1, t2 = len(PICKS1) * B, len(PICKS2) * B
-    s1, lse1, tgt1 = scores_call(
-        first_kernel, scale2, [sources, near, *msgs[:7]],
-        [((t1, 2 * ns), f32), ((1, 2 * ns), f32), ((f, t1), bf)],
-        [((t1, f), bf), ((t1, 128), f32)], 4 * t1 * ns * f,
+    s1, lse1, tgt1, tg, pot = scores_call(
+        own_kernel_first, scale2, [sources, *msgs[:6]],
+        [((t1, ns), f32), ((1, ns), f32), ((f, t1), bf), ((t1, f), bf), ((t1, 128), f32)], [], 2 * t1 * ns * f,
     )
-    s2, rows, tgt, lt = scores_call(
-        last_kernel, scale2, [sources, near, lse1, tgt1, *msgs],
+    s2, lse2, logs = scores_call(
+        near_kernel_first, scale2, [near, log_src.reshape(1, ns), tg, pot],
+        [((t1, ns), f32), ((1, ns), f32), ((2, ns // 128, 128), f32)], [], 2 * t1 * ns * f,
+    )
+    s3, rows, tgt, lt = scores_call(
+        last_kernel, scale2, [sources, near, lse1, lse2, tgt1, *msgs],
         [((t2, 2 * ns), f32), ((32, 2, ns // 128, 128), f32), ((f, t1 + t2), bf), ((len(OFF), 128), f32)],
         [((t2, f), bf), ((t2, 128), f32)], 4 * t2 * ns * f,
     )
-    return (s1, s2), rows, tgt, lt
+    return (s1, s2, s3), rows, logs, tgt, lt
 
 
 def merged_lse(parts):
@@ -234,24 +276,37 @@
     return (lax.axis_index("z") + OFF[p]) % 16
 
 
-def cols_kernel(parts, log_own, log_near, s1, s2, sp_out, msg_out, held, lse):
+def cols_kernel(parts, logs, s1, s2, s3, sp_out, msg_out, held, lse):
     yh = lax.axis_index("yh")
     for h in range(2):
         lse[h] = merged_lse(parts[:, h])
     for h, block in enumerate((yh, 1 - yh)):
-        sp = (log_near if h else log_own)[...] * LOG2E - lse[block]
+        sp = logs[h] - lse[block]
         for r in range(8):
             sp_out[:, (h * 8 + r) * 128 : (h * 8 + r + 1) * 128] = sp[r : r + 1, :]
     held[...] = jnp.zeros_like(held)
     n1 = len(OFF1)
+    ns = s1.shape[1]
     for p in range(len(OFF)):
-        s_ref, base = (s1, p * B) if p < n1 else (s2, (p - n1) * B)
-        pieces = []
+        tops, totals = [], []
         for r in range(0, B, 8):
-            lifted = s_ref[base + r : base + r + 8, :] + sp_out[...]
-            top = jnp.max(lifted, axis=1, keepdims=True)
-            pieces.append(top + jnp.log2(jnp.sum(jnp.exp2(lifted - top), axis=1, keepdims=True)))
-        row = to_row(jnp.concatenate(pieces, axis=0))
+            lifted = []
+            for k in range(2 * ns // 128):
+                ref, base, col = (s3, (p - n1) * B, k * 128)
+                if p < n1:
+                    ref, base, col = (s1, p * B, k * 128) if k * 128 < ns else (s2, p * B, k * 128 - ns)
+                lifted.append(ref[base + r : base + r + 8, col : col + 128] + sp_out[:, k * 128 : (k + 1) * 128])
+            top = lifted[0]
+            for v in lifted[1:]:
+                top = jnp.maximum(top, v)
+            total = jnp.exp2(lifted[0] - top)
+            for v in lifted[1:]:
+                total = total + jnp.exp2(v - top)
+            tops.append(top)
+            totals.append(total)
+        tops, totals = jnp.concatenate(tops, axis=0), jnp.concatenate(totals, axis=0)
+        top = jnp.max(tops, axis=1, keepdims=True)
+        row = to_row(top + jnp.log2(jnp.sum(totals * jnp.exp2(tops - top), axis=1, keepdims=True)))
         row = jnp.concatenate([row, row], axis=1)
         slot = slot_of(p)
         at = slot // 2
@@ -260,8 +315,8 @@
     msg_out[...] = jnp.broadcast_to(held[...][None], msg_out.shape)
 
 
-def cols_call(parts, log_own, log_near, s):
-    ns = s[0].shape[1]
+def cols_call(parts, logs, s):
+    ns = s[2].shape[1]
     return pl.pallas_call(
         cols_kernel,
         name="cols",
@@ -270,10 +325,10 @@
         scratch_shapes=[pltpu.VMEM((8, 128), jnp.float32), pltpu.VMEM((2, 8, 128), jnp.float32)],
         out_shape=[jax.ShapeDtypeStruct((1, ns), jnp.float32), jax.ShapeDtypeStruct((16, 8, 128), jnp.float32)],
         compiler_params=params(16),
-    )(parts, log_own, log_near, *s)
-
-
-def moved_kernel(parts, lt, sp, s1, s2, tgt, pot_out, theirs_out, mass_out, wide, tp, lse):
+    )(parts, logs, *s)
+
+
+def moved_kernel(parts, lt, sp, s1, s2, s3, tgt, pot_out, theirs_out, mass_out, wide, tp, lse):
     lse[...] = merged_lse(parts[...])
     for p in range(len(OFF)):
         slot = slot_of(p)
@@ -284,14 +339,19 @@
             pot_out[:, 0:B] = tpot * LN2
         tp[p * B : (p + 1) * B, :] = jnp.broadcast_to(to_col(tpot), (B, 128))
 
-    t1 = s1.shape[0]
+    t1, ns = s1.shape
     half = tgt.shape[0] // 2
     for n in range(sp.shape[1] // CH):
         at = slice(n * CH, (n + 1) * CH)
         spn = sp[:, at]
         mass = jnp.zeros((8, CH), jnp.float32)
         for r in range(0, tp.shape[0], 32):
-            s = s1[r : r + 32, at] if r < t1 else s2[r - t1 : r - t1 + 32, at]
+            if r >= t1:
+                s = s3[r - t1 : r - t1 + 32, at]
+            elif n * CH < ns:
+                s = s1[r : r + 32, at]
+            else:
+                s = s2[r : r + 32, n * CH - ns : (n + 1) * CH - ns]
             e = jnp.exp2(s + spn + jnp.concatenate([tp[r : r + 32, :]] * (CH // 128), axis=1))
             mass = mass + jnp.sum(e.reshape(4, 8, CH), axis=0)
             wide[r : r + 32, at] = e.astype(jnp.bfloat16)
@@ -310,7 +370,7 @@
     return pl.pallas_call(
         moved_kernel,
         name="moved",
-        in_specs=[WHOLE] * 6,
+        in_specs=[WHOLE] * 7,
         out_specs=[WHOLE] * 4,
         scratch_shapes=[pltpu.VMEM((t, 128), jnp.float32), pltpu.VMEM((8, 128), jnp.float32)],
         out_shape=[
@@ -413,23 +473,17 @@
     f = sources.shape[1]
     scale2 = LOG2E / math.sqrt(f)
 
-    other = [(0, 3), (3, 0), (1, 2), (2, 1)]
-    near = lax.ppermute(sources, ("yh", "yl"), other)
     own = own_call(targets, potential, log_tgt)
     ra = from_z(own, 4)
     la = from_z(own, -5)
+    near = lax.ppermute(near_call(sources, log_src), ("yh", "yl"), [(0, 3), (3, 0), (1, 2), (2, 1)])
     rb = from_z(joined([(0, 0), (1, 0)], [own, ra]), 2)
     lb = from_z(joined([(1, 0), (0, 0)], [own, la]), -2)
-    rc1 = from_z(joined([(0, 0), (1, 0), (2, 0)], [own, ra, la]), 1)
-    lc1 = from_z(joined([(0, 0), (1, 0)], [own, la]), -1)
-    rc2 = from_z(rb, 1)
-    lc2 = from_z(lb, -1)
-    log_own = log_src.reshape(8, 128)
-    log_near = lax.ppermute(log_own, ("yh", "yl"), other)
-    s, rows, tgt, lt = all_scores(sources, near, [own, ra, la, rb, lb, rc1, lc1, rc2, lc2], scale2)
-    rows, log_near = lax.optimization_barrier((rows, log_near))
+    rc = from_z(joined([(0, 0), (1, 0), (1, 1), (2, 0), (3, 0)], [own, rb, ra, la]), 1)
+    lc = from_z(joined([(0, 0), (1, 0), (1, 1), (2, 0)], [own, lb, la]), -1)
+    s, rows, logs, tgt, lt = all_scores(sources, log_src, near, [own, ra, la, rb, lb, rc, lc], scale2)
     row_parts = lax.all_to_all(rows, PLANE, split_axis=0, concat_axis=0, tiled=True)
-    sp, cols = cols_call(row_parts, log_own, log_near, s)
+    sp, cols = cols_call(row_parts, logs, s)
     col_parts = lax.all_to_all(cols, "z", split_axis=0, concat_axis=0, tiled=True)
     tpot, theirs, mass, wide = moved_call(col_parts, lt, sp, s, tgt)
     theirs = lax.ppermute(theirs, "c", [(0, 1), (1, 0)])

time: 131 us -> 136 us (1.038)
  waiting for transfers between devices: 8.1 us -> 27.9 us
  starting transfers between devices: 53 us -> 40.5 us
  blocking collectives: 55.3 us -> 53.2 us
    ppermute x8 -> x6, waiting for transfers between devices: 7.06 us -> 26.9 us  [from_z(): return lax.ppermute(array, 'z', [((i + d) % n, i) for i in range(n)])]
    ppermute x8 -> x6, starting transfers between devices: 41.5 us -> 30.9 us  [from_z(): return lax.ppermute(array, 'z', [((i + d) % n, i) for i in range(n)])]
    all_to_all x1, blocking collectives: 19 us -> 15.5 us  [body(): lax.all_to_all(cols, 'z', split_axis=0, concat_axis=0, tiled=True)]
    ppermute x2 -> x1, starting transfers between devices: 7.51 us -> 5.59 us  [body(): lax.ppermute(near_call(sources, log_src), ('yh', 'yl'), [(0, 3), (3, 0),...]
    all_to_all x1, blocking collectives: 16 us -> 17.5 us  [body(): lax.all_to_all(rows, PLANE, split_axis=0, concat_axis=0, tiled=True)]
    pallas_call x1 -> x2, Pallas kernels: 2.26 us -> 3.53 us  [the longest x1 2.26 us: moved_call(): pl.pallas_call(moved_kernel, name='moved', in_specs=[WHOLE] * 7, out_spec...]
    pallas_call x2 -> x3, Pallas kernels: 4.01 us -> 4.31 us  [scores_call(): pl.pallas_call(lambda *a: kernel(scale2, *a), in_specs=[WHOLE] * len(args...]
  transfers between devices with their start and end apart: 11 -> 8, of which waited for: 4 -> 5; matrix products, arithmetic and copies ran while one was open for 0% -> 0% of each run, Pallas kernels for 5% -> 4%
where the time goes in v7:
time: 136 us
  blocking collectives  53.2 us (39%)
  starting transfers between devices  40.5 us (30%)
  waiting for transfers between devices  27.9 us (21%)
  Pallas kernels  13.5 us (10%)
    ppermute x6, starting transfers between devices, from_z(): return lax.ppermute(array, 'z', [((i + d) % n, i) for i in range(n)])  30.9 us
    ppermute x6, waiting for transfers between devices, from_z(): return lax.ppermute(array, 'z', [((i + d) % n, i) for i in range(n)])  26.9 us
    all_to_all x1, blocking collectives, body(): lax.all_to_all(packed, CHIPS, split_axis=0, concat_axis=0, tiled=True)  20.2 us
    all_to_all x1, blocking collectives, body(): lax.all_to_all(rows, PLANE, split_axis=0, concat_axis=0, tiled=True)  17.5 us
    all_to_all x1, blocking collectives, body(): lax.all_to_all(cols, 'z', split_axis=0, concat_axis=0, tiled=True)  15.5 us
    ppermute x1, starting transfers between devices, body(): lax.ppermute(near_call(sources, log_src), ('yh', 'yl'), [(0, 3), (3, 0),...  5.59 us
    pallas_call x3, Pallas kernels, scores_call(): pl.pallas_call(lambda *a: kernel(scale2, *a), in_specs=[WHOLE] * len(args...  4.31 us
    ppermute x1, starting transfers between devices, body(): theirs = lax.ppermute(theirs, 'c', [(0, 1), (1, 0)])  3.94 us
  transfers between devices with their start and end apart: 8, of which 5 were waited for; matrix products, arithmetic and copies ran while one was open for 0% of the time, Pallas kernels for 4%

profile of v7, /device:TPU:1, one launch (start us, length us, event | category | flops | bytes accessed | tf_op | source)
XLA Modules:
  0.0 135.9 jit_solution(12873763282991601187)
XLA Ops:
  0.6 1.3 near_message.1
  1.9 5.6 %collective-permute-start = (bf16[1032,512]{1,0:T(8,128)(2,1)S(1)}, bf16[1032,512]{1,0:T(8,128)(2,1)S(1)}, u32[]{:S(2)}, u32[]{:S(2)}) collective-permute-start(bf16[1032,512]{1,0:T(8,128)(2,1)S(1)} %near_message.1), channel_id=1, source_target_pairs={{0,24},{24,0},{8,16},{16,8},{1,25},{25,1},{9,17},{17,9},{2,26},{26... | collective-permute-start | bytes 3170312 | tf_op jit(solution)/shard_map/ppermute | solution.py:479
  7.5 0.9 own.1.refs_0_.a_1_.a_5_
  8.4 12.5 %collective-permute-start.1 = (bf16[72,512]{1,0:T(8,128)(2,1)S(1)}, bf16[72,512]{1,0:T(8,128)(2,1)S(1)}, u32[]{:S(2)}, u32[]{:S(2)}) collective-permute-start(bf16[72,512]{1,0:T(8,128)(2,1)S(1)} %own.1.refs_0_.a_1_.a_5_), channel_id=1, source_target_pairs={{128,0},{160,32},{192,64},{224,96},{256,128},{288,160},{320,192},{... | collective-permute-start | bytes 221192 | tf_op jit(solution)/shard_map/ppermute | solution.py:38
  20.9 3.5 %collective-permute-done.1.refs_1_.refs_2_.a_2_.a_6_ = bf16[72,512]{1,0:T(8,128)(2,1)S(1)} collective-permute-done((bf16[72,512]{1,0:T(8,128)(2,1)S(1)}, bf16[72,512]{1,0:T(8,128)(2,1)S(1)}, u32[]{:S(2)}, u32[]{:S(2)}) %collective-permute-start.1) | collective-permute-done | bytes 73760 | tf_op jit(solution)/shard_map/ppermute | solution.py:38
  24.5 7.4 %collective-permute-start.3 = (bf16[136,512]{1,0:T(8,128)(2,1)S(1)}, bf16[136,512]{1,0:T(8,128)(2,1)S(1)}, u32[]{:S(2)}, u32[]{:S(2)}) collective-permute-start(bf16[136,512]{1,0:T(8,128)(2,1)S(1)} %shard_map.76), channel_id=1, source_target_pairs={{64,0},{96,32},{128,64},{160,96},{192,128},{224,160},{256,192},{28... | collective-permute-start | bytes 417800 | tf_op jit(solution)/shard_map/ppermute | solution.py:38
  31.9 1.9 %collective-permute-start.2 = (bf16[72,512]{1,0:T(8,128)(2,1)S(1)}, bf16[72,512]{1,0:T(8,128)(2,1)S(1)}, u32[]{:S(2)}, u32[]{:S(2)}) collective-permute-start(bf16[72,512]{1,0:T(8,128)(2,1)S(1)} %own.1.refs_0_.a_1_.a_5_), channel_id=1, source_target_pairs={{352,0},{384,32},{416,64},{448,96},{480,128},{0,160},{32,192},{64,... | collective-permute-start | bytes 221192 | tf_op jit(solution)/shard_map/ppermute | solution.py:38
  33.8 12.9 %collective-permute-done.2.refs_1_.refs_3_.a_3_.refs_2_.a_7_ = bf16[72,512]{1,0:T(8,128)(2,1)S(1)} collective-permute-done((bf16[72,512]{1,0:T(8,128)(2,1)S(1)}, bf16[72,512]{1,0:T(8,128)(2,1)S(1)}, u32[]{:S(2)}, u32[]{:S(2)}) %collective-permute-start.2) | collective-permute-done | bytes 73760 | tf_op jit(solution)/shard_map/ppermute | solution.py:38
  46.9 1.9 %collective-permute-start.5 = (bf16[328,512]{1,0:T(8,128)(2,1)S(1)}, bf16[328,512]{1,0:T(8,128)(2,1)S(1)}, u32[]{:S(2)}, u32[]{:S(2)}) collective-permute-start(bf16[328,512]{1,0:T(8,128)(2,1)S(1)} %shard_map.78), channel_id=1, source_target_pairs={{32,0},{64,32},{96,64},{128,96},{160,128},{192,160},{224,192},{256... | collective-permute-start | bytes 1007624 | tf_op jit(solution)/shard_map/ppermute | solution.py:38
  48.9 1.9 %collective-permute-start.4 = (bf16[136,512]{1,0:T(8,128)(2,1)S(1)}, bf16[136,512]{1,0:T(8,128)(2,1)S(1)}, u32[]{:S(2)}, u32[]{:S(2)}) collective-permute-start(bf16[136,512]{1,0:T(8,128)(2,1)S(1)} %shard_map.77), channel_id=1, source_target_pairs={{448,0},{480,32},{0,64},{32,96},{64,128},{96,160},{128,192},{160,2... | collective-permute-start | bytes 417800 | tf_op jit(solution)/shard_map/ppermute | solution.py:38
  50.8 6.2 %collective-permute-done.4.a_5_.refs_1_.a_9_ = bf16[136,512]{1,0:T(8,128)(2,1)S(1)} collective-permute-done((bf16[136,512]{1,0:T(8,128)(2,1)S(1)}, bf16[136,512]{1,0:T(8,128)(2,1)S(1)}, u32[]{:S(2)}, u32[]{:S(2)}) %collective-permute-start.4) | collective-permute-done | bytes 139296 | tf_op jit(solution)/shard_map/ppermute | solution.py:38
  57.1 5.3 %collective-permute-start.6 = (bf16[264,512]{1,0:T(8,128)(2,1)S(1)}, bf16[264,512]{1,0:T(8,128)(2,1)S(1)}, u32[]{:S(2)}, u32[]{:S(2)}) collective-permute-start(bf16[264,512]{1,0:T(8,128)(2,1)S(1)} %shard_map.81), channel_id=1, source_target_pairs={{480,0},{0,32},{32,64},{64,96},{96,128},{128,160},{160,192},{192,2... | collective-permute-start | bytes 811016 | tf_op jit(solution)/shard_map/ppermute | solution.py:38
  62.5 1.6 %shard_map.79 = (f32[768,1024]{1,0:T(8,128)S(1)}, f32[1,1024]{1,0:T(1,128)S(1)}, bf16[512,768]{1,0:T(8,128)(2,1)S(1)}, bf16[768,512]{1,0:T(8,128)(2,1)S(1)}, f32[768,128]{1,0:T(8,128)S(1)}) custom-call(bf16[1024,512]{1,0:T(8,128)(2,1)S(1)} %copy-done, bf16[72,512]{1,0:T(8,128)(2,1)S(1)} %own.1.refs_0_.a_1_.a_5_, ...), custom_call_target="tpu_custom_call" | custom-call | flops 805306368 | bytes 4194304 | tf_op jit(solution)/shard_map/pallas_call | solution.py:239
  64.1 1.6 %shard_map.80 = (f32[768,1024]{1,0:T(8,128)S(1)}, f32[1,1024]{1,0:T(1,128)S(1)}, f32[2,8,128]{2,1,0:T(8,128)S(1)}) custom-call(bf16[1032,512]{1,0:T(8,128)(2,1)S(1)} %collective-permute-done.a_0_.a_1_, f32[1,1024]{1,0:T(1,128)S(1)} %bitcast.7, bf16[768,512]{1,0:T(8,128)(2,1)S(1)} %get-tuple-element.25.a_2_, f32[768,128]{1,0:T(8,128)S(1)} %get-tuple-element.26.a_3_), custom_call_target="tpu_custom_call" | custom-call | flops 805306368 | bytes 4194304 | tf_op jit(solution)/shard_map/pallas_call | solution.py:239
  65.7 4.2 %collective-permute-done.6.a_11_ = bf16[264,512]{1,0:T(8,128)(2,1)S(1)} collective-permute-done((bf16[264,512]{1,0:T(8,128)(2,1)S(1)}, bf16[264,512]{1,0:T(8,128)(2,1)S(1)}, u32[]{:S(2)}, u32[]{:S(2)}) %collective-permute-start.6) | collective-permute-done | bytes 270368 | tf_op jit(solution)/shard_map/ppermute | solution.py:38
  69.8 1.1 shard_map.82
  70.9 17.5 %all_to_all.15.parts = f32[32,2,8,128]{3,2,1,0:T(8,128)S(1)} all-to-all(f32[32,2,8,128]{3,2,1,0:T(8,128)S(1)} %get-tuple-element.30), channel_id=1, replica_groups=mesh['z'=16,'yh'=2,'yl'=2,'x'=4,'c'=2] {'c','x','yh','yl'}, dimensions={0} | all-to-all | bytes 524288 | tf_op jit(solution)/shard_map/all_to_all | solution.py:485
  88.4 2.2 %cols.1 = (f32[1,2048]{1,0:T(1,128)S(1)}, f32[16,8,128]{2,1,0:T(8,128)S(1)}) custom-call(f32[32,2,8,128]{3,2,1,0:T(8,128)S(1)} %all_to_all.15.parts, f32[2,8,128]{2,1,0:T(8,128)S(1)} %get-tuple-element.31.logs, f32[768,1024]{1,0:T(8,128)S(1)} %get-tuple-element.32.s1, f32[768,1024]{1,0:T(8,128)S(1)} %get-tuple-element.33.s2, ...), custom_call_target="tpu_custom_call" | custom-call | tf_op jit(solution)/shard_map/cols/pallas_call | solution.py:320
  90.6 15.5 %all_to_all.16.parts = f32[16,8,128]{2,1,0:T(8,128)S(1)} all-to-all(f32[16,8,128]{2,1,0:T(8,128)S(1)} %get-tuple-element.35), channel_id=1, replica_groups=mesh['z'=16,'yh'=2,'yl'=2,'x'=4,'c'=2] {'z'}, dimensions={0} | all-to-all | bytes 131072 | tf_op jit(solution)/shard_map/all_to_all | solution.py:487
  106.1 2.3 %moved.1 = (f32[1,128]{1,0:T(1,128)S(1)}, bf16[264,2048]{1,0:T(8,128)(2,1)S(1)}, f32[1,2048]{1,0:T(1,128)S(1)}, bf16[1024,2048]{1,0:T(8,128)(2,1)S(1)}) custom-call(f32[16,8,128]{2,1,0:T(8,128)S(1)} %all_to_all.16.parts, f32[16,128]{1,0:T(8,128)S(1)} %get-tuple-element.36.lt, f32[1,2048]{1,0:T(1,128)S(1)} %get-tuple-element.37.sp, ...), custom_call_target="tpu_custom_call" | custom-call | tf_op jit(solution)/shard_map/moved/pallas_call | solution.py:370
  108.3 3.9 %collective-permute-start.7 = (bf16[264,2048]{1,0:T(8,128)(2,1)S(1)}, bf16[264,2048]{1,0:T(8,128)(2,1)S(1)}, u32[]{:S(2)}, u32[]{:S(2)}) collective-permute-start(bf16[264,2048]{1,0:T(8,128)(2,1)S(1)} %get-tuple-element.39), channel_id=1, source_target_pairs={{0,1},{1,0},{2,3},{3,2},{4,5},{5,4},{6,7},{7,6},{8,9},{9,8},{10,11... | collective-permute-start | bytes 3244040 | tf_op jit(solution)/shard_map/ppermute | solution.py:489
  112.3 1.3 mine.1
  113.5 1.0 collective-permute-done.7.theirs
  114.8 20.2 %all_to_all.17.parts = bf16[16,272,128]{2,1,0:T(8,128)(2,1)S(1)} all-to-all(bf16[16,272,128]{2,1,0:T(8,128)(2,1)S(1)} %pack.1), channel_id=1, replica_groups=mesh['z'=16,'yh'=2,'yl'=2,'x'=4,'c'=2] {'x','yh','yl'}, dimensions={0} | all-to-all | bytes 2228224 | tf_op jit(solution)/shard_map/all_to_all | solution.py:491
  (13 shorter events, 1.4 us)
Async XLA Ops:
  1.9 60.5 %copy-start = (bf16[1024,512]{1,0:T(8,128)(2,1)S(1)}, bf16[1024,512]{1,0:T(8,128)(2,1)}, u32[]{:S(2)}) copy-start(bf16[1024,512]{1,0:T(8,128)(2,1)} %a_0_.3) | copy-start | bytes 3145732
  1.9 62.1 %collective-permute-start = (bf16[1032,512]{1,0:T(8,128)(2,1)S(1)}, bf16[1032,512]{1,0:T(8,128)(2,1)S(1)}, u32[]{:S(2)}, u32[]{:S(2)}) collective-permute-start(bf16[1032,512]{1,0:T(8,128)(2,1)S(1)} %near_message.1), channel_id=1, source_target_pairs={{0,24},{24,0},{8,16},{16,8},{1,25},{25,1},{9,17},{17,9},{2,26},{26... | collective-permute-start | bytes 3170312 | tf_op jit(solution)/shard_map/ppermute | solution.py:479
  8.4 16.0 %collective-permute-start.1 = (bf16[72,512]{1,0:T(8,128)(2,1)S(1)}, bf16[72,512]{1,0:T(8,128)(2,1)S(1)}, u32[]{:S(2)}, u32[]{:S(2)}) collective-permute-start(bf16[72,512]{1,0:T(8,128)(2,1)S(1)} %own.1.refs_0_.a_1_.a_5_), channel_id=1, source_target_pairs={{128,0},{160,32},{192,64},{224,96},{256,128},{288,160},{320,192},{... | collective-permute-start | bytes 221192 | tf_op jit(solution)/shard_map/ppermute | solution.py:38
  24.5 22.3 %collective-permute-start.3 = (bf16[136,512]{1,0:T(8,128)(2,1)S(1)}, bf16[136,512]{1,0:T(8,128)(2,1)S(1)}, u32[]{:S(2)}, u32[]{:S(2)}) collective-permute-start(bf16[136,512]{1,0:T(8,128)(2,1)S(1)} %shard_map.76), channel_id=1, source_target_pairs={{64,0},{96,32},{128,64},{160,96},{192,128},{224,160},{256,192},{28... | collective-permute-start | bytes 417800 | tf_op jit(solution)/shard_map/ppermute | solution.py:38
  31.9 14.9 %collective-permute-start.2 = (bf16[72,512]{1,0:T(8,128)(2,1)S(1)}, bf16[72,512]{1,0:T(8,128)(2,1)S(1)}, u32[]{:S(2)}, u32[]{:S(2)}) collective-permute-start(bf16[72,512]{1,0:T(8,128)(2,1)S(1)} %own.1.refs_0_.a_1_.a_5_), channel_id=1, source_target_pairs={{352,0},{384,32},{416,64},{448,96},{480,128},{0,160},{32,192},{64,... | collective-permute-start | bytes 221192 | tf_op jit(solution)/shard_map/ppermute | solution.py:38
  46.9 15.6 %collective-permute-start.5 = (bf16[328,512]{1,0:T(8,128)(2,1)S(1)}, bf16[328,512]{1,0:T(8,128)(2,1)S(1)}, u32[]{:S(2)}, u32[]{:S(2)}) collective-permute-start(bf16[328,512]{1,0:T(8,128)(2,1)S(1)} %shard_map.78), channel_id=1, source_target_pairs={{32,0},{64,32},{96,64},{128,96},{160,128},{192,160},{224,192},{256... | collective-permute-start | bytes 1007624 | tf_op jit(solution)/shard_map/ppermute | solution.py:38
  48.9 8.2 %collective-permute-start.4 = (bf16[136,512]{1,0:T(8,128)(2,1)S(1)}, bf16[136,512]{1,0:T(8,128)(2,1)S(1)}, u32[]{:S(2)}, u32[]{:S(2)}) collective-permute-start(bf16[136,512]{1,0:T(8,128)(2,1)S(1)} %shard_map.77), channel_id=1, source_target_pairs={{448,0},{480,32},{0,64},{32,96},{64,128},{96,160},{128,192},{160,2... | collective-permute-start | bytes 417800 | tf_op jit(solution)/shard_map/ppermute | solution.py:38
  57.1 6.9 %copy-start.1 = (f32[1024]{0:T(1024)S(1)}, f32[1024]{0:T(1024)}, u32[]{:S(2)}) copy-start(f32[1024]{0:T(1024)} %param.6) | copy-start | bytes 12292
  57.1 12.7 %collective-permute-start.6 = (bf16[264,512]{1,0:T(8,128)(2,1)S(1)}, bf16[264,512]{1,0:T(8,128)(2,1)S(1)}, u32[]{:S(2)}, u32[]{:S(2)}) collective-permute-start(bf16[264,512]{1,0:T(8,128)(2,1)S(1)} %shard_map.81), channel_id=1, source_target_pairs={{480,0},{0,32},{32,64},{64,96},{96,128},{128,160},{160,192},{192,2... | collective-permute-start | bytes 811016 | tf_op jit(solution)/shard_map/ppermute | solution.py:38
  108.3 6.3 %collective-permute-start.7 = (bf16[264,2048]{1,0:T(8,128)(2,1)S(1)}, bf16[264,2048]{1,0:T(8,128)(2,1)S(1)}, u32[]{:S(2)}, u32[]{:S(2)}) collective-permute-start(bf16[264,2048]{1,0:T(8,128)(2,1)S(1)} %get-tuple-element.39), channel_id=1, source_target_pairs={{0,1},{1,0},{2,3},{3,2},{4,5},{5,4},{6,7},{7,6},{8,9},{9,8},{10,11... | collective-permute-start | bytes 3244040 | tf_op jit(solution)/shard_map/ppermute | solution.py:489

commit v8 on v7

--- a/solution.py
+++ b/solution.py
@@ -33,9 +33,13 @@
     return pltpu.CompilerParams(vmem_limit_bytes=mib * MIB)
 
 
+def sent(array, axes, pairs):
+    return lax.ppermute(array, axes, pairs)
+
+
 def from_z(array, d):
     n = lax.axis_size("z")
-    return lax.ppermute(array, "z", [((i + d) % n, i) for i in range(n)])
+    return sent(array, ("z", "c"), [((i + (d if c == 0 else -d)) % n * 2 + c, i * 2 + c) for i in range(n) for c in (0, 1)])
 
 
 def split(v):
@@ -273,7 +277,8 @@
 
 
 def slot_of(p):
-    return (lax.axis_index("z") + OFF[p]) % 16
+    off = jnp.where(lax.axis_index("c") == 0, OFF[p], 16 - OFF[p])
+    return (lax.axis_index("z") + off) % 16
 
 
 def cols_kernel(parts, logs, s1, s2, s3, sp_out, msg_out, held, lse):
@@ -476,7 +481,7 @@
     own = own_call(targets, potential, log_tgt)
     ra = from_z(own, 4)
     la = from_z(own, -5)
-    near = lax.ppermute(near_call(sources, log_src), ("yh", "yl"), [(0, 3), (3, 0), (1, 2), (2, 1)])
+    near = sent(near_call(sources, log_src), ("yh", "yl"), [(0, 3), (3, 0), (1, 2), (2, 1)])
     rb = from_z(joined([(0, 0), (1, 0)], [own, ra]), 2)
     lb = from_z(joined([(1, 0), (0, 0)], [own, la]), -2)
     rc = from_z(joined([(0, 0), (1, 0), (1, 1), (2, 0), (3, 0)], [own, rb, ra, la]), 1)

time: 136 us -> 133 us (0.978)
  waiting for transfers between devices: 27.9 us -> 16.6 us
  blocking collectives: 53.2 us -> 59.2 us
  starting transfers between devices: 40.5 us -> 41.9 us
    ppermute x7, waiting for transfers between devices: 26.9 us -> 15.6 us  [sent(): return lax.ppermute(array, axes, pairs)]
    all_to_all x1, blocking collectives: 17.5 us -> 21.3 us  [body(): lax.all_to_all(rows, PLANE, split_axis=0, concat_axis=0, tiled=True)]
    all_to_all x1, blocking collectives: 15.5 us -> 17.7 us  [body(): lax.all_to_all(cols, 'z', split_axis=0, concat_axis=0, tiled=True)]
    ppermute x7, starting transfers between devices: 36.5 us -> 37.9 us  [sent(): return lax.ppermute(array, axes, pairs)]
where the time goes in v8:
time: 133 us; the launch traced here: 132 us
  blocking collectives  59.2 us (45%)
  starting transfers between devices  41.9 us (32%)
  waiting for transfers between devices  16.6 us (12%)
  Pallas kernels  13.5 us (10%)
    ppermute x7, starting transfers between devices, sent(): return lax.ppermute(array, axes, pairs)  37.9 us
    all_to_all x1, blocking collectives, body(): lax.all_to_all(rows, PLANE, split_axis=0, concat_axis=0, tiled=True)  21.3 us
    all_to_all x1, blocking collectives, body(): lax.all_to_all(packed, CHIPS, split_axis=0, concat_axis=0, tiled=True)  20.2 us
    all_to_all x1, blocking collectives, body(): lax.all_to_all(cols, 'z', split_axis=0, concat_axis=0, tiled=True)  17.7 us
    ppermute x7, waiting for transfers between devices, sent(): return lax.ppermute(array, axes, pairs)  15.6 us
    pallas_call x3, Pallas kernels, scores_call(): pl.pallas_call(lambda *a: kernel(scale2, *a), in_specs=[WHOLE] * len(args...  4.3 us
    ppermute x1, starting transfers between devices, body(): theirs = lax.ppermute(theirs, 'c', [(0, 1), (1, 0)])  3.94 us
  transfers between devices with their start and end apart: 8, of which 5 were waited for; matrix products, arithmetic and copies ran while one was open for 0% of the time, Pallas kernels for 4%

profile of v8, /device:TPU:1, one launch (start us, length us, event | category | flops | bytes accessed | tf_op | source)
XLA Modules:
  0.0 132.0 jit_solution(608865928953920644)
XLA Ops:
  0.6 1.3 near_message.1
  1.9 5.6 %collective-permute-start = (bf16[1032,512]{1,0:T(8,128)(2,1)S(1)}, bf16[1032,512]{1,0:T(8,128)(2,1)S(1)}, u32[]{:S(2)}, u32[]{:S(2)}) collective-permute-start(bf16[1032,512]{1,0:T(8,128)(2,1)S(1)} %near_message.1), channel_id=1, source_target_pairs={{0,24},{24,0},{8,16},{16,8},{1,25},{25,1},{9,17},{17,9},{2,26},{26... | collective-permute-start | bytes 3170312 | tf_op jit(solution)/shard_map/ppermute | solution.py:37
  7.5 0.9 own.1.refs_0_.a_1_.a_5_
  8.4 8.8 %collective-permute-start.1 = (bf16[72,512]{1,0:T(8,128)(2,1)S(1)}, bf16[72,512]{1,0:T(8,128)(2,1)S(1)}, u32[]{:S(2)}, u32[]{:S(2)}) collective-permute-start(bf16[72,512]{1,0:T(8,128)(2,1)S(1)} %own.1.refs_0_.a_1_.a_5_), channel_id=1, source_target_pairs={{128,0},{385,1},{160,32},{417,33},{192,64},{449,65},{224,96},{481,... | collective-permute-start | bytes 221192 | tf_op jit(solution)/shard_map/ppermute | solution.py:37
  17.2 5.7 %collective-permute-done.1.refs_1_.refs_2_.a_2_.a_6_ = bf16[72,512]{1,0:T(8,128)(2,1)S(1)} collective-permute-done((bf16[72,512]{1,0:T(8,128)(2,1)S(1)}, bf16[72,512]{1,0:T(8,128)(2,1)S(1)}, u32[]{:S(2)}, u32[]{:S(2)}) %collective-permute-start.1) | collective-permute-done | bytes 73760 | tf_op jit(solution)/shard_map/ppermute | solution.py:37
  23.0 4.5 %collective-permute-start.3 = (bf16[136,512]{1,0:T(8,128)(2,1)S(1)}, bf16[136,512]{1,0:T(8,128)(2,1)S(1)}, u32[]{:S(2)}, u32[]{:S(2)}) collective-permute-start(bf16[136,512]{1,0:T(8,128)(2,1)S(1)} %shard_map.76), channel_id=1, source_target_pairs={{64,0},{449,1},{96,32},{481,33},{128,64},{1,65},{160,96},{33,97},{... | collective-permute-start | bytes 417800 | tf_op jit(solution)/shard_map/ppermute | solution.py:37
  27.5 8.4 %collective-permute-start.2 = (bf16[72,512]{1,0:T(8,128)(2,1)S(1)}, bf16[72,512]{1,0:T(8,128)(2,1)S(1)}, u32[]{:S(2)}, u32[]{:S(2)}) collective-permute-start(bf16[72,512]{1,0:T(8,128)(2,1)S(1)} %own.1.refs_0_.a_1_.a_5_), channel_id=1, source_target_pairs={{352,0},{161,1},{384,32},{193,33},{416,64},{225,65},{448,96},{257,... | collective-permute-start | bytes 221192 | tf_op jit(solution)/shard_map/ppermute | solution.py:37
  35.9 4.4 %collective-permute-done.2.refs_1_.refs_3_.a_3_.refs_2_.a_7_ = bf16[72,512]{1,0:T(8,128)(2,1)S(1)} collective-permute-done((bf16[72,512]{1,0:T(8,128)(2,1)S(1)}, bf16[72,512]{1,0:T(8,128)(2,1)S(1)}, u32[]{:S(2)}, u32[]{:S(2)}) %collective-permute-start.2) | collective-permute-done | bytes 73760 | tf_op jit(solution)/shard_map/ppermute | solution.py:37
  40.4 1.9 %collective-permute-start.5 = (bf16[328,512]{1,0:T(8,128)(2,1)S(1)}, bf16[328,512]{1,0:T(8,128)(2,1)S(1)}, u32[]{:S(2)}, u32[]{:S(2)}) collective-permute-start(bf16[328,512]{1,0:T(8,128)(2,1)S(1)} %shard_map.78), channel_id=1, source_target_pairs={{32,0},{481,1},{64,32},{1,33},{96,64},{33,65},{128,96},{65,97},{16... | collective-permute-start | bytes 1007624 | tf_op jit(solution)/shard_map/ppermute | solution.py:37
  42.4 5.7 %collective-permute-start.4 = (bf16[136,512]{1,0:T(8,128)(2,1)S(1)}, bf16[136,512]{1,0:T(8,128)(2,1)S(1)}, u32[]{:S(2)}, u32[]{:S(2)}) collective-permute-start(bf16[136,512]{1,0:T(8,128)(2,1)S(1)} %shard_map.77), channel_id=1, source_target_pairs={{448,0},{65,1},{480,32},{97,33},{0,64},{129,65},{32,96},{161,97},{... | collective-permute-start | bytes 417800 | tf_op jit(solution)/shard_map/ppermute | solution.py:37
  48.1 4.5 %collective-permute-done.4.a_5_.refs_1_.a_9_ = bf16[136,512]{1,0:T(8,128)(2,1)S(1)} collective-permute-done((bf16[136,512]{1,0:T(8,128)(2,1)S(1)}, bf16[136,512]{1,0:T(8,128)(2,1)S(1)}, u32[]{:S(2)}, u32[]{:S(2)}) %collective-permute-start.4) | collective-permute-done | bytes 139296 | tf_op jit(solution)/shard_map/ppermute | solution.py:37
  52.6 3.1 %collective-permute-start.6 = (bf16[264,512]{1,0:T(8,128)(2,1)S(1)}, bf16[264,512]{1,0:T(8,128)(2,1)S(1)}, u32[]{:S(2)}, u32[]{:S(2)}) collective-permute-start(bf16[264,512]{1,0:T(8,128)(2,1)S(1)} %shard_map.81), channel_id=1, source_target_pairs={{480,0},{33,1},{0,32},{65,33},{32,64},{97,65},{64,96},{129,97},{96... | collective-permute-start | bytes 811016 | tf_op jit(solution)/shard_map/ppermute | solution.py:37
  55.7 1.6 %shard_map.79 = (f32[768,1024]{1,0:T(8,128)S(1)}, f32[1,1024]{1,0:T(1,128)S(1)}, bf16[512,768]{1,0:T(8,128)(2,1)S(1)}, bf16[768,512]{1,0:T(8,128)(2,1)S(1)}, f32[768,128]{1,0:T(8,128)S(1)}) custom-call(bf16[1024,512]{1,0:T(8,128)(2,1)S(1)} %copy-done, bf16[72,512]{1,0:T(8,128)(2,1)S(1)} %own.1.refs_0_.a_1_.a_5_, ...), custom_call_target="tpu_custom_call" | custom-call | flops 805306368 | bytes 4194304 | tf_op jit(solution)/shard_map/pallas_call | solution.py:243
  57.3 1.6 %shard_map.80 = (f32[768,1024]{1,0:T(8,128)S(1)}, f32[1,1024]{1,0:T(1,128)S(1)}, f32[2,8,128]{2,1,0:T(8,128)S(1)}) custom-call(bf16[1032,512]{1,0:T(8,128)(2,1)S(1)} %collective-permute-done.a_0_.a_1_, f32[1,1024]{1,0:T(1,128)S(1)} %bitcast.7, bf16[768,512]{1,0:T(8,128)(2,1)S(1)} %get-tuple-element.25.a_2_, f32[768,128]{1,0:T(8,128)S(1)} %get-tuple-element.26.a_3_), custom_call_target="tpu_custom_call" | custom-call | flops 805306368 | bytes 4194304 | tf_op jit(solution)/shard_map/pallas_call | solution.py:243
  58.9 1.0 collective-permute-done.6.a_11_
  60.0 1.1 shard_map.82
  61.1 21.3 %all_to_all.15.parts = f32[32,2,8,128]{3,2,1,0:T(8,128)S(1)} all-to-all(f32[32,2,8,128]{3,2,1,0:T(8,128)S(1)} %get-tuple-element.30), channel_id=1, replica_groups=mesh['z'=16,'yh'=2,'yl'=2,'x'=4,'c'=2] {'c','x','yh','yl'}, dimensions={0} | all-to-all | bytes 524288 | tf_op jit(solution)/shard_map/all_to_all | solution.py:490
  82.4 2.1 %cols.1 = (f32[1,2048]{1,0:T(1,128)S(1)}, f32[16,8,128]{2,1,0:T(8,128)S(1)}) custom-call(f32[32,2,8,128]{3,2,1,0:T(8,128)S(1)} %all_to_all.15.parts, f32[2,8,128]{2,1,0:T(8,128)S(1)} %get-tuple-element.31.logs, f32[768,1024]{1,0:T(8,128)S(1)} %get-tuple-element.32.s1, f32[768,1024]{1,0:T(8,128)S(1)} %get-tuple-element.33.s2, ...), custom_call_target="tpu_custom_call" | custom-call | tf_op jit(solution)/shard_map/cols/pallas_call | solution.py:325
  84.5 17.7 %all_to_all.16.parts = f32[16,8,128]{2,1,0:T(8,128)S(1)} all-to-all(f32[16,8,128]{2,1,0:T(8,128)S(1)} %get-tuple-element.35), channel_id=1, replica_groups=mesh['z'=16,'yh'=2,'yl'=2,'x'=4,'c'=2] {'z'}, dimensions={0} | all-to-all | bytes 131072 | tf_op jit(solution)/shard_map/all_to_all | solution.py:492
  102.2 2.3 %moved.1 = (f32[1,128]{1,0:T(1,128)S(1)}, bf16[264,2048]{1,0:T(8,128)(2,1)S(1)}, f32[1,2048]{1,0:T(1,128)S(1)}, bf16[1024,2048]{1,0:T(8,128)(2,1)S(1)}) custom-call(f32[16,8,128]{2,1,0:T(8,128)S(1)} %all_to_all.16.parts, f32[16,128]{1,0:T(8,128)S(1)} %get-tuple-element.36.lt, f32[1,2048]{1,0:T(1,128)S(1)} %get-tuple-element.37.sp, ...), custom_call_target="tpu_custom_call" | custom-call | tf_op jit(solution)/shard_map/moved/pallas_call | solution.py:375
  104.5 3.9 %collective-permute-start.7 = (bf16[264,2048]{1,0:T(8,128)(2,1)S(1)}, bf16[264,2048]{1,0:T(8,128)(2,1)S(1)}, u32[]{:S(2)}, u32[]{:S(2)}) collective-permute-start(bf16[264,2048]{1,0:T(8,128)(2,1)S(1)} %get-tuple-element.39), channel_id=1, source_target_pairs={{0,1},{1,0},{2,3},{3,2},{4,5},{5,4},{6,7},{7,6},{8,9},{9,8},{10,11... | collective-permute-start | bytes 3244040 | tf_op jit(solution)/shard_map/ppermute | solution.py:494
  108.4 1.3 mine.1
  109.7 1.0 collective-permute-done.7.theirs
  111.0 20.2 %all_to_all.17.parts = bf16[16,272,128]{2,1,0:T(8,128)(2,1)S(1)} all-to-all(bf16[16,272,128]{2,1,0:T(8,128)(2,1)S(1)} %pack.1), channel_id=1, replica_groups=mesh['z'=16,'yh'=2,'yl'=2,'x'=4,'c'=2] {'x','yh','yl'}, dimensions={0} | all-to-all | bytes 2228224 | tf_op jit(solution)/shard_map/all_to_all | solution.py:496
  (13 shorter events, 1.4 us)
Async XLA Ops:
  1.9 53.8 %copy-start = (bf16[1024,512]{1,0:T(8,128)(2,1)S(1)}, bf16[1024,512]{1,0:T(8,128)(2,1)}, u32[]{:S(2)}) copy-start(bf16[1024,512]{1,0:T(8,128)(2,1)} %a_0_.3) | copy-start | bytes 3145732
  1.9 55.4 %collective-permute-start = (bf16[1032,512]{1,0:T(8,128)(2,1)S(1)}, bf16[1032,512]{1,0:T(8,128)(2,1)S(1)}, u32[]{:S(2)}, u32[]{:S(2)}) collective-permute-start(bf16[1032,512]{1,0:T(8,128)(2,1)S(1)} %near_message.1), channel_id=1, source_target_pairs={{0,24},{24,0},{8,16},{16,8},{1,25},{25,1},{9,17},{17,9},{2,26},{26... | collective-permute-start | bytes 3170312 | tf_op jit(solution)/shard_map/ppermute | solution.py:37
  8.4 14.5 %collective-permute-start.1 = (bf16[72,512]{1,0:T(8,128)(2,1)S(1)}, bf16[72,512]{1,0:T(8,128)(2,1)S(1)}, u32[]{:S(2)}, u32[]{:S(2)}) collective-permute-start(bf16[72,512]{1,0:T(8,128)(2,1)S(1)} %own.1.refs_0_.a_1_.a_5_), channel_id=1, source_target_pairs={{128,0},{385,1},{160,32},{417,33},{192,64},{449,65},{224,96},{481,... | collective-permute-start | bytes 221192 | tf_op jit(solution)/shard_map/ppermute | solution.py:37
  23.0 17.3 %collective-permute-start.3 = (bf16[136,512]{1,0:T(8,128)(2,1)S(1)}, bf16[136,512]{1,0:T(8,128)(2,1)S(1)}, u32[]{:S(2)}, u32[]{:S(2)}) collective-permute-start(bf16[136,512]{1,0:T(8,128)(2,1)S(1)} %shard_map.76), channel_id=1, source_target_pairs={{64,0},{449,1},{96,32},{481,33},{128,64},{1,65},{160,96},{33,97},{... | collective-permute-start | bytes 417800 | tf_op jit(solution)/shard_map/ppermute | solution.py:37
  27.5 12.8 %collective-permute-start.2 = (bf16[72,512]{1,0:T(8,128)(2,1)S(1)}, bf16[72,512]{1,0:T(8,128)(2,1)S(1)}, u32[]{:S(2)}, u32[]{:S(2)}) collective-permute-start(bf16[72,512]{1,0:T(8,128)(2,1)S(1)} %own.1.refs_0_.a_1_.a_5_), channel_id=1, source_target_pairs={{352,0},{161,1},{384,32},{193,33},{416,64},{225,65},{448,96},{257,... | collective-permute-start | bytes 221192 | tf_op jit(solution)/shard_map/ppermute | solution.py:37
  40.4 15.3 %collective-permute-start.5 = (bf16[328,512]{1,0:T(8,128)(2,1)S(1)}, bf16[328,512]{1,0:T(8,128)(2,1)S(1)}, u32[]{:S(2)}, u32[]{:S(2)}) collective-permute-start(bf16[328,512]{1,0:T(8,128)(2,1)S(1)} %shard_map.78), channel_id=1, source_target_pairs={{32,0},{481,1},{64,32},{1,33},{96,64},{33,65},{128,96},{65,97},{16... | collective-permute-start | bytes 1007624 | tf_op jit(solution)/shard_map/ppermute | solution.py:37
  42.4 10.2 %collective-permute-start.4 = (bf16[136,512]{1,0:T(8,128)(2,1)S(1)}, bf16[136,512]{1,0:T(8,128)(2,1)S(1)}, u32[]{:S(2)}, u32[]{:S(2)}) collective-permute-start(bf16[136,512]{1,0:T(8,128)(2,1)S(1)} %shard_map.77), channel_id=1, source_target_pairs={{448,0},{65,1},{480,32},{97,33},{0,64},{129,65},{32,96},{161,97},{... | collective-permute-start | bytes 417800 | tf_op jit(solution)/shard_map/ppermute | solution.py:37
  52.6 4.7 %copy-start.1 = (f32[1024]{0:T(1024)S(1)}, f32[1024]{0:T(1024)}, u32[]{:S(2)}) copy-start(f32[1024]{0:T(1024)} %param.6) | copy-start | bytes 12292
  52.6 7.3 %collective-permute-start.6 = (bf16[264,512]{1,0:T(8,128)(2,1)S(1)}, bf16[264,512]{1,0:T(8,128)(2,1)S(1)}, u32[]{:S(2)}, u32[]{:S(2)}) collective-permute-start(bf16[264,512]{1,0:T(8,128)(2,1)S(1)} %shard_map.81), channel_id=1, source_target_pairs={{480,0},{33,1},{0,32},{65,33},{32,64},{97,65},{64,96},{129,97},{96... | collective-permute-start | bytes 811016 | tf_op jit(solution)/shard_map/ppermute | solution.py:37
  104.5 6.3 %collective-permute-start.7 = (bf16[264,2048]{1,0:T(8,128)(2,1)S(1)}, bf16[264,2048]{1,0:T(8,128)(2,1)S(1)}, u32[]{:S(2)}, u32[]{:S(2)}) collective-permute-start(bf16[264,2048]{1,0:T(8,128)(2,1)S(1)} %get-tuple-element.39), channel_id=1, source_target_pairs={{0,1},{1,0},{2,3},{3,2},{4,5},{5,4},{6,7},{7,6},{8,9},{9,8},{10,11... | collective-permute-start | bytes 3244040 | tf_op jit(solution)/shard_map/ppermute | solution.py:494
